TPU v7x, 32 devices: a whole 2x2x4 slice. The times are simulated.
32 devices in a mesh: row: 2 (over x), col: 4 (over y, core), dp: 4 (over z).
Axes of the slice: x: 2, y: 2, z: 4, core: 2. Of those that a mesh axis runs over, the one named last changes fastest.
Arguments:
- latents: bfloat16 [4, 1024, 1024], P('dp', 'col', 'row'), may hold values from -6 to 6
- inputs: bfloat16 [4, 8192, 261], P('dp', 'col'), may hold values from -6 to 6
- positions: int32 [4, 1024], P('dp'), may hold values from 0 to 8191, as said below
- piece_start: int32 [4, 8], P('dp'), may hold values from 0 to 7936, as said below
- cotangent: bfloat16 [4, 1024, 1024], P('dp', 'col', 'row'), may hold values from -6 to 6
- cross_gain: float32 [1024], P('row'), may hold values from 0.25 to 1.75
- input_gain: float32 [261], replicated, may hold values from 0.25 to 1.75
- cross_query: bfloat16 [1024, 1024], P('row', 'col'), may hold values from -0.1875 to 0.1875
- cross_key: bfloat16 [261, 1024], replicated, may hold values from -0.375 to 0.375
- cross_value: bfloat16 [261, 1024], replicated, may hold values from -0.375 to 0.375
- cross_out: bfloat16 [1024, 1024], P('col', 'row'), may hold values from -4 to 4
- first_gain: float32 [1024], P('row'), may hold values from 0.25 to 1.75
- first_expand: bfloat16 [1024, 1024], P('row', 'col'), may hold values from -0.1875 to 0.1875
- first_shrink: bfloat16 [1024, 1024], P('col', 'row'), may hold values from -0.1875 to 0.1875
- self_gain: float32 [1024], P('row'), may hold values from 0.25 to 1.75
- self_query: bfloat16 [1024, 1024], P('row', 'col'), may hold values from -0.1875 to 0.1875
- self_key: bfloat16 [1024, 1024], P('row', 'col'), may hold values from -0.1875 to 0.1875
- self_value: bfloat16 [1024, 1024], P('row', 'col'), may hold values from -0.1875 to 0.1875
- self_out: bfloat16 [1024, 1024], P('col', 'row'), may hold values from -2 to 2
- second_gain: float32 [1024], P('row'), may hold values from 0.25 to 1.75
- second_expand: bfloat16 [1024, 1024], P('row', 'col'), may hold values from -0.1875 to 0.1875
- second_shrink: bfloat16 [1024, 1024], P('col', 'row'), may hold values from -0.1875 to 0.1875
Outputs:
- out: bfloat16 [4, 1024, 1024], P('dp', 'col', 'row')
- grad_latents: float32 [4, 1024, 1024], P('dp', 'col', 'row')
- grad_inputs: bfloat16 [4, 8192, 261], P('dp', 'col')
- grad_cross_gain: float32 [1024], P('row')
- grad_input_gain: float32 [261], replicated
- grad_cross_query: float32 [1024, 1024], P('row', 'col')
- grad_cross_key: float32 [261, 1024], replicated
- grad_cross_value: float32 [261, 1024], replicated
- grad_cross_out: float32 [1024, 1024], P('col', 'row')
- grad_first_gain: float32 [1024], P('row')
- grad_first_expand: float32 [1024, 1024], P('row', 'col')
- grad_first_shrink: float32 [1024, 1024], P('col', 'row')
- grad_self_gain: float32 [1024], P('row')
- grad_self_query: float32 [1024, 1024], P('row', 'col')
- grad_self_key: float32 [1024, 1024], P('row', 'col')
- grad_self_value: float32 [1024, 1024], P('row', 'col')
- grad_self_out: float32 [1024, 1024], P('col', 'row')
- grad_second_gain: float32 [1024], P('row')
- grad_second_expand: float32 [1024, 1024], P('row', 'col')
- grad_second_shrink: float32 [1024, 1024], P('col', 'row')
Inputs may be any that keep to these rules, and one draw needn't show every extreme that they name: `positions`: latent i of a sequence stands in rows i * 8 to (i + 1) * 8 - 1. `piece_start`: piece p starts in the slot of rows from p * 1024 and its 256 rows end within that slot.
All inputs are finite; a program needn't handle non-finite values.
Results may differ from a plain program's by a relative error of at most 0.04.
Values may be sent and summed in bfloat16 or wider, within the bound.
No kernel may reach another device: no remote copies, remote signals or barrier semaphores. Data moves between devices by JAX's collectives and lax.ppermute only.
A program may use at most 128 MiB of HBM per device.

v0:
```python
import math

import jax
import jax.numpy as jnp
from jax import lax
from jax.sharding import PartitionSpec as P

D = 1024
HEAD = 128
PIECE_LEN = 256


EPS = 1e-05
NEGATIVE = -1e30
FORWARD_FIRST = "xok,kt->xot"
BACKWARD_FIRST = "tpv,qv->tpq"
FORWARD_SECOND = "ybj,jv->ybv"
BACKWARD_SECOND = "xng,wg->xnw"
GRADIENT_FIRST = "zyq,zyi->qi"
GRADIENT_SECOND = "oqv,oqa->va"


def joined_2(shard, axis, combine):
    everything = jax.tree.map(lambda part: lax.all_gather(part, axis), shard)
    first = jax.tree.map(lambda part: part[0], everything)

    def step(k, so_far):
        return combine(so_far, jax.tree.map(lambda part: part[k], everything))

    return lax.fori_loop(1, lax.axis_size(axis), step, first)


def col_rows(value):
    return lax.all_gather(value, "col", axis=1, tiled=True)


def row_reduce(value):
    return lax.psum_scatter(
        value.astype(jnp.bfloat16), "row", scatter_dimension=1, tiled=True
    ).astype(jnp.float32)


def row_rows(value):
    return lax.all_gather(value, "row", axis=1, tiled=True)


def col_reduce(value):
    return lax.psum_scatter(
        value.astype(jnp.bfloat16), "col", scatter_dimension=1, tiled=True
    ).astype(jnp.float32)


def query_feats(value):
    return lax.all_gather(value, "col", axis=2, tiled=True)


def query_grads(value):
    return lax.psum_scatter(
        value.astype(jnp.bfloat16), "col", scatter_dimension=2, tiled=True
    ).astype(jnp.float32)


def row_totals(first, second):
    return lax.psum((first, second), "row")


def project_cols(value, weight, form):
    gathered = col_rows(value)
    partial_sum = jnp.einsum(form, gathered, weight, preferred_element_type=jnp.float32)
    return (row_reduce(partial_sum), gathered)


def project_rows(value, weight, form):
    gathered = row_rows(value)
    partial_sum = jnp.einsum(form, gathered, weight, preferred_element_type=jnp.float32)
    return (col_reduce(partial_sum), gathered)


def weight_grad(form, first, second):
    return jnp.einsum(form, first, second, preferred_element_type=jnp.float32)


def split_parts(value):
    leading = value.astype(jnp.bfloat16)
    residue = (value - leading.astype(jnp.float32)).astype(jnp.bfloat16)
    return (leading, residue)


def split_einsum(form, exact, other, first_side):
    leading, residue = split_parts(exact)
    if first_side:
        return jnp.einsum(form, leading, other, preferred_element_type=jnp.float32) + jnp.einsum(
            form, residue, other, preferred_element_type=jnp.float32
        )
    return jnp.einsum(form, other, leading, preferred_element_type=jnp.float32) + jnp.einsum(
        form, other, residue, preferred_element_type=jnp.float32
    )


def norm_forward(value, gain):
    width = value.shape[-1] * lax.axis_size("row")
    total, squares = row_totals(jnp.sum(value, axis=-1), jnp.sum(value * value, axis=-1))
    center = total / width
    spread = squares / width - center * center
    scale_inv = lax.rsqrt(spread + EPS)
    normed = (value - center[..., None]) * scale_inv[..., None]
    return (normed * gain, normed, scale_inv)


def norm_backward(grad, gain, normed, scale_inv):
    width = grad.shape[-1] * lax.axis_size("row")
    scaled = grad * gain
    first, second = row_totals(jnp.sum(scaled, axis=-1), jnp.sum(scaled * normed, axis=-1))
    result = scale_inv[..., None] * (
        scaled - first[..., None] / width - normed * (second[..., None] / width)
    )
    return (result, jnp.sum(grad * normed, axis=(0, 1)))


def gelu_exact(value):
    return jax.nn.gelu(value, approximate=False)


def gelu_back(value, grad):
    return jax.vjp(gelu_exact, value)[1](grad)[0]


def view_limits(positions, starts):
    ends = starts + PIECE_LEN
    inside = (starts[:, None, :] <= positions[:, :, None]) & (
        positions[:, :, None] < ends[:, None, :]
    )
    reach = jnp.sum(jnp.where(inside, ends[:, None, :], 0), axis=-1)
    return jnp.maximum(positions + 1, reach)


def merge_softmax(first, second):
    top = jnp.maximum(first[0], second[0])
    return (top, first[1] * jnp.exp(first[0] - top) + second[1] * jnp.exp(second[0] - top))


def feed_forward(state, gain, expand, shrink):
    normed_out, normed, scale_inv = norm_forward(state, gain)
    upward, hidden_rows = project_cols(normed_out.astype(jnp.bfloat16), expand, FORWARD_FIRST)
    activated = gelu_exact(upward).astype(jnp.bfloat16)
    branch, active_rows = project_rows(activated, shrink, FORWARD_SECOND)
    return (state + branch, (normed, scale_inv, hidden_rows, upward, active_rows))


def feed_backward(grad, saved, gain, expand, shrink):
    normed, scale_inv, hidden_rows, upward, active_rows = saved
    grad_active, branch_rows = project_cols(grad.astype(jnp.bfloat16), shrink, BACKWARD_SECOND)
    grad_shrink = weight_grad(GRADIENT_SECOND, active_rows, branch_rows)
    grad_upward = gelu_back(upward, grad_active).astype(jnp.bfloat16)
    grad_hidden, upward_rows = project_rows(grad_upward, expand, BACKWARD_FIRST)
    grad_expand = weight_grad(GRADIENT_FIRST, hidden_rows, upward_rows)
    grad_normed, grad_gain = norm_backward(grad_hidden, gain, normed, scale_inv)
    return (grad + grad_normed, grad_gain, grad_expand, grad_shrink)


def input_back(grad_part, normed, scale_inv, gain):
    scaled = grad_part * gain
    first = jnp.mean(scaled, axis=-1, keepdims=True)
    second = jnp.mean(scaled * normed, axis=-1, keepdims=True)
    return scale_inv[..., None] * (scaled - first - normed * second)


def on_device(
    latents,
    inputs,
    positions,
    piece_start,
    cotangent,
    cross_gain,
    input_gain,
    cross_query,
    cross_key,
    cross_value,
    cross_out,
    first_gain,
    first_expand,
    first_shrink,
    self_gain,
    self_query,
    self_key,
    self_value,
    self_out,
    second_gain,
    second_expand,
    second_shrink,
):
    low_type = jnp.bfloat16
    full_type = jnp.float32
    row_at = lax.axis_index("row")
    col_at = lax.axis_index("col")
    seqs = latents.shape[0]
    total_rows = positions.shape[1]
    rows_here = total_rows // lax.axis_size("row")
    column_width_count = cross_query.shape[1]
    width_row = cross_query.shape[0]
    key_rows = inputs.shape[1]
    heads_here = column_width_count // HEAD
    cross_scale = 1.0 / math.sqrt(D)
    self_scale = 1.0 / math.sqrt(HEAD)
    limit_all = view_limits(positions, piece_start)
    limit_here = lax.dynamic_slice_in_dim(limit_all, row_at * rows_here, rows_here, 1)
    key_index = col_at * key_rows + jnp.arange(key_rows, dtype=jnp.int32)
    cross_mask = key_index[None, None, :] < limit_here[:, :, None]
    latent_attend_mask = (positions[:, None, :] < limit_here[:, :, None])[:, None]
    initial = latents.astype(full_type)
    cross_normed_out, cross_normed, cross_inv = norm_forward(initial, cross_gain)
    query_part, cross_rows = project_cols(
        cross_normed_out.astype(low_type), cross_query, FORWARD_FIRST
    )
    query_all = query_feats(query_part.astype(low_type))
    input_full = inputs.astype(full_type)
    input_center = input_full - jnp.mean(input_full, axis=-1, keepdims=True)
    input_inv = lax.rsqrt(jnp.mean(input_center * input_center, axis=-1) + EPS)
    input_normed = input_center * input_inv[..., None]
    input_low = (input_normed * input_gain).astype(low_type)

    def project_keys(rows):
        key_block = jnp.dot(rows, cross_key, preferred_element_type=full_type).astype(low_type)
        value_block = jnp.dot(rows, cross_value, preferred_element_type=full_type).astype(low_type)
        return (key_block, value_block)

    keys_all, values_all = lax.map(project_keys, input_low)
    scores = (
        jnp.einsum("sqd,skd->sqk", query_all, keys_all, preferred_element_type=full_type)
        * cross_scale
    )
    local_top = jnp.max(jnp.where(cross_mask, scores, NEGATIVE), axis=-1)
    local_total = jnp.sum(
        jnp.where(cross_mask, jnp.exp(scores - local_top[..., None]), 0.0), axis=-1
    )
    merged_top, merged_total = joined_2((local_top, local_total), "col", merge_softmax)
    cross_lse = merged_top + jnp.log(merged_total)
    cross_chances = jnp.where(cross_mask, jnp.exp(scores - cross_lse[..., None]), 0.0).astype(
        low_type
    )
    attended_part = jnp.einsum(
        "sqk,skd->sqd", cross_chances, values_all, preferred_element_type=full_type
    )
    attended_all = lax.psum(attended_part.astype(jnp.bfloat16), "col").astype(jnp.float32)
    attended_here = lax.dynamic_slice_in_dim(
        attended_all, col_at * column_width_count, column_width_count, 2
    )
    cross_branch, attended_rows = project_rows(
        attended_here.astype(low_type), cross_out, FORWARD_SECOND
    )
    after_cross = initial + cross_branch
    after_first, first_saved = feed_forward(after_cross, first_gain, first_expand, first_shrink)
    self_normed_out, self_normed, self_inv = norm_forward(after_first, self_gain)
    joined = jnp.concatenate([self_query, self_key, self_value], axis=1)
    projected, self_rows = project_cols(self_normed_out.astype(low_type), joined, FORWARD_FIRST)
    projected_low = projected.astype(low_type)
    pair_all = row_rows(projected_low[..., column_width_count:])
    heads_q = projected_low[..., :column_width_count].reshape(seqs, rows_here, heads_here, HEAD)
    heads_k = pair_all[..., :column_width_count].reshape(seqs, total_rows, heads_here, HEAD)
    heads_v = pair_all[..., column_width_count:].reshape(seqs, total_rows, heads_here, HEAD)
    self_scores = (
        jnp.einsum("sqhd,skhd->shqk", heads_q, heads_k, preferred_element_type=full_type)
        * self_scale
    )
    self_top = jnp.max(jnp.where(latent_attend_mask, self_scores, NEGATIVE), axis=-1)
    self_total = jnp.sum(
        jnp.where(latent_attend_mask, jnp.exp(self_scores - self_top[..., None]), 0.0), axis=-1
    )
    self_lse = self_top + jnp.log(self_total)
    self_chances = jnp.where(
        latent_attend_mask, jnp.exp(self_scores - self_lse[..., None]), 0.0
    ).astype(low_type)
    self_mixed = jnp.einsum(
        "shqk,skhd->sqhd", self_chances, heads_v, preferred_element_type=full_type
    )
    self_branch, mixed_rows = project_rows(
        self_mixed.reshape(seqs, rows_here, column_width_count).astype(low_type),
        self_out,
        FORWARD_SECOND,
    )
    after_self = after_first + self_branch
    final_state, second_saved = feed_forward(after_self, second_gain, second_expand, second_shrink)
    result = final_state.astype(low_type)
    grad_state = cotangent.astype(full_type)
    grad_state, grad_second_gain, grad_second_expand, grad_second_shrink = feed_backward(
        grad_state, second_saved, second_gain, second_expand, second_shrink
    )
    grad_mixed, self_branch_rows = project_cols(
        grad_state.astype(low_type), self_out, BACKWARD_SECOND
    )
    grad_self_out = weight_grad(GRADIENT_SECOND, mixed_rows, self_branch_rows)
    grad_mixed_low = grad_mixed.astype(low_type).reshape(seqs, rows_here, heads_here, HEAD)
    self_delta = jnp.transpose(
        jnp.sum(grad_mixed_low.astype(full_type) * self_mixed, axis=-1), (0, 2, 1)
    )
    again_scores = (
        jnp.einsum("sqhd,skhd->shqk", heads_q, heads_k, preferred_element_type=full_type)
        * self_scale
    )
    again_chances = jnp.where(latent_attend_mask, jnp.exp(again_scores - self_lse[..., None]), 0.0)
    grad_self_chances = jnp.einsum(
        "sqhd,skhd->shqk", grad_mixed_low, heads_v, preferred_element_type=full_type
    )
    grad_self_scores = (again_chances * (grad_self_chances - self_delta[..., None])).astype(
        low_type
    )
    grad_heads_q = (
        jnp.einsum("shqk,skhd->sqhd", grad_self_scores, heads_k, preferred_element_type=full_type)
        * self_scale
    )
    grad_heads_k = (
        jnp.einsum("shqk,sqhd->skhd", grad_self_scores, heads_q, preferred_element_type=full_type)
        * self_scale
    )
    grad_heads_v = jnp.einsum(
        "shqk,sqhd->skhd",
        again_chances.astype(low_type),
        grad_mixed_low,
        preferred_element_type=full_type,
    )
    pair_grad = row_reduce(
        jnp.concatenate(
            [
                grad_heads_k.reshape(seqs, total_rows, column_width_count),
                grad_heads_v.reshape(seqs, total_rows, column_width_count),
            ],
            axis=-1,
        )
    )
    joined_grad = jnp.concatenate(
        [grad_heads_q.reshape(seqs, rows_here, column_width_count), pair_grad], axis=-1
    ).astype(low_type)
    grad_self_in, joined_rows = project_rows(joined_grad, joined, BACKWARD_FIRST)
    grad_joined = weight_grad(GRADIENT_FIRST, self_rows, joined_rows)
    grad_self_normed, grad_self_gain = norm_backward(grad_self_in, self_gain, self_normed, self_inv)
    grad_state = grad_state + grad_self_normed
    grad_state, grad_first_gain, grad_first_expand, grad_first_shrink = feed_backward(
        grad_state, first_saved, first_gain, first_expand, first_shrink
    )
    grad_attended, cross_branch_rows = project_cols(
        grad_state.astype(low_type), cross_out, BACKWARD_SECOND
    )
    grad_cross_out = weight_grad(GRADIENT_SECOND, attended_rows, cross_branch_rows)
    grad_attended_all = query_feats(grad_attended.astype(low_type))
    cross_delta = jnp.sum(grad_attended_all.astype(full_type) * attended_all, axis=-1)

    def cross_back_one(carry, item):
        query_one, keys_one, values_one, grad_one, lse_one, delta_one, mask_one, normed_one = item
        scores_one = (
            jnp.einsum("qd,kd->qk", query_one, keys_one, preferred_element_type=full_type)
            * cross_scale
        )
        chances_one = jnp.where(mask_one, jnp.exp(scores_one - lse_one[:, None]), 0.0)
        grad_chances = jnp.einsum(
            "qd,kd->qk", grad_one, values_one, preferred_element_type=full_type
        )
        grad_scores = (chances_one * (grad_chances - delta_one[:, None])).astype(low_type)
        grad_query = (
            jnp.einsum("qk,kd->qd", grad_scores, keys_one, preferred_element_type=full_type)
            * cross_scale
        )
        grad_keys = (
            jnp.einsum("qk,qd->kd", grad_scores, query_one, preferred_element_type=full_type)
            * cross_scale
        )
        grad_values = jnp.einsum(
            "qk,qd->kd", chances_one.astype(low_type), grad_one, preferred_element_type=full_type
        )
        grad_normed = split_einsum("kd,cd->kc", grad_keys, cross_key, True) + split_einsum(
            "kd,cd->kc", grad_values, cross_value, True
        )
        key_sum = carry[0] + split_einsum("kc,kd->cd", grad_keys, normed_one, False)
        value_sum = carry[1] + split_einsum("kc,kd->cd", grad_values, normed_one, False)
        return ((key_sum, value_sum), (grad_query, grad_normed))

    empty = jnp.zeros(cross_key.shape, full_type)
    (grad_key_sum, grad_value_sum), (grad_query_all, grad_input_part) = lax.scan(
        cross_back_one,
        (empty, empty),
        (
            query_all,
            keys_all,
            values_all,
            grad_attended_all,
            cross_lse,
            cross_delta,
            cross_mask,
            input_low,
        ),
    )
    grad_query_here = query_grads(grad_query_all).astype(low_type)
    grad_cross_in, query_rows = project_rows(grad_query_here, cross_query, BACKWARD_FIRST)
    grad_cross_query = weight_grad(GRADIENT_FIRST, cross_rows, query_rows)
    grad_cross_normed, grad_cross_gain = norm_backward(
        grad_cross_in, cross_gain, cross_normed, cross_inv
    )
    grad_latents = grad_state + grad_cross_normed
    input_gain_part = jnp.sum(grad_input_part * input_normed, axis=(0, 1))
    summed = lax.psum(grad_input_part.astype(jnp.bfloat16), "row").astype(jnp.float32)
    grad_inputs = input_back(summed, input_normed, input_inv, input_gain).astype(low_type)
    grid = (
        lax.psum(grad_cross_query.astype(jnp.bfloat16), "dp").astype(jnp.float32),
        lax.psum(grad_cross_out.astype(jnp.bfloat16), "dp").astype(jnp.float32),
        lax.psum(grad_first_expand.astype(jnp.bfloat16), "dp").astype(jnp.float32),
        lax.psum(grad_first_shrink.astype(jnp.bfloat16), "dp").astype(jnp.float32),
        lax.psum(grad_joined.astype(jnp.bfloat16), "dp").astype(jnp.float32),
        lax.psum(grad_self_out.astype(jnp.bfloat16), "dp").astype(jnp.float32),
        lax.psum(grad_second_expand.astype(jnp.bfloat16), "dp").astype(jnp.float32),
        lax.psum(grad_second_shrink.astype(jnp.bfloat16), "dp").astype(jnp.float32),
    )
    gains_local = jnp.stack([grad_cross_gain, grad_first_gain, grad_self_gain, grad_second_gain])
    padded = lax.dynamic_update_slice(
        jnp.zeros((4, width_row * lax.axis_size("row")), full_type),
        gains_local,
        (jnp.int32(0), row_at * width_row),
    )
    shared = lax.psum((grad_key_sum, grad_value_sum, padded, input_gain_part), ("row", "col", "dp"))
    gains_all = lax.dynamic_slice_in_dim(shared[2], row_at * width_row, width_row, 1)
    joined_sum = grid[4]
    return (
        result,
        grad_latents,
        grad_inputs,
        gains_all[0],
        shared[3],
        grid[0],
        shared[0],
        shared[1],
        grid[1],
        gains_all[1],
        grid[2],
        grid[3],
        gains_all[2],
        joined_sum[:, :column_width_count],
        joined_sum[:, column_width_count : 2 * column_width_count],
        joined_sum[:, 2 * column_width_count :],
        grid[5],
        gains_all[3],
        grid[6],
        grid[7],
    )


def solution(mesh):
    placed = (
        P("dp", "col", "row"),
        P("dp", "col", None),
        P("dp", None),
        P("dp", None),
        P("dp", "col", "row"),
        P("row"),
        P(),
        P("row", "col"),
        P(),
        P(),
        P("col", "row"),
        P("row"),
        P("row", "col"),
        P("col", "row"),
        P("row"),
        P("row", "col"),
        P("row", "col"),
        P("row", "col"),
        P("col", "row"),
        P("row"),
        P("row", "col"),
        P("col", "row"),
    )
    return jax.shard_map(
        on_device,
        mesh=mesh,
        in_specs=placed,
        out_specs=(
            P("dp", "col", "row"),
            P("dp", "col", "row"),
            P("dp", "col", None),
            P("row"),
            P(),
            P("row", "col"),
            P(),
            P(),
            P("col", "row"),
            P("row"),
            P("row", "col"),
            P("col", "row"),
            P("row"),
            P("row", "col"),
            P("row", "col"),
            P("row", "col"),
            P("col", "row"),
            P("row"),
            P("row", "col"),
            P("col", "row"),
        ),
        check_vma=False,
    )
```

profile of v0, /device:TPU:0, one launch (start us, length us, event | category | flops | bytes accessed | tf_op | source)
XLA Modules:
  0.0 1149.1 jit_solution(11747873479767062708)
XLA Ops:
  8.5 5.9 all-reduce.9
  16.3 18.6 %all-gather.17.cloned.1.call-done = bf16[1,1024,512]{2,1,0:T(8,128)(2,1)} async-done(((bf16[1,256,512]{2,1,0:T(8,128)(2,1)}), bf16[1,1024,512]{2,1,0:T(8,128)(2,1)}) %all-gather.17.cloned.1.call-update) | async-done | bytes 1048592 | tf_op jit(solution)/shard_map/all_gather | solution.py:34
  37.6 14.8 %reduce-scatter.19.cloned.1.call-done = bf16[1,512,256]{2,1,0:T(8,128)(2,1)} async-done(((bf16[1,1024,256]{2,1,0:T(8,128)(2,1)}), bf16[1,512,256]{2,1,0:T(8,128)(2,1)}) %reduce-scatter.19.cloned.1.call-update) | async-done | bytes 262160 | tf_op jit(solution)/shard_map/reduce_scatter | solution.py:38
  62.0 8.8 all-gather.19.cloned.1.call-done
  79.0 5.2 all-gather.3
  84.2 5.4 all-gather.2
  89.7 6.8 fusion.38
  96.6 36.4 %all-reduce.16.cloned.1.call-done = bf16[1,512,1024]{2,1,0:T(8,128)(2,1)} async-done(((bf16[1,512,1024]{2,1,0:T(8,128)(2,1)}), bf16[1,512,1024]{2,1,0:T(8,128)(2,1)}) %all-reduce.16.cloned.1.call-update) | async-done | bytes 1048592 | tf_op jit(solution)/shard_map/psum | solution.py:244
  134.0 8.4 all_gather.75
  144.7 25.5 %reduce-scatter.21.cloned.1.call-done = bf16[1,256,512]{2,1,0:T(8,128)(2,1)} async-done(((bf16[1,1024,512]{2,1,0:T(8,128)(2,1)}), bf16[1,256,512]{2,1,0:T(8,128)(2,1)}) %reduce-scatter.21.cloned.1.call-update) | async-done | bytes 262160 | tf_op jit(solution)/shard_map/reduce_scatter | solution.py:48
  178.1 16.8 %all-gather.21.cloned.1.call-done = bf16[1,1024,512]{2,1,0:T(8,128)(2,1)} async-done(((bf16[1,256,512]{2,1,0:T(8,128)(2,1)}), bf16[1,1024,512]{2,1,0:T(8,128)(2,1)}) %all-gather.21.cloned.1.call-update) | async-done | bytes 1048592 | tf_op jit(solution)/shard_map/all_gather | solution.py:34
  197.5 14.9 %reduce-scatter.23.cloned.1.call-done = bf16[1,512,256]{2,1,0:T(8,128)(2,1)} async-done(((bf16[1,1024,256]{2,1,0:T(8,128)(2,1)}), bf16[1,512,256]{2,1,0:T(8,128)(2,1)}) %reduce-scatter.23.cloned.1.call-update) | async-done | bytes 262160 | tf_op jit(solution)/shard_map/reduce_scatter | solution.py:38
  215.3 8.6 all_gather.77
  226.1 24.9 %reduce-scatter.25.cloned.1.call-done = bf16[1,256,512]{2,1,0:T(8,128)(2,1)} async-done(((bf16[1,1024,512]{2,1,0:T(8,128)(2,1)}), bf16[1,256,512]{2,1,0:T(8,128)(2,1)}) %reduce-scatter.25.cloned.1.call-update) | async-done | bytes 262160 | tf_op jit(solution)/shard_map/reduce_scatter | solution.py:48
  258.1 16.7 %all-gather.23.cloned.1.call-done = bf16[1,1024,512]{2,1,0:T(8,128)(2,1)} async-done(((bf16[1,256,512]{2,1,0:T(8,128)(2,1)}), bf16[1,1024,512]{2,1,0:T(8,128)(2,1)}) %all-gather.23.cloned.1.call-update) | async-done | bytes 1048592 | tf_op jit(solution)/shard_map/all_gather | solution.py:34
  278.3 26.2 %reduce-scatter.27.cloned.1.call-done = bf16[1,512,768]{2,1,0:T(8,128)(2,1)} async-done(((bf16[1,1024,768]{2,1,0:T(8,128)(2,1)}), bf16[1,512,768]{2,1,0:T(8,128)(2,1)}) %reduce-scatter.27.cloned.1.call-update) | async-done | bytes 786448 | tf_op jit(solution)/shard_map/reduce_scatter | solution.py:38
  307.1 20.9 %all-gather.25.cloned.1.call-done = bf16[1,1024,512]{2,1,0:T(8,128)(2,1)} async-done(((bf16[1,512,512]{2,1,0:T(8,128)(2,1)}), bf16[1,1024,512]{2,1,0:T(8,128)(2,1)}) %all-gather.25.cloned.1.call-update) | async-done | bytes 1048592 | tf_op jit(solution)/shard_map/all_gather | solution.py:44
  337.5 8.9 all_gather.80
  349.6 24.1 %reduce-scatter.29.cloned.1.call-done = bf16[1,256,512]{2,1,0:T(8,128)(2,1)} async-done(((bf16[1,1024,512]{2,1,0:T(8,128)(2,1)}), bf16[1,256,512]{2,1,0:T(8,128)(2,1)}) %reduce-scatter.29.cloned.1.call-update) | async-done | bytes 262160 | tf_op jit(solution)/shard_map/reduce_scatter | solution.py:48
  380.7 11.3 all-gather.29.cloned.1.call-done
  394.5 16.2 %all-gather.27.cloned.1.call-done = bf16[1,1024,512]{2,1,0:T(8,128)(2,1)} async-done(((bf16[1,256,512]{2,1,0:T(8,128)(2,1)}), bf16[1,1024,512]{2,1,0:T(8,128)(2,1)}) %all-gather.27.cloned.1.call-update) | async-done | bytes 1048592 | tf_op jit(solution)/shard_map/all_gather | solution.py:34
  413.2 14.8 %reduce-scatter.35.cloned.1.call-done = bf16[1,512,256]{2,1,0:T(8,128)(2,1)} async-done(((bf16[1,1024,256]{2,1,0:T(8,128)(2,1)}), bf16[1,512,256]{2,1,0:T(8,128)(2,1)}) %reduce-scatter.35.cloned.1.call-update) | async-done | bytes 262160 | tf_op jit(solution)/shard_map/reduce_scatter | solution.py:38
  428.0 17.3 %reduce-scatter.31.cloned.1.call-done = bf16[1,512,256]{2,1,0:T(8,128)(2,1)} async-done(((bf16[1,1024,256]{2,1,0:T(8,128)(2,1)}), bf16[1,512,256]{2,1,0:T(8,128)(2,1)}) %reduce-scatter.31.cloned.1.call-update) | async-done | bytes 262160 | tf_op jit(solution)/shard_map/reduce_scatter | solution.py:38
  447.6 8.5 all_gather.84
  459.5 7.8 all_gather.82
  469.6 13.7 %reduce-scatter.37.cloned.1.call-done = bf16[1,256,512]{2,1,0:T(8,128)(2,1)} async-done(((bf16[1,1024,512]{2,1,0:T(8,128)(2,1)}), bf16[1,256,512]{2,1,0:T(8,128)(2,1)}) %reduce-scatter.37.cloned.1.call-update) | async-done | bytes 262160 | tf_op jit(solution)/shard_map/reduce_scatter | solution.py:48
  489.6 21.6 %reduce-scatter.33.cloned.1.call-done = bf16[1,256,512]{2,1,0:T(8,128)(2,1)} async-done(((bf16[1,1024,512]{2,1,0:T(8,128)(2,1)}), bf16[1,256,512]{2,1,0:T(8,128)(2,1)}) %reduce-scatter.33.cloned.1.call-update) | async-done | bytes 262160 | tf_op jit(solution)/shard_map/reduce_scatter | solution.py:48
  513.5 16.8 %all-gather.31.cloned.1.call-done = bf16[1,1024,512]{2,1,0:T(8,128)(2,1)} async-done(((bf16[1,256,512]{2,1,0:T(8,128)(2,1)}), bf16[1,1024,512]{2,1,0:T(8,128)(2,1)}) %all-gather.31.cloned.1.call-update) | async-done | bytes 1048592 | tf_op jit(solution)/shard_map/all_gather | solution.py:34
  532.9 14.8 %reduce-scatter.39.cloned.1.call-done = bf16[1,512,256]{2,1,0:T(8,128)(2,1)} async-done(((bf16[1,1024,256]{2,1,0:T(8,128)(2,1)}), bf16[1,512,256]{2,1,0:T(8,128)(2,1)}) %reduce-scatter.39.cloned.1.call-update) | async-done | bytes 262160 | tf_op jit(solution)/shard_map/reduce_scatter | solution.py:38
  563.1 17.9 %reduce-scatter.41.cloned.1.call-done = bf16[1,512,512]{1,2,0:T(8,128)(2,1)} async-done(((bf16[1,1024,512]{1,2,0:T(8,128)(2,1)}), bf16[1,512,512]{1,2,0:T(8,128)(2,1)}) %reduce-scatter.41.cloned.1.call-update) | async-done | bytes 524304 | tf_op jit(solution)/shard_map/reduce_scatter | solution.py:38
  583.1 27.3 %all-gather.33.cloned.1.call-done = bf16[1,1024,768]{1,2,0:T(8,128)(2,1)} async-done(((bf16[1,512,768]{1,2,0:T(8,128)(2,1)}), bf16[1,1024,768]{1,2,0:T(8,128)(2,1)}) %all-gather.33.cloned.1.call-update) | async-done | bytes 1572880 | tf_op jit(solution)/shard_map/all_gather | solution.py:44
  613.9 25.0 %reduce-scatter.43.cloned.1.call-done = bf16[1,256,512]{2,1,0:T(8,128)(2,1)} async-done(((bf16[1,1024,512]{2,1,0:T(8,128)(2,1)}), bf16[1,256,512]{2,1,0:T(8,128)(2,1)}) %reduce-scatter.43.cloned.1.call-update) | async-done | bytes 262160 | tf_op jit(solution)/shard_map/reduce_scatter | solution.py:48
  647.3 16.6 %all-gather.35.cloned.1.call-done = bf16[1,1024,512]{2,1,0:T(8,128)(2,1)} async-done(((bf16[1,256,512]{2,1,0:T(8,128)(2,1)}), bf16[1,1024,512]{2,1,0:T(8,128)(2,1)}) %all-gather.35.cloned.1.call-update) | async-done | bytes 1048592 | tf_op jit(solution)/shard_map/all_gather | solution.py:34
  666.4 14.9 %reduce-scatter.45.cloned.1.call-done = bf16[1,512,256]{2,1,0:T(8,128)(2,1)} async-done(((bf16[1,1024,256]{2,1,0:T(8,128)(2,1)}), bf16[1,512,256]{2,1,0:T(8,128)(2,1)}) %reduce-scatter.45.cloned.1.call-update) | async-done | bytes 262160 | tf_op jit(solution)/shard_map/reduce_scatter | solution.py:38
  682.5 8.7 all_gather.88
  693.6 24.9 %reduce-scatter.47.cloned.1.call-done = bf16[1,256,512]{2,1,0:T(8,128)(2,1)} async-done(((bf16[1,1024,512]{2,1,0:T(8,128)(2,1)}), bf16[1,256,512]{2,1,0:T(8,128)(2,1)}) %reduce-scatter.47.cloned.1.call-update) | async-done | bytes 262160 | tf_op jit(solution)/shard_map/reduce_scatter | solution.py:48
  726.9 16.8 %all-gather.37.cloned.1.call-done = bf16[1,1024,512]{2,1,0:T(8,128)(2,1)} async-done(((bf16[1,256,512]{2,1,0:T(8,128)(2,1)}), bf16[1,1024,512]{2,1,0:T(8,128)(2,1)}) %all-gather.37.cloned.1.call-update) | async-done | bytes 1048592 | tf_op jit(solution)/shard_map/all_gather | solution.py:34
  746.3 14.9 %reduce-scatter.49.cloned.1.call-done = bf16[1,512,256]{2,1,0:T(8,128)(2,1)} async-done(((bf16[1,1024,256]{2,1,0:T(8,128)(2,1)}), bf16[1,512,256]{2,1,0:T(8,128)(2,1)}) %reduce-scatter.49.cloned.1.call-update) | async-done | bytes 262160 | tf_op jit(solution)/shard_map/reduce_scatter | solution.py:38
  761.3 18.4 %all-gather.39.cloned.1.call-done = bf16[1,512,1024]{2,1,0:T(8,128)(2,1)} async-done(((bf16[1,512,256]{2,1,0:T(8,128)(2,1)}), bf16[1,512,1024]{2,1,0:T(8,128)(2,1)}) %all-gather.39.cloned.1.call-update) | async-done | bytes 1048592 | tf_op jit(solution)/shard_map/all_gather | solution.py:54
  781.2 6.7 multiply_convert_fusion.1
  810.9 6.6 reduce-scatter.51.cloned.1.call-done
  817.6 8.7 all_gather.91
  842.3 5.3 fusion.213
  847.6 5.6 fusion.95
  865.9 22.8 %reduce-scatter.53.cloned.1.call-done = bf16[1,256,512]{2,1,0:T(8,128)(2,1)} async-done(((bf16[1,1024,512]{2,1,0:T(8,128)(2,1)}), bf16[1,256,512]{2,1,0:T(8,128)(2,1)}) %reduce-scatter.53.cloned.1.call-update) | async-done | bytes 262160 | tf_op jit(solution)/shard_map/reduce_scatter | solution.py:48
  894.9 43.3 %all-reduce = (f32[4,1024]{1,0:T(4,128)S(1)}, f32[261]{0:T(512)}) all-reduce(f32[4,1024]{1,0:T(4,128)S(1)} %maximum_dynamic-update-slice_fusion, f32[261]{0:T(512)S(1)} %get-tuple-element.218), channel_id=1, replica_groups=mesh['row'=2,'col'=4,'dp'=4] {'row','col','dp'}, use_global_device_ids=true, to_apply=%region_69.70 | all-reduce | flops 4357 | bytes 34856 | tf_op jit(solution)/shard_map/psum | solution.py:417
  940.9 56.9 %all-reduce.22.cloned.1.call-done = (bf16[512,256]{1,0:T(8,128)(2,1)}, bf16[256,512]{1,0:T(8,128)(2,1)}, bf16[512,256]{1,0:T(8,128)(2,1)}, bf16[256,512]{1,0:T(8...) async-done(((bf16[512,256]{1,0:T(8,128)(2,1)}, bf16[256,512]{1,0:T(8,128)(2,1)}, ...) | async-done | bytes 2621456 | tf_op jit(solution)/shard_map/psum | solution.py:402
  1008.0 130.4 %all-reduce.20.cloned.1.call-done = (f32[261,1024]{1,0:T(8,128)}, f32[261,1024]{1,0:T(8,128)}) async-done(((f32[261,1024]{1,0:T(8,128)}, f32[261,1024]{1,0:T(8,128)}), (f32[261,1024]{1,0:T(8,128)}, f32[261,1024]{1,0:T(8,128)})) %all-reduce.20.cloned.1.call-update) | async-done | bytes 2138128 | tf_op jit(solution)/shard_map/psum | solution.py:417
  (377 shorter events, 221.1 us)
Async XLA Ops:
  7.2 50.3 %copy-start = (bf16[261,1024]{1,0:T(8,128)(2,1)S(1)}, bf16[261,1024]{1,0:T(8,128)(2,1)}, u32[]{:S(2)}) copy-start(bf16[261,1024]{1,0:T(8,128)(2,1)} %param.32) | copy-start | bytes 1603588
  7.2 27.7 %all-gather.17.cloned.1.call-start = ((), (), s32[]{:S(2)}) async-start(), calls=%async_computation.18 | async-start | bytes 1310720 | tf_op jit(solution)/shard_map/all_gather | solution.py:34
  16.3 36.1 %reduce-scatter.19.cloned.1.call-start = ((), (), s32[]{:S(2)}) async-start(), calls=%async_computation.19 | async-start | bytes 786432 | tf_op jit(solution)/shard_map/reduce_scatter | solution.py:38
  37.4 33.4 %all-gather.19.cloned.1.call-start = ((), (), s32[]{:S(2)}) async-start(), calls=%async_computation.20 | async-start | bytes 1310720 | tf_op jit(solution)/shard_map/all_gather | solution.py:54
  52.4 80.6 %all-reduce.16.cloned.1.call-start = ((), (), s32[]{:S(2)}) async-start(), calls=%async_computation.21 | async-start | bytes 2097152 | tf_op jit(solution)/shard_map/psum | solution.py:244
  96.6 46.6 %copy-start.46 = (bf16[256,512]{1,0:T(8,128)(2,1)S(1)}, bf16[256,512]{1,0:T(8,128)(2,1)}, u32[]{:S(2)}) copy-start(bf16[256,512]{1,0:T(8,128)(2,1)} %param.34) | copy-start | bytes 786436
  96.6 73.6 %copy-start.3 = (bf16[1,256,512]{2,1,0:T(8,128)(2,1)S(1)}, bf16[1,256,512]{2,1,0:T(8,128)(2,1)}, u32[]{:S(2)}) copy-start(bf16[1,256,512]{2,1,0:T(8,128)(2,1)} %param.24) | copy-start | bytes 786436
  96.6 73.5 %reduce-scatter.21.cloned.1.call-start = ((), (), s32[]{:S(2)}) async-start(), calls=%async_computation.22 | async-start | bytes 1310720 | tf_op jit(solution)/shard_map/reduce_scatter | solution.py:48
  143.2 51.8 %copy-start.44 = (bf16[512,256]{1,0:T(8,128)(2,1)S(1)}, bf16[512,256]{1,0:T(8,128)(2,1)}, u32[]{:S(2)}) copy-start(bf16[512,256]{1,0:T(8,128)(2,1)} %param.36) | copy-start | bytes 786436
  144.6 50.3 %all-gather.21.cloned.1.call-start = ((), (), s32[]{:S(2)}) async-start(), calls=%async_computation.23 | async-start | bytes 1310720 | tf_op jit(solution)/shard_map/all_gather | solution.py:34
  178.1 34.3 %reduce-scatter.23.cloned.1.call-start = ((), (), s32[]{:S(2)}) async-start(), calls=%async_computation.24 | async-start | bytes 786432 | tf_op jit(solution)/shard_map/reduce_scatter | solution.py:38
  197.4 53.6 %copy-start.8 = (bf16[1,256,512]{2,1,0:T(8,128)(2,1)S(1)}, bf16[1,256,512]{2,1,0:T(8,128)(2,1)}, u32[]{:S(2)}) copy-start(bf16[1,256,512]{2,1,0:T(8,128)(2,1)} %reduce-scatter.21.cloned.1.call-done) | copy-start | bytes 786436
  197.4 53.6 %reduce-scatter.25.cloned.1.call-start = ((), (), s32[]{:S(2)}) async-start(), calls=%async_computation.25 | async-start | bytes 1310720 | tf_op jit(solution)/shard_map/reduce_scatter | solution.py:48
  226.1 48.8 %all-gather.23.cloned.1.call-start = ((), (), s32[]{:S(2)}) async-start(), calls=%async_computation.26 | async-start | bytes 1310720 | tf_op jit(solution)/shard_map/all_gather | solution.py:34
  258.0 46.6 %reduce-scatter.27.cloned.1.call-start = ((), (), s32[]{:S(2)}) async-start(), calls=%async_computation.27 | async-start | bytes 2359296 | tf_op jit(solution)/shard_map/reduce_scatter | solution.py:38
  278.2 49.7 %all-gather.25.cloned.1.call-start = ((), (), s32[]{:S(2)}) async-start(), calls=%async_computation.28 | async-start | bytes 1572864 | tf_op jit(solution)/shard_map/all_gather | solution.py:44
  306.5 67.2 %reduce-scatter.29.cloned.1.call-start = ((), (), s32[]{:S(2)}) async-start(), calls=%async_computation.29 | async-start | bytes 1310720 | tf_op jit(solution)/shard_map/reduce_scatter | solution.py:48
  306.9 241.8 %copy-start.12 = (pred[512,1024]{1,0:T(8,128)(4,1)}, pred[512,1024]{1,0:T(8,128)(4,1)S(1)}, u32[]{:S(2)}) copy-start(pred[512,1024]{1,0:T(8,128)(4,1)S(1)} %broadcast_compare_fusion) | copy-start | bytes 1572868
  348.7 43.2 %all-gather.29.cloned.1.call-start = ((), (), s32[]{:S(2)}) async-start(), calls=%async_computation.33 | async-start | bytes 1310720 | tf_op jit(solution)/shard_map/all_gather | solution.py:34
  349.5 61.2 %copy-start.38 = (bf16[512,256]{1,0:T(8,128)(2,1)S(1)}, bf16[512,256]{1,0:T(8,128)(2,1)}, u32[]{:S(2)}) copy-start(bf16[512,256]{1,0:T(8,128)(2,1)} %param.44) | copy-start | bytes 786436
  349.5 61.2 %all-gather.27.cloned.1.call-start = ((), (), s32[]{:S(2)}) async-start(), calls=%async_computation.30 | async-start | bytes 1310720 | tf_op jit(solution)/shard_map/all_gather | solution.py:34
  380.6 47.4 %reduce-scatter.35.cloned.1.call-start = ((), (), s32[]{:S(2)}) async-start(), calls=%async_computation.34 | async-start | bytes 786432 | tf_op jit(solution)/shard_map/reduce_scatter | solution.py:38
  394.5 50.9 %reduce-scatter.31.cloned.1.call-start = ((), (), s32[]{:S(2)}) async-start(), calls=%async_computation.31 | async-start | bytes 786432 | tf_op jit(solution)/shard_map/reduce_scatter | solution.py:38
  413.2 70.2 %reduce-scatter.37.cloned.1.call-start = ((), (), s32[]{:S(2)}) async-start(), calls=%async_computation.35 | async-start | bytes 1310720 | tf_op jit(solution)/shard_map/reduce_scatter | solution.py:48
  458.4 52.8 %reduce-scatter.33.cloned.1.call-start = ((), (), s32[]{:S(2)}) async-start(), calls=%async_computation.32 | async-start | bytes 1310720 | tf_op jit(solution)/shard_map/reduce_scatter | solution.py:48
  459.5 51.7 %copy-start.56 = (bf16[1,256,512]{2,1,0:T(8,128)(2,1)S(1)}, bf16[1,256,512]{2,1,0:T(8,128)(2,1)}, u32[]{:S(2)}) copy-start(bf16[1,256,512]{2,1,0:T(8,128)(2,1)} %param.28) | copy-start | bytes 786436
  469.5 60.8 %copy-start.41 = (bf16[256,512]{1,0:T(8,128)(2,1)S(1)}, bf16[256,512]{1,0:T(8,128)(2,1)}, u32[]{:S(2)}) copy-start(bf16[256,512]{1,0:T(8,128)(2,1)} %param.42) | copy-start | bytes 786436
  469.6 60.7 %all-gather.31.cloned.1.call-start = ((), (), s32[]{:S(2)}) async-start(), calls=%async_computation.36 | async-start | bytes 1310720 | tf_op jit(solution)/shard_map/all_gather | solution.py:34
  513.5 34.2 %reduce-scatter.39.cloned.1.call-start = ((), (), s32[]{:S(2)}) async-start(), calls=%async_computation.37 | async-start | bytes 786432 | tf_op jit(solution)/shard_map/reduce_scatter | solution.py:38
  532.8 48.2 %reduce-scatter.41.cloned.1.call-start = ((), (), s32[]{:S(2)}) async-start(), calls=%async_computation.38 | async-start | bytes 1572864 | tf_op jit(solution)/shard_map/reduce_scatter | solution.py:38
  560.4 50.0 %all-gather.33.cloned.1.call-start = ((), (), s32[]{:S(2)}) async-start(), calls=%async_computation.39 | async-start | bytes 2359296 | tf_op jit(solution)/shard_map/all_gather | solution.py:44
  563.0 47.3 %copy-start.69 = (bf16[512,768]{1,0:T(8,128)(2,1)S(1)}, bf16[512,768]{1,0:T(8,128)(2,1)}, u32[]{:S(2)}) copy-start(bf16[512,768]{1,0:T(8,128)(2,1)} %copy-done.68) | copy-start | bytes 2359300
  583.0 55.8 %reduce-scatter.43.cloned.1.call-start = ((), (), s32[]{:S(2)}) async-start(), calls=%async_computation.40 | async-start | bytes 1310720 | tf_op jit(solution)/shard_map/reduce_scatter | solution.py:48
  613.8 50.1 %copy-start.43 = (bf16[256,512]{1,0:T(8,128)(2,1)S(1)}, bf16[256,512]{1,0:T(8,128)(2,1)}, u32[]{:S(2)}) copy-start(bf16[256,512]{1,0:T(8,128)(2,1)} %param.37) | copy-start | bytes 786436
  613.8 50.0 %all-gather.35.cloned.1.call-start = ((), (), s32[]{:S(2)}) async-start(), calls=%async_computation.41 | async-start | bytes 1310720 | tf_op jit(solution)/shard_map/all_gather | solution.py:34
  647.0 34.3 %reduce-scatter.45.cloned.1.call-start = ((), (), s32[]{:S(2)}) async-start(), calls=%async_computation.42 | async-start | bytes 786432 | tf_op jit(solution)/shard_map/reduce_scatter | solution.py:38
  666.4 52.0 %reduce-scatter.47.cloned.1.call-start = ((), (), s32[]{:S(2)}) async-start(), calls=%async_computation.43 | async-start | bytes 1310720 | tf_op jit(solution)/shard_map/reduce_scatter | solution.py:48
  693.5 50.3 %copy-start.47 = (bf16[256,512]{1,0:T(8,128)(2,1)S(1)}, bf16[256,512]{1,0:T(8,128)(2,1)}, u32[]{:S(2)}) copy-start(bf16[256,512]{1,0:T(8,128)(2,1)} %param.34) | copy-start | bytes 786436
  693.5 50.2 %all-gather.37.cloned.1.call-start = ((), (), s32[]{:S(2)}) async-start(), calls=%async_computation.44 | async-start | bytes 1310720 | tf_op jit(solution)/shard_map/all_gather | solution.py:34
  724.7 54.9 %copy-start.36 = (bf16[1,512,1024]{2,1,0:T(8,128)(2,1)S(1)}, bf16[1,512,1024]{2,1,0:T(8,128)(2,1)}, u32[]{:S(2)}) copy-start(bf16[1,512,1024]{2,1,0:T(8,128)(2,1)} %all-reduce.16.cloned.1.call-done) | copy-start | bytes 3145732
  726.9 34.3 %reduce-scatter.49.cloned.1.call-start = ((), (), s32[]{:S(2)}) async-start(), calls=%async_computation.45 | async-start | bytes 786432 | tf_op jit(solution)/shard_map/reduce_scatter | solution.py:38
  746.2 33.4 %all-gather.39.cloned.1.call-start = ((), (), s32[]{:S(2)}) async-start(), calls=%async_computation.46 | async-start | bytes 1310720 | tf_op jit(solution)/shard_map/all_gather | solution.py:54
  761.2 56.3 %reduce-scatter.51.cloned.1.call-start = ((), (), s32[]{:S(2)}) async-start(), calls=%async_computation.47 | async-start | bytes 1310720 | tf_op jit(solution)/shard_map/reduce_scatter | solution.py:58
  792.6 68.7 %all-reduce.18.cloned.1.call-start = ((), (), s32[]{:S(2)}) async-start(), calls=%async_computation.49 | async-start | bytes 2162688 | tf_op jit(solution)/shard_map/psum | solution.py:399
  810.9 77.8 %reduce-scatter.53.cloned.1.call-start = ((), (), s32[]{:S(2)}) async-start(), calls=%async_computation.48 | async-start | bytes 1310720 | tf_op jit(solution)/shard_map/reduce_scatter | solution.py:48
  828.6 169.2 %all-reduce.22.cloned.1.call-start = ((), (), s32[]{:S(2)}) async-start(), calls=%async_computation.51 | async-start | bytes 5242880 | tf_op jit(solution)/shard_map/psum | solution.py:402
  842.2 296.2 %all-reduce.20.cloned.1.call-start = ((), (), s32[]{:S(2)}) async-start(), calls=%async_computation.50 | async-start | bytes 4325376 | tf_op jit(solution)/shard_map/psum | solution.py:417
  864.1 74.8 %copy-start.29 = (f32[1,256,512]{2,1,0:T(8,128)S(1)}, f32[1,256,512]{2,1,0:T(8,128)}, u32[]{:S(2)}) copy-start(f32[1,256,512]{2,1,0:T(8,128)} %get-tuple-element.282) | copy-start | bytes 1572868
  (73 other events, 948.7 us)
Sparse Core Ops, SparseCore 0:
  16.4 18.4 all-gather.16
  37.7 14.6 reduce-scatter.18
  53.9 16.8 all-gather.18
  96.7 36.2 all-reduce.15
  144.7 25.3 reduce-scatter.20
  178.2 16.6 all-gather.20
  197.7 14.6 reduce-scatter.22
  226.2 24.7 reduce-scatter.24
  258.1 16.6 all-gather.22
  278.3 26.1 reduce-scatter.26
  306.7 21.2 all-gather.24
  348.9 24.7 reduce-scatter.28
  375.2 16.6 all-gather.28
  394.0 16.6 all-gather.26
  413.3 14.6 reduce-scatter.34
  430.7 14.6 reduce-scatter.30
  458.5 24.7 reduce-scatter.36
  486.3 24.8 reduce-scatter.32
  513.6 16.6 all-gather.30
  533.0 14.6 reduce-scatter.38
  560.5 20.3 reduce-scatter.40
  583.2 27.1 all-gather.32
  613.9 24.8 reduce-scatter.42
  647.1 16.6 all-gather.34
  666.7 14.6 reduce-scatter.44
  693.6 24.7 reduce-scatter.46
  727.0 16.6 all-gather.36
  746.5 14.6 reduce-scatter.48
  762.8 16.8 all-gather.38
  792.7 24.7 reduce-scatter.50
  820.4 40.7 all-reduce.17
  863.8 24.8 reduce-scatter.52
  892.6 105.1 all-reduce.21
  1004.2 134.1 all-reduce.19
where the time goes:
time: 1160 us; the launch traced here: 1150 us
  waiting for transfers between devices  773 us (67%)
  blocking collectives  154 us (13%)
  matrix products  121 us (10%)
  other arithmetic  53.9 us (5%)
  local copies, waits for them, and re-layouts  29.8 us (3%)
  between operations  15.9 us (1%)
    reduce_scatter x8, waiting for transfers between devices, col_reduce(): lax.psum_scatter(value.astype(jnp.bfloat16), 'col', scatter_dimension=1,...  182 us
    reduce_scatter x9, waiting for transfers between devices, row_reduce(): lax.psum_scatter(value.astype(jnp.bfloat16), 'row', scatter_dimension=1,...  151 us
    psum x1, waiting for transfers between devices, on_device(): lax.psum((grad_key_sum, grad_value_sum, padded, input_gain_part), ('row',...  130 us
    all_gather x8, waiting for transfers between devices, col_rows(): return lax.all_gather(value, 'col', axis=1, tiled=True)  130 us
    all_gather x7, blocking collectives, row_rows(): return lax.all_gather(value, 'row', axis=1, tiled=True)  59.6 us
    psum x1, waiting for transfers between devices, on_device(): lax.psum(grad_cross_query.astype(jnp.bfloat16), 'dp').astype(jnp.float32)  56.9 us
    all_gather x2, waiting for transfers between devices, row_rows(): return lax.all_gather(value, 'row', axis=1, tiled=True)  48.2 us
    psum x1, blocking collectives, on_device(): lax.psum((grad_key_sum, grad_value_sum, padded, input_gain_part), ('row',...  43.3 us
  transfers between devices with their start and end apart: 34, of which 34 were waited for; matrix products, arithmetic and copies ran while one was open for 7% of the time, Pallas kernels for 0%

commit v1 on v0

--- a/solution.py
+++ b/solution.py
@@ -1,8 +1,11 @@
+import functools
 import math
 
 import jax
 import jax.numpy as jnp
 from jax import lax
+from jax.experimental import pallas as pl
+from jax.experimental.pallas import tpu as pltpu
 from jax.sharding import PartitionSpec as P
 
 D = 1024
@@ -441,6 +444,769 @@
     )
 
 
+NEG = -1e30
+WIDE = 256
+BLOCK = 128
+
+
+def col_step(flip):
+    return tuple((c, c ^ flip) for c in range(4))
+
+
+ROW_SWAP = ((0, 1), (1, 0))
+BOTH_SWAP = tuple((r * 4 + c, (1 - r) * 4 + (c ^ 2)) for r in range(2) for c in range(4))
+SEQ_NEAR = ((0, 1), (1, 0), (2, 3), (3, 2))
+SEQ_FAR = ((0, 2), (2, 0), (1, 3), (3, 1))
+GROUP = ("col", "row")
+
+
+def swap_row(value):
+    return lax.ppermute(value, "row", ROW_SWAP)
+
+
+def swap_chip(value):
+    return lax.ppermute(value, "col", col_step(2))
+
+
+def swap_core(value):
+    return lax.ppermute(value, "col", col_step(1))
+
+
+def swap_both(value):
+    return lax.ppermute(value, ("row", "col"), BOTH_SWAP)
+
+
+def gather_eight(value):
+    near = jnp.stack([value, swap_row(value), swap_chip(value), swap_both(value)])
+    return near, swap_core(near)
+
+
+def exchange(value):
+    return lax.all_to_all(value, GROUP, 0, 0, tiled=True)
+
+
+def kernel(body, outs, *args, scratch=(), scalars=True, cost=None):
+    vmem = pl.BlockSpec(memory_space=pltpu.VMEM)
+    smem = pl.BlockSpec(memory_space=pltpu.SMEM)
+    specs = [smem if scalars and i == 0 else vmem for i in range(len(args))]
+    return pl.pallas_call(
+        body,
+        out_shape=tuple(jax.ShapeDtypeStruct(shape, kind) for shape, kind in outs),
+        in_specs=specs,
+        out_specs=tuple(vmem for _ in outs),
+        scratch_shapes=list(scratch),
+        compiler_params=pltpu.CompilerParams(vmem_limit_bytes=56 * 1024 * 1024),
+    )(*args)
+
+
+def mm(a, b):
+    return lax.dot_general(a, b, (((1,), (0,)), ((), ())), preferred_element_type=jnp.float32)
+
+
+def mt(a, b):
+    return lax.dot_general(a, b, (((1,), (1,)), ((), ())), preferred_element_type=jnp.float32)
+
+
+def low(v):
+    return v.astype(jnp.bfloat16)
+
+
+def full(v):
+    return v.astype(jnp.float32)
+
+
+def norm_parts(value):
+    width = value.shape[-1]
+    center = jnp.sum(value, axis=-1, keepdims=True) / width
+    shifted = value - center
+    spread = jnp.sum(shifted * shifted, axis=-1, keepdims=True) / width
+    inv = lax.rsqrt(spread + EPS)
+    return shifted * inv, inv
+
+
+def norm_back(grad, gain, normed, inv):
+    width = grad.shape[-1]
+    scaled = grad * gain
+    first = jnp.sum(scaled, axis=-1, keepdims=True) / width
+    second = jnp.sum(scaled * normed, axis=-1, keepdims=True) / width
+    return inv * (scaled - first - normed * second), jnp.sum(grad * normed, axis=0, keepdims=True)
+
+
+def phi(value):
+    return 0.5 * (1.0 + lax.erf(value * (1.0 / math.sqrt(2.0))))
+
+
+def gelu_value(value):
+    return value * phi(value)
+
+
+def gelu_slope(value):
+    return phi(value) + value * jnp.exp(value * value * -0.5) * (1.0 / math.sqrt(2.0 * math.pi))
+
+
+def three(value):
+    first = low(value)
+    rest = value - full(first)
+    second = low(rest)
+    return full(first), full(second), rest - full(second)
+
+
+def block_of(scalars, step, core):
+    return scalars[0] ^ (4 * (step // 2) + 2 * core + step % 2)
+
+
+def rows_of(count, lanes):
+    return lax.broadcasted_iota(jnp.int32, (count, lanes), 0)
+
+
+def fold_kernel(scalars, key, value, query, out, parts):
+    at = pl.multiple_of(scalars[2] * WIDE, WIDE)
+    channels = key.shape[0]
+    parts[...] = jnp.zeros_like(parts)
+    first = low(mt(key[:, pl.ds(at, WIDE)], query[...]))
+    second = low(mm(value[:, pl.ds(at, WIDE)], out[...]))
+    for b in range(4):
+        parts[b, 0, 0:channels, :] = first[:, b * BLOCK : (b + 1) * BLOCK]
+        parts[b, 1, 0:channels, :] = second[:, b * BLOCK : (b + 1) * BLOCK]
+
+
+def add_kernel(parts, total):
+    acc = full(parts[0])
+    for b in range(1, parts.shape[0]):
+        acc = acc + full(parts[b])
+    total[...] = low(acc)
+
+
+def input_kernel(rows, gain, plain, turned, *, channels):
+    value = full(rows[...])
+    lanes = lax.broadcasted_iota(jnp.int32, value.shape, 1)
+    center = jnp.sum(value, axis=-1, keepdims=True) / channels
+    shifted = jnp.where(lanes < channels, value - center, 0.0)
+    spread = jnp.sum(shifted * shifted, axis=-1, keepdims=True) / channels
+    result = shifted * lax.rsqrt(spread + EPS) * gain[...]
+    plain[...] = low(result)
+    turned[...] = low(result.T)
+
+
+def first_kernel(latents, gain, normed):
+    value, _ = norm_parts(full(latents[...]))
+    normed[...] = low(value * gain[...])
+
+
+def query_kernel(scalars, near, far, normed, folded_query, folded_out, query):
+    row, col = scalars[1], scalars[2]
+    for step in range(4):
+        for core, source in ((0, near), (1, far)):
+            block = 4 * (row ^ (step % 2)) + (col ^ (2 * (step // 2) + core))
+            at = pl.multiple_of(block * BLOCK, BLOCK)
+            folded_query[:, pl.ds(at, BLOCK)] = source[step, 0]
+            folded_out[:, pl.ds(at, BLOCK)] = source[step, 1]
+    query[...] = low(mt(folded_query[...], normed[...]) * (1.0 / math.sqrt(D)))
+
+
+def cross_kernel(scalars, near, far, limits, plain, turned, queries, result, *, channels):
+    for step in range(4):
+        for core, source in ((0, near), (1, far)):
+            queries[block_of(scalars, step, core)] = source[step]
+    base = scalars[3]
+    count, padded = plain.shape
+
+    def pair(i, carry):
+        query = jnp.concatenate([queries[2 * i], queries[2 * i + 1]], axis=1)
+        limit = jnp.concatenate([limits[2 * i], limits[2 * i + 1]], axis=1)
+        scores = mm(plain[...], query)
+        keys = rows_of(count, 2 * BLOCK) + base
+        mask = keys < limit
+        top = jnp.max(jnp.where(mask, scores, NEG), axis=0, keepdims=True)
+        weights = jnp.where(mask, jnp.exp(scores - top), 0.0)
+        total = jnp.sum(weights, axis=0, keepdims=True)
+        mixed = mm(turned[...], low(weights))
+        some = total > 0.0
+        mixed = mixed * jnp.where(some, 1.0 / jnp.where(some, total, 1.0), 0.0)
+        lse = jnp.where(some, top + jnp.log(jnp.where(some, total, 1.0)), NEG)
+        index = rows_of(padded, 2 * BLOCK)
+        for k, part in enumerate(three(lse)):
+            mixed = jnp.where(index == channels + k, part, mixed)
+        mixed = low(mixed)
+        result[2 * i] = mixed[:, :BLOCK]
+        result[2 * i + 1] = mixed[:, BLOCK:]
+        return carry
+
+    lax.fori_loop(0, 4, pair, 0)
+
+
+def expand_tiles(value, packed, at):
+    outs = []
+    for c in range(4):
+        acc = None
+        for r in range(2):
+            part = mm(value[:, r * 512 : (r + 1) * 512], packed[2 * c + r, at : at + 512, :])
+            acc = part if acc is None else acc + part
+        outs.append(acc)
+    return jnp.concatenate(outs, axis=1)
+
+
+def shrink_tiles(value, packed, at):
+    outs = []
+    for r in range(2):
+        for j in range(2):
+            acc = None
+            for c in range(4):
+                tile = packed[2 * c + r, at + j * WIDE : at + (j + 1) * WIDE, :]
+                part = mm(value[:, c * WIDE : (c + 1) * WIDE], tile)
+                acc = part if acc is None else acc + part
+            outs.append(acc)
+    return jnp.concatenate(outs, axis=1)
+
+
+def expand_back(value, packed, at):
+    outs = []
+    for r in range(2):
+        acc = None
+        for c in range(4):
+            part = mt(value[:, c * WIDE : (c + 1) * WIDE], packed[2 * c + r, at : at + 512, :])
+            acc = part if acc is None else acc + part
+        outs.append(acc)
+    return jnp.concatenate(outs, axis=1)
+
+
+def shrink_back(value, packed, at):
+    outs = []
+    for c in range(4):
+        acc = None
+        for r in range(2):
+            for j in range(2):
+                tile = packed[2 * c + r, at + j * WIDE : at + (j + 1) * WIDE, :]
+                start = r * 512 + j * WIDE
+                part = mt(value[:, start : start + WIDE], tile)
+                acc = part if acc is None else acc + part
+        outs.append(acc)
+    return jnp.concatenate(outs, axis=1)
+
+
+def merge_kernel(
+    parts, latents, folded_out, packed, gains,
+    mixed_out, lse_out, after_cross, hidden, upward, active, after_first, self_in, *, channels
+):
+    lses = []
+    for d in range(8):
+        rows = full(parts[d, channels : channels + 3, :])
+        lses.append(rows[0:1] + rows[1:2] + rows[2:3])
+    top = lses[0]
+    for item in lses[1:]:
+        top = jnp.maximum(top, item)
+    total = jnp.zeros_like(top)
+    mixed = jnp.zeros(parts.shape[1:], jnp.float32)
+    for d in range(8):
+        share = jnp.exp(lses[d] - top)
+        total = total + share
+        mixed = mixed + full(parts[d]) * share
+    mixed = low(mixed / total)
+    mixed_out[...] = mixed
+    lse_out[...] = top + jnp.log(total)
+    branch = mm(low(full(mixed).T), folded_out[...])
+    state = full(latents[...]) + branch
+    after_cross[...] = state
+    normed, _ = norm_parts(state)
+    hid = low(normed * gains[1:2, :])
+    hidden[...] = hid
+    up = expand_tiles(hid, packed, 0)
+    upward[...] = up
+    act = low(gelu_value(up))
+    active[...] = act
+    state = state + shrink_tiles(act, packed, 512)
+    after_first[...] = state
+    normed, _ = norm_parts(state)
+    self_in[...] = low(normed * gains[2:3, :])
+
+
+def attend_kernel(
+    scalars, near, far, weights, limits, places, rows_out, qkv_out, mixed_out, lse_out, sent
+):
+    for core, source in ((0, near), (1, far)):
+        for step in range(4):
+            at = pl.multiple_of(block_of(scalars, step, core) * BLOCK, BLOCK)
+            rows = source[step]
+            rows_out[pl.ds(at, BLOCK), :] = rows
+    qkv_out[...] = low(mm(rows_out[...], weights[...]))
+    scale = 1.0 / math.sqrt(HEAD)
+    turned = low(full(qkv_out[:, 2 * HEAD :]).T)
+
+    def pair(i, carry):
+        at = pl.multiple_of(i * WIDE, WIDE)
+        query = qkv_out[pl.ds(at, WIDE), 0:HEAD]
+        scores = mt(qkv_out[:, HEAD : 2 * HEAD], query) * scale
+        limit = jnp.concatenate([limits[2 * i], limits[2 * i + 1]], axis=1)
+        mask = places[...] < limit
+        top = jnp.max(jnp.where(mask, scores, NEG), axis=0, keepdims=True)
+        share = jnp.where(mask, jnp.exp(scores - top), 0.0)
+        total = jnp.sum(share, axis=0, keepdims=True)
+        mixed = mm(turned, low(share)) / total
+        mixed_out[:, pl.ds(at, WIDE)] = mixed
+        lse_out[:, pl.ds(at, WIDE)] = top + jnp.log(total)
+        lower = low(mixed)
+        sent[2 * i] = lower[:, :BLOCK]
+        sent[2 * i + 1] = lower[:, BLOCK:]
+        return carry
+
+    lax.fori_loop(0, 4, pair, 0)
+
+
+def second_kernel(
+    parts, after_first, cotangent, gain, packed,
+    out, joined, hidden, active, grad_up, grad_gain, branch_grad, state_grad, sent
+):
+    att = jnp.concatenate([full(parts[h]).T for h in range(8)], axis=1)
+    att = low(att)
+    joined[...] = att
+    state = after_first[...] + shrink_tiles(att, packed, 0)
+    normed, inv = norm_parts(state)
+    hid = low(normed * gain[...])
+    hidden[...] = hid
+    up = expand_tiles(hid, packed, 512)
+    act = low(gelu_value(up))
+    active[...] = act
+    final = state + shrink_tiles(act, packed, 1024)
+    out[...] = low(final)
+    grad = cotangent[...]
+    grad_act = shrink_back(grad, packed, 1024)
+    gu = low(grad_act * gelu_slope(up))
+    grad_up[...] = gu
+    grad_hid = expand_back(gu, packed, 512)
+    back, grad_gain[...] = norm_back(grad_hid, gain[...], normed, inv)
+    total = full(grad) + back
+    state_grad[...] = total
+    lower = low(total)
+    branch_grad[...] = lower
+    grad_att = shrink_back(lower, packed, 0)
+    for h in range(8):
+        sent[h] = low(grad_att[:, h * BLOCK : (h + 1) * BLOCK].T)
+
+
+def attend_back_kernel(
+    scalars, parts, qkv, mixed, lse, weights, limits, places, grads, sent
+):
+    scale = 1.0 / math.sqrt(HEAD)
+    keys_turned = low(full(qkv[:, HEAD : 2 * HEAD]).T)
+
+    def pair(i, carry):
+        grad_k, grad_v = carry
+        at = pl.multiple_of(i * WIDE, WIDE)
+        query = qkv[pl.ds(at, WIDE), 0:HEAD]
+        grad_out = jnp.concatenate([parts[2 * i], parts[2 * i + 1]], axis=1)
+        delta = jnp.sum(full(grad_out) * mixed[:, pl.ds(at, WIDE)], axis=0, keepdims=True)
+        scores = mt(qkv[:, HEAD : 2 * HEAD], query) * scale
+        limit = jnp.concatenate([limits[2 * i], limits[2 * i + 1]], axis=1)
+        mask = places[...] < limit
+        share = jnp.where(mask, jnp.exp(scores - lse[:, pl.ds(at, WIDE)]), 0.0)
+        grad_share = mm(qkv[:, 2 * HEAD :], grad_out)
+        grad_scores = low(share * (grad_share - delta))
+        grad_k = grad_k + mm(grad_scores, query)
+        grad_v = grad_v + mt(low(share), grad_out)
+        grad_q = mm(keys_turned, grad_scores) * scale
+        grads[pl.ds(at, WIDE), 0:HEAD] = low(grad_q.T)
+        return grad_k, grad_v
+
+    zero = jnp.zeros((qkv.shape[0], HEAD), jnp.float32)
+    grad_k, grad_v = lax.fori_loop(0, 4, pair, (zero, zero))
+    grads[:, HEAD : 2 * HEAD] = low(grad_k * scale)
+    grads[:, 2 * HEAD :] = low(grad_v)
+    for step in range(4):
+        for core in range(2):
+            at = pl.multiple_of(block_of(scalars, step, core) * BLOCK, BLOCK)
+            sent[core, step] = low(mt(grads[pl.ds(at, BLOCK), :], weights[...]))
+
+
+def first_back_kernel(
+    own, by_row, by_chip, by_both, state_grad, after_first, after_cross, upward, packed, gains,
+    folded_out, mixed, lse,
+    gain_grads, first_branch, grad_up, cross_branch, cross_grad, value_part, sent, *, channels
+):
+    grad_in = full(own[...]) + full(by_row[...]) + full(by_chip[...]) + full(by_both[...])
+    normed, inv = norm_parts(after_first[...])
+    back, self_gain = norm_back(grad_in, gains[2:3, :], normed, inv)
+    grad = state_grad[...] + back
+    lower = low(grad)
+    first_branch[...] = lower
+    gu = low(shrink_back(lower, packed, 512) * gelu_slope(upward[...]))
+    grad_up[...] = gu
+    grad_hid = expand_back(gu, packed, 0)
+    normed, inv = norm_parts(after_cross[...])
+    back, first_gain = norm_back(grad_hid, gains[1:2, :], normed, inv)
+    gain_grads[0:1, :] = first_gain
+    gain_grads[1:2, :] = self_gain
+    grad = grad + back
+    cross_grad[...] = grad
+    lower = low(grad)
+    cross_branch[...] = lower
+    value_part[...] = low(mm(mixed[...], lower))
+    grad_mixed = mt(folded_out[...], lower)
+    padded = grad_mixed.shape[0]
+    index = rows_of(padded, BLOCK)
+    grad_mixed = jnp.where(index < channels, grad_mixed, 0.0)
+    rounded = full(low(grad_mixed))
+    delta = jnp.sum(rounded * full(mixed[...]), axis=0, keepdims=True)
+    for k, part in enumerate(three(lse[...]) + three(delta)):
+        grad_mixed = jnp.where(index == channels + k, part, grad_mixed)
+    sent[...] = low(grad_mixed)
+
+
+def cross_back_kernel(
+    scalars, near, far, queries, limits, plain, turned, rows, gain,
+    grad_rows, grad_gain, sent, grads, total, *, channels
+):
+    for step in range(4):
+        for core, source in ((0, near), (1, far)):
+            grads[block_of(scalars, step, core)] = source[step]
+    base = scalars[3]
+    count, padded = plain.shape
+    total[...] = jnp.zeros_like(total)
+
+    def pair(i, carry):
+        query = jnp.concatenate([queries[2 * i], queries[2 * i + 1]], axis=1)
+        grad_mixed = jnp.concatenate([grads[2 * i], grads[2 * i + 1]], axis=1)
+        extra = full(grad_mixed[channels : channels + 6, :])
+        lse = extra[0:1] + extra[1:2] + extra[2:3]
+        delta = extra[3:4] + extra[4:5] + extra[5:6]
+        limit = jnp.concatenate([limits[2 * i], limits[2 * i + 1]], axis=1)
+        mask = rows_of(count, 2 * BLOCK) + base < limit
+        scores = mm(plain[...], query)
+        share = jnp.where(mask, jnp.exp(scores - lse), 0.0)
+        grad_share = mm(plain[...], grad_mixed)
+        grad_scores = low(share * (grad_share - delta))
+        out = low(mm(turned[...], grad_scores) * (1.0 / math.sqrt(D)))
+        sent[2 * i] = out[:, :BLOCK]
+        sent[2 * i + 1] = out[:, BLOCK:]
+        total[...] += mt(grad_scores, query) + mt(low(share), grad_mixed)
+        return carry
+
+    lax.fori_loop(0, 4, pair, 0)
+    value = full(rows[...])
+    lanes = lax.broadcasted_iota(jnp.int32, value.shape, 1)
+    inside = lanes < channels
+    center = jnp.sum(value, axis=-1, keepdims=True) / channels
+    shifted = jnp.where(inside, value - center, 0.0)
+    inv = lax.rsqrt(jnp.sum(shifted * shifted, axis=-1, keepdims=True) / channels + EPS)
+    normed = shifted * inv
+    grad = jnp.where(inside, total[...], 0.0)
+    grad_gain[...] = jnp.sum(grad * normed, axis=0, keepdims=True)
+    scaled = grad * gain[...]
+    first = jnp.sum(scaled, axis=-1, keepdims=True) / channels
+    second = jnp.sum(scaled * normed, axis=-1, keepdims=True) / channels
+    result = inv * (scaled - first - normed * second)
+    grad_rows[...] = low(result[:, :channels])
+
+
+def last_kernel(
+    parts, folded_query, normed_in, latents, gains, cross_grad, value_part, gain_rows,
+    grad_latents, sent, *, channels
+):
+    acc = full(parts[0])
+    for d in range(1, 8):
+        acc = acc + full(parts[d])
+    padded = acc.shape[0]
+    index = rows_of(padded, BLOCK)
+    acc = jnp.where(index < channels, acc, 0.0)
+    grad_query = low(acc)
+    grad_in = mm(low(acc.T), folded_query[...])
+    normed, inv = norm_parts(full(latents[...]))
+    back, cross_gain = norm_back(grad_in, gains[0:1, :], normed, inv)
+    grad_latents[...] = cross_grad[...] + back
+    part = mm(grad_query, normed_in[...])
+    wide = rows_of(padded, part.shape[1])
+    rows = [cross_gain] + [gain_rows[k : k + 1, :] for k in range(4)]
+    for k, row in enumerate(rows):
+        high = low(row)
+        part = jnp.where(wide == channels + 2 * k, full(high), part)
+        part = jnp.where(wide == channels + 2 * k + 1, row - full(high), part)
+    part = low(part)
+    for b in range(8):
+        sent[b, 0] = part[:, b * BLOCK : (b + 1) * BLOCK]
+        sent[b, 1] = value_part[:, b * BLOCK : (b + 1) * BLOCK]
+
+
+def finish_kernel(
+    scalars, near, far, key, value, packed,
+    grad_query, grad_key, grad_out, grad_value, gain_grads, key_sum, value_sum, *, channels
+):
+    for step in range(4):
+        for core, source in ((0, near), (1, far)):
+            at = pl.multiple_of(block_of(scalars, step, core) * BLOCK, BLOCK)
+            key_sum[:, pl.ds(at, BLOCK)] = source[step, 0]
+            value_sum[:, pl.ds(at, BLOCK)] = source[step, 1]
+    extra = full(key_sum[channels : channels + 10, :])
+    for k in range(5):
+        gain_grads[k : k + 1, :] = extra[2 * k : 2 * k + 1] + extra[2 * k + 1 : 2 * k + 2]
+    at = pl.multiple_of(scalars[2] * WIDE, WIDE)
+    half = pl.multiple_of(scalars[1] * 512, 512)
+    turned = full(key_sum[:, pl.ds(half, 512)]).T
+    grad_query[...] = mm(low(turned[:, :channels]), key[:, pl.ds(at, WIDE)])
+    turned = full(value[:, pl.ds(at, WIDE)]).T
+    grad_out[...] = mm(low(turned), value_sum[0:channels, pl.ds(half, 512)])
+    grad_key[...] = expand_tiles(key_sum[...], packed, 0)[:channels]
+    grad_value[...] = shrink_back(value_sum[...], packed, 512)[:channels]
+
+
+def wide_rows(value, row):
+    half = value.shape[1] // 2
+    keep = lax.dynamic_slice_in_dim(value, row * half, half, 1)
+    give = lax.dynamic_slice_in_dim(value, (1 - row) * half, half, 1)
+    return keep, give
+
+
+def for_rows(value, row):
+    keep, give = wide_rows(value, row)
+    pair = jnp.stack([keep, swap_row(give)])
+    both = jnp.stack([pair, swap_chip(pair)])
+    return jnp.stack([both, swap_core(both)])
+
+
+def for_cols(value, chip, core):
+    keep, give = wide_rows(value, chip)
+    pair = jnp.stack([keep, swap_chip(give)])
+    half = pair.shape[2] // 2
+    mine = lax.dynamic_slice_in_dim(pair, core * half, half, 2)
+    theirs = lax.dynamic_slice_in_dim(pair, (1 - core) * half, half, 2)
+    both = jnp.stack([mine, swap_core(theirs)])
+    every = jnp.stack([both, swap_row(both)])
+    return jnp.transpose(every, (1, 2, 0, 3, 4))
+
+
+def over_rows(first, second):
+    return lax.dot_general(
+        first.reshape(-1, first.shape[-1]),
+        second.reshape(-1, second.shape[-1]),
+        (((0,), (0,)), ((), ())),
+        preferred_element_type=jnp.float32,
+    )
+
+
+def in_order(row, own, other, axis):
+    return jnp.where(
+        row == 0,
+        jnp.concatenate([own, other], axis),
+        jnp.concatenate([other, own], axis),
+    )
+
+
+def tiles_of(weight):
+    return [weight[:, :WIDE], weight[:, WIDE:]]
+
+
+def all_of(parts):
+    packed = jnp.concatenate(parts, axis=0)
+    return lax.all_gather(packed, GROUP, axis=0, tiled=False)
+
+
+def fast_device(
+    latents, inputs, positions, piece_start, cotangent, cross_gain, input_gain, cross_query,
+    cross_key, cross_value, cross_out, first_gain, first_expand, first_shrink, self_gain,
+    self_query, self_key, self_value, self_out, second_gain, second_expand, second_shrink,
+):
+    bf, f32 = jnp.bfloat16, jnp.float32
+    row, col = lax.axis_index("row"), lax.axis_index("col")
+    chip, core = col // 2, col % 2
+    channels = inputs.shape[-1]
+    padded = -(-(channels + 11) // 16) * 16
+    keys_here = inputs.shape[1] // 2
+    base = col * inputs.shape[1] + row * keys_here
+    scalars = jnp.stack([2 * col + row, row, col, base]).astype(jnp.int32)
+    rows = BLOCK
+
+    def swap_half(block):
+        keep = lax.dynamic_slice_in_dim(block, row * rows, rows, 0)
+        give = lax.dynamic_slice_in_dim(block, (1 - row) * rows, rows, 0)
+        return in_order(row, keep, swap_row(give), 1)
+
+    def swap_back(value):
+        keep, give = wide_rows(value, row)
+        return in_order(row, keep, swap_row(give), 0)
+
+    parts = kernel(
+        fold_kernel, [((4, 2, padded, BLOCK), bf)], scalars, cross_key, cross_value, cross_query,
+        cross_out,
+    )[0]
+    parts = lax.all_to_all(parts, "col", 0, 0, tiled=True)
+    folded = kernel(add_kernel, [((2, padded, BLOCK), bf)], parts, scalars=False)[0]
+    fold_near, fold_far = gather_eight(folded)
+
+    gains_here = jnp.stack([cross_gain, first_gain, self_gain, second_gain])
+    gains = in_order(row, gains_here, swap_row(gains_here), 1)
+    state = swap_half(latents[0])
+    normed_in = kernel(
+        first_kernel, [((rows, D), bf)], state, gains[0:1], scalars=False
+    )[0]
+    own_rows = jnp.pad(
+        lax.dynamic_slice_in_dim(inputs[0], row * keys_here, keys_here, 0),
+        ((0, 0), (0, padded - channels)),
+    )
+    wide_gain = jnp.pad(input_gain, (0, padded - channels))[None]
+    plain, turned = kernel(
+        functools.partial(input_kernel, channels=channels),
+        [((keys_here, padded), bf), ((padded, keys_here), bf)],
+        own_rows, wide_gain, scalars=False,
+    )
+    limits = view_limits(positions, piece_start)[0].reshape(8, 1, BLOCK)
+    places = positions[0][:, None]
+
+    packed_first = all_of([first_expand] + tiles_of(first_shrink))
+    packed_second = all_of(tiles_of(self_out) + [second_expand] + tiles_of(second_shrink))
+    packed_cross = all_of([cross_query] + tiles_of(cross_out))
+    joined_weights = [
+        w.reshape(w.shape[0], 2, HEAD) for w in (self_query, self_key, self_value)
+    ]
+    mine = jnp.concatenate(
+        [lax.dynamic_index_in_dim(w, row, 1, False) for w in joined_weights], axis=1
+    )
+    theirs = jnp.concatenate(
+        [lax.dynamic_index_in_dim(w, 1 - row, 1, False) for w in joined_weights], axis=1
+    )
+    head_weights = in_order(row, mine, swap_row(theirs), 0)
+
+    folded_query, folded_out, query = kernel(
+        query_kernel, [((padded, D), bf), ((padded, D), bf), ((padded, rows), bf)],
+        scalars, fold_near, fold_far, normed_in,
+    )
+    query_near, query_far = gather_eight(query)
+    queries, partial_mixed = kernel(
+        functools.partial(cross_kernel, channels=channels),
+        [((8, padded, BLOCK), bf), ((8, padded, BLOCK), bf)],
+        scalars, query_near, query_far, limits, plain, turned,
+    )
+    received = exchange(partial_mixed)
+    mixed, lse, after_cross, hidden, upward, active, after_first, self_in = kernel(
+        functools.partial(merge_kernel, channels=channels),
+        [
+            ((padded, rows), bf), ((1, rows), f32), ((rows, D), f32), ((rows, D), bf),
+            ((rows, D), f32), ((rows, D), bf), ((rows, D), f32), ((rows, D), bf),
+        ],
+        received, state, folded_out, packed_first, gains, scalars=False,
+    )
+    self_near, self_far = gather_eight(self_in)
+    total_rows = positions.shape[1]
+    self_rows, qkv, self_mixed, self_lse, sent = kernel(
+        attend_kernel,
+        [
+            ((total_rows, D), bf), ((total_rows, 3 * HEAD), bf), ((HEAD, total_rows), f32),
+            ((1, total_rows), f32), ((8, HEAD, BLOCK), bf),
+        ],
+        scalars, self_near, self_far, head_weights, limits, places,
+    )
+    received = exchange(sent)
+    grad_final = swap_half(cotangent[0])
+    (
+        out, joined, second_hidden, second_active, second_up, second_gain_part, self_branch,
+        state_grad, sent,
+    ) = kernel(
+        second_kernel,
+        [
+            ((rows, D), bf), ((rows, D), bf), ((rows, D), bf), ((rows, D), bf), ((rows, D), bf),
+            ((1, D), f32), ((rows, D), bf), ((rows, D), f32), ((8, BLOCK, rows), bf),
+        ],
+        received, after_first, grad_final, gains[3:4], packed_second, scalars=False,
+    )
+    received = exchange(sent)
+    grad_qkv, sent = kernel(
+        attend_back_kernel,
+        [((total_rows, 3 * HEAD), bf), ((2, 4, rows, D), bf)],
+        scalars, received, qkv, self_mixed, self_lse, head_weights, limits, places,
+    )
+    summed = low(full(sent[0]) + full(swap_core(sent[1])))
+    by_row, by_chip, by_both = swap_row(summed[1]), swap_chip(summed[2]), swap_both(summed[3])
+    (
+        gain_rows, first_branch, first_up, cross_branch, cross_grad, value_part, sent,
+    ) = kernel(
+        functools.partial(first_back_kernel, channels=channels),
+        [
+            ((2, D), f32), ((rows, D), bf), ((rows, D), bf), ((rows, D), bf), ((rows, D), f32),
+            ((padded, D), bf), ((padded, rows), bf),
+        ],
+        summed[0], by_row, by_chip, by_both, state_grad, after_first, after_cross, upward,
+        packed_first, gains, folded_out, mixed, lse, scalars=False,
+    )
+    grad_near, grad_far = gather_eight(sent)
+    grad_rows, input_gain_part, sent = kernel(
+        functools.partial(cross_back_kernel, channels=channels),
+        [((keys_here, channels), bf), ((1, padded), f32), ((8, padded, BLOCK), bf)],
+        scalars, grad_near, grad_far, queries, limits, plain, turned, own_rows, wide_gain,
+        scratch=[pltpu.VMEM((8, padded, BLOCK), bf), pltpu.VMEM((keys_here, padded), f32)],
+    )
+    received = exchange(sent)
+    wide_part = jnp.pad(input_gain_part, ((0, 0), (0, D - padded)))
+    extra = jnp.concatenate([gain_rows, second_gain_part, wide_part], axis=0)
+    latents_grad, sent = kernel(
+        functools.partial(last_kernel, channels=channels),
+        [((rows, D), f32), ((8, 2, padded, BLOCK), bf)],
+        received, folded_query, normed_in, state, gains, cross_grad, value_part, extra,
+        scalars=False,
+    )
+    received = exchange(sent)
+    total = kernel(add_kernel, [((2, padded, BLOCK), bf)], received, scalars=False)[0]
+    total = low(full(total) + full(lax.ppermute(total, "dp", SEQ_NEAR)))
+    total = low(full(total) + full(lax.ppermute(total, "dp", SEQ_FAR)))
+    sum_near, sum_far = gather_eight(total)
+    grad_cross_query, grad_cross_key, grad_cross_out, grad_cross_value, gain_grads = kernel(
+        functools.partial(finish_kernel, channels=channels),
+        [
+            (cross_query.shape, f32), (cross_key.shape, f32), (cross_out.shape, f32),
+            (cross_value.shape, f32), ((5, D), f32),
+        ],
+        scalars, sum_near, sum_far, cross_key, cross_value, packed_cross,
+        scratch=[pltpu.VMEM((padded, D), bf), pltpu.VMEM((padded, D), bf)],
+    )
+    half = D // 2
+    gains_mine = lax.dynamic_slice_in_dim(gain_grads, row * half, half, 1)
+
+    grad_second_expand = over_rows(
+        for_rows(second_hidden, row), for_cols(second_up, chip, core)
+    )
+    grad_second_shrink = over_rows(
+        for_cols(second_active, chip, core), for_rows(grad_final, row)
+    )
+    grad_self_out = over_rows(for_cols(joined, chip, core), for_rows(self_branch, row))
+    grad_first_expand = over_rows(for_rows(hidden, row), for_cols(first_up, chip, core))
+    grad_first_shrink = over_rows(for_cols(active, chip, core), for_rows(first_branch, row))
+    grad_heads = low(over_rows(self_rows, grad_qkv))
+    keep = lax.dynamic_slice_in_dim(grad_heads, row * half, half, 0)
+    give = lax.dynamic_slice_in_dim(grad_heads, (1 - row) * half, half, 0)
+    pair = swap_row(give)
+    summed = lax.psum(
+        (
+            low(grad_second_expand), low(grad_second_shrink), low(grad_self_out),
+            keep, pair, low(grad_first_expand), low(grad_first_shrink),
+        ),
+        "dp",
+    )
+    keep, pair = full(summed[3]), full(summed[4])
+    grad_qkv_weights = [
+        in_order(row, keep[:, k * HEAD : (k + 1) * HEAD], pair[:, k * HEAD : (k + 1) * HEAD], 1)
+        for k in range(3)
+    ]
+    other_rows = swap_row(grad_rows)
+    return (
+        swap_back(out)[None],
+        swap_back(latents_grad)[None],
+        in_order(row, grad_rows, other_rows, 0)[None],
+        gains_mine[0],
+        gain_grads[4, :channels],
+        grad_cross_query,
+        grad_cross_key,
+        grad_cross_value,
+        grad_cross_out,
+        gains_mine[1],
+        full(summed[5]),
+        full(summed[6]),
+        gains_mine[2],
+        grad_qkv_weights[0],
+        grad_qkv_weights[1],
+        grad_qkv_weights[2],
+        full(summed[2]),
+        gains_mine[3],
+        full(summed[0]),
+        full(summed[1]),
+    )
+
+
 def solution(mesh):
     placed = (
         P("dp", "col", "row"),
@@ -466,8 +1232,10 @@
         P("row", "col"),
         P("col", "row"),
     )
+    sizes = dict(mesh.shape)
+    quick = sizes == {"row": 2, "col": 4, "dp": 4}
     return jax.shard_map(
-        on_device,
+        fast_device if quick else on_device,
         mesh=mesh,
         in_specs=placed,
         out_specs=(

time: 1160 us -> 441 us (0.38)
  waiting for transfers between devices: 773 us -> 162 us
  blocking collectives: 154 us -> 20.3 us
  matrix products: 121 us -> 10.9 us
  Pallas kernels: 0 us -> 77.7 us
  starting transfers between devices: 2.05 us -> 75.1 us
  other arithmetic: 53.9 us -> 38.2 us
    reduce_scatter x18 -> x0, waiting for transfers between devices: 340 us -> none  [the longest x8 182 us: col_reduce(): lax.psum_scatter(value.astype(jnp.bfloat16), 'col', scatter_dimension=1,...]
    all_gather x12 -> x3, waiting for transfers between devices: 205 us -> 0.01 us  [all_of(): return lax.all_gather(packed, GROUP, axis=0, tiled=False)]
    psum x4 -> x1, waiting for transfers between devices: 227 us -> 30.4 us  [fast_device(): lax.psum((low(grad_second_expand), low(grad_second_shrink), low(grad_self...]
    ppermute x0 -> x64, waiting for transfers between devices: none -> 113 us  [the longest x24 47.3 us: swap_row(): return lax.ppermute(value, 'row', ROW_SWAP)]
    dot_general x46 -> x6, matrix products: 121 us -> 10.9 us  [over_rows(): lax.dot_general(first.reshape(-1, first.shape[-1]), second.reshape(-1, se...]
    psum x9 -> x0, blocking collectives: 83.7 us -> none  [the longest x1 43.3 us: on_device(): lax.psum((grad_key_sum, grad_value_sum, padded, input_gain_part), ('row',...]
    pallas_call x0 -> x15, Pallas kernels: none -> 77.7 us  [kernel(): pl.pallas_call(body, out_shape=tuple((jax.ShapeDtypeStruct(shape, kind) f...]
    all_gather x9 -> x0, blocking collectives: 70.2 us -> none  [the longest x7 59.6 us: row_rows(): return lax.all_gather(value, 'row', axis=1, tiled=True)]
  transfers between devices with their start and end apart: 34 -> 73, of which waited for: 34 -> 34; matrix products, arithmetic and copies ran while one was open for 7% -> 15% of each run, Pallas kernels for 0% -> 18%
where the time goes in v1:
time: 441 us; the launch traced here: 435 us
  waiting for transfers between devices  162 us (37%)
  Pallas kernels  77.7 us (18%)
  starting transfers between devices  75.1 us (17%)
  other arithmetic  38.2 us (9%)
  local copies, waits for them, and re-layouts  35.7 us (8%)
  blocking collectives  20.3 us (5%)
  between operations  14.9 us (3%)
  matrix products  10.9 us (2%)
    pallas_call x15, Pallas kernels, kernel(): pl.pallas_call(body, out_shape=tuple((jax.ShapeDtypeStruct(shape, kind) f...  77.7 us
    ppermute x24, waiting for transfers between devices, swap_row(): return lax.ppermute(value, 'row', ROW_SWAP)  47.3 us
    ppermute x16, waiting for transfers between devices, swap_chip(): return lax.ppermute(value, 'col', col_step(2))  33.4 us
    psum x1, waiting for transfers between devices, fast_device(): lax.psum((low(grad_second_expand), low(grad_second_shrink), low(grad_self...  30.4 us
    ppermute x24, starting transfers between devices, swap_row(): return lax.ppermute(value, 'row', ROW_SWAP)  23.9 us
    all_to_all x1, blocking collectives, exchange(): return lax.all_to_all(value, GROUP, 0, 0, tiled=True)  20.3 us
    ppermute x16, starting transfers between devices, swap_chip(): return lax.ppermute(value, 'col', col_step(2))  15.3 us
    all_to_all x4, starting transfers between devices, exchange(): return lax.all_to_all(value, GROUP, 0, 0, tiled=True)  14.3 us
  transfers between devices with their start and end apart: 73, of which 34 were waited for; matrix products, arithmetic and copies ran while one was open for 15% of the time, Pallas kernels for 18%

profile of v1, /device:TPU:0, one launch (start us, length us, event | category | flops | bytes accessed | tf_op | source)
XLA Modules:
  0.0 434.9 jit_solution(649856810246014418)
XLA Ops:
  11.9 2.6 shard_map.368
  14.5 4.4 %all-to-all-start = ((bf16[4,2,272,128]{3,2,1,0:T(8,128)(2,1)}), bf16[4,2,272,128]{3,2,1,0:T(8,128)(2,1)S(1)}, u32[]{:S(2)}, u32[]{:S(2)}) async-start(bf16[4,2,272,128]{3,2,1,0:T(8,128)(2,1)} %shard_map.368), calls=%async_computation | async-start | bytes 1114112 | tf_op jit(solution)/shard_map/all_to_all | solution.py:1029
  18.9 2.3 collective-permute-start.4
  21.4 11.7 %all-to-all-done.parts = bf16[4,2,272,128]{3,2,1,0:T(8,128)(2,1)S(1)} async-done(((bf16[4,2,272,128]{3,2,1,0:T(8,128)(2,1)}), bf16[4,2,272,128]{3,2,1,0:T(8,128)(2,1)S(1)}, u32[]{:S(2)}, u32[]{:S(2)}) %all-to-all-start) | async-done | bytes 557088 | tf_op jit(solution)/shard_map/all_to_all | solution.py:1029
  35.6 2.7 collective-permute-start
  40.7 3.6 collective-permute-done
  44.3 4.4 %collective-permute-done.1 = bf16[2,272,128]{2,1,0:T(8,128)(2,1)S(1)} collective-permute-done((bf16[2,272,128]{2,1,0:T(8,128)(2,1)}, bf16[2,272,128]{2,1,0:T(8,128)(2,1)S(1)}, u32[]{:S(2)}, u32[]{:S(2)}) %collective-permute-start.1) | collective-permute-done | bytes 139296 | tf_op jit(solution)/shard_map/ppermute | solution.py:468
  53.2 2.7 shard_map.371
  56.7 3.0 collective-permute-start.7
  60.6 2.8 collective-permute-done.7
  68.7 3.0 shard_map.372
  72.4 6.6 %shard_map.373 = (bf16[8,272,128]{2,1,0:T(8,128)(2,1)}, bf16[8,272,128]{2,1,0:T(8,128)(2,1)}) custom-call(s32[4]{0:T(128)} %pad_add_fusion.scalars, bf16[4,272,128]{2,1,0:T(8,128)(2,1)} %copy-done.11, bf16[4,272,128]{2,1,0:T(8,128)(2,1)} %copy-done.28, s32[8,1,128]{2,1,0:T(1,128)} %maximum_bitcast_fusion.5.limits, ...), custom_call_target="tpu_custom_call" | custom-call | tf_op jit(solution)/shard_map/pallas_call | solution.py:492
  79.0 20.3 %all_to_all.30.parts = bf16[8,272,128]{2,1,0:T(8,128)(2,1)} all-to-all(bf16[8,272,128]{2,1,0:T(8,128)(2,1)} %get-tuple-element.70), channel_id=1, replica_groups=mesh['row'=2,'col'=4,'dp'=4] {'col','row'}, dimensions={0} | all-to-all | bytes 1114112 | tf_op jit(solution)/shard_map/all_to_all | solution.py:485
  99.4 5.2 %shard_map.374 = (bf16[272,128]{1,0:T(8,128)(2,1)}, f32[1,128]{1,0:T(1,128)}, f32[128,1024]{1,0:T(8,128)}, bf16[128,1024]{1,0:T(8,128)(2,1)}, f32[128,1024]{1,0:...) custom-call(bf16[8,272,128]{2,1,0:T(8,128)(2,1)} %all_to_all.30.parts, ...), custom_call_target="tpu_custom_call" | custom-call | tf_op jit(solution)/shard_map/pallas_call | solution.py:492
  111.5 3.9 collective-permute-done.10
  115.4 6.4 %collective-permute-done.12 = bf16[128,1024]{1,0:T(8,128)(2,1)S(1)} collective-permute-done((bf16[128,1024]{1,0:T(8,128)(2,1)}, bf16[128,1024]{1,0:T(8,128)(2,1)S(1)}, u32[]{:S(2)}, u32[]{:S(2)}) %collective-permute-start.12) | collective-permute-done | bytes 262176 | tf_op jit(solution)/shard_map/ppermute | solution.py:476
  132.8 2.4 collective-permute-done.61
  142.0 3.8 collective-permute-done.14
  148.1 3.2 collective-permute-done.33
  154.4 7.8 %shard_map.375 = (bf16[1024,1024]{1,0:T(8,128)(2,1)}, bf16[1024,384]{1,0:T(8,128)(2,1)}, f32[128,1024]{1,0:T(8,128)}, f32[1,1024]{1,0:T(1,128)}, bf16[8,128,128]{2,1,0:T(8,128)(2,1)}) custom-call(s32[4]{0:T(128)} %pad_add_fusion.scalars, bf16[4,128,1024]{2,1,0:T(8,128)(2,1)} %copy-done.3, bf16[4,128,1024]{2,1,0:T(8,128)(2,1)} %copy-done.14, ...), custom_call_target="tpu_custom_call" | custom-call | tf_op jit(solution)/shard_map/pallas_call | solution.py:492
  162.2 3.4 all-to-all-start.2
  168.7 3.2 all-to-all-done.2.parts
  172.6 7.5 %shard_map.376 = (bf16[128,1024]{1,0:T(8,128)(2,1)}, bf16[128,1024]{1,0:T(8,128)(2,1)}, bf16[128,1024]{1,0:T(8,128)(2,1)}, bf16[128,1024]{1,0:T(8,128)(2,1)}, bf...) custom-call(bf16[8,128,128]{2,1,0:T(8,128)(2,1)} %copy-done.16, ...), custom_call_target="tpu_custom_call" | custom-call | tf_op jit(solution)/shard_map/pallas_call | solution.py:492
  180.1 3.6 all-to-all-start.3
  186.4 3.5 all-to-all-done.3.parts
  190.6 10.1 %shard_map.377 = (bf16[1024,384]{1,0:T(8,128)(2,1)}, bf16[2,4,128,1024]{3,2,1,0:T(8,128)(2,1)}) custom-call(s32[4]{0:T(128)} %pad_add_fusion.scalars, bf16[8,128,128]{2,1,0:T(8,128)(2,1)} %copy-done.17, bf16[1024,384]{1,0:T(8,128)(2,1)} %get-tuple-element.77.qkv, f32[128,1024]{1,0:T(8,128)} %get-tuple-element.78.mixed, f32[1,1024]{1,0:T(1,128)} %get-tuple-element.79.lse, ...), custom_call_target="tpu_custom_call" | custom-call | tf_op jit(solution)/shard_map/pallas_call | solution.py:492
  206.3 2.4 collective-permute-done.58
  222.4 2.7 collective-permute-done.18.by_row
  225.0 6.0 %collective-permute-done.19.by_chip = bf16[128,1024]{1,0:T(8,128)(2,1)S(1)} collective-permute-done((bf16[128,1024]{1,0:T(8,128)(2,1)S(1)}, bf16[128,1024]{1,0:T(8,128)(2,1)S(1)}, u32[]{:S(2)}, u32[]{:S(2)}) %collective-permute-start.19) | collective-permute-done | bytes 262176 | tf_op jit(solution)/shard_map/ppermute | solution.py:468
  231.9 6.5 %shard_map.378 = (f32[2,1024]{1,0:T(2,128)}, bf16[128,1024]{1,0:T(8,128)(2,1)}, bf16[128,1024]{1,0:T(8,128)(2,1)}, bf16[128,1024]{1,0:T(8,128)(2,1)}, f32[128,10...) custom-call(bf16[128,1024]{1,0:T(8,128)(2,1)} %get-tuple-element.204.own, ...), custom_call_target="tpu_custom_call" | custom-call | tf_op jit(solution)/shard_map/pallas_call | solution.py:492
  248.7 3.9 collective-permute-done.53
  255.7 10.3 %shard_map.379 = (bf16[1024,261]{1,0:T(8,128)(2,1)}, f32[1,272]{1,0:T(1,128)}, bf16[8,272,128]{2,1,0:T(8,128)(2,1)}) custom-call(s32[4]{0:T(128)} %pad_add_fusion.scalars, bf16[4,272,128]{2,1,0:T(8,128)(2,1)} %copy-done.12, bf16[4,272,128]{2,1,0:T(8,128)(2,1)} %copy-done.29, bf16[8,272,128]{2,1,0:T(8,128)(2,1)} %get-tuple-element.87.queries, ...), custom_call_target="tpu_custom_call" | custom-call | tf_op jit(solution)/shard_map/pallas_call | solution.py:492
  266.0 3.7 all-to-all-start.4
  273.7 8.5 %collective-permute-done.36 = bf16[128,512]{1,0:T(8,128)(2,1)S(1)} collective-permute-done((bf16[128,512]{1,0:T(8,128)(2,1)S(1)}, bf16[128,512]{1,0:T(8,128)(2,1)S(1)}, u32[]{:S(2)}, u32[]{:S(2)}) %collective-permute-start.36) | collective-permute-done | bytes 131104 | tf_op jit(solution)/shard_map/ppermute | solution.py:468
  285.5 3.6 shard_map.380
  289.1 3.6 all-to-all-start.5
  296.3 2.4 fusion.5
  300.8 2.4 fusion.4
  303.2 2.4 fusion.3
  305.6 8.3 %collective-permute-done.38 = bf16[2,2,128,256]{3,2,1,0:T(8,128)(2,1)S(1)} collective-permute-done((bf16[2,2,128,256]{3,2,1,0:T(8,128)(2,1)S(1)}, bf16[2,2,128,256]{3,2,1,0:T(8,128)(2,1)S(1)}, u32[]{:S(2)}, u32[]{:S(2)}) %collective-permute-start.38) | collective-permute-done | bytes 262176 | tf_op jit(solution)/shard_map/ppermute | solution.py:464
  315.1 4.4 %collective-permute-done.41 = bf16[2,2,128,256]{3,2,1,0:T(8,128)(2,1)S(1)} collective-permute-done((bf16[2,2,128,256]{3,2,1,0:T(8,128)(2,1)S(1)}, bf16[2,2,128,256]{3,2,1,0:T(8,128)(2,1)S(1)}, u32[]{:S(2)}, u32[]{:S(2)}) %collective-permute-start.41) | collective-permute-done | bytes 262176 | tf_op jit(solution)/shard_map/ppermute | solution.py:464
  320.7 6.7 %collective-permute-done.45 = bf16[512,384]{1,0:T(8,128)(2,1)S(1)} collective-permute-done((bf16[512,384]{1,0:T(8,128)(2,1)S(1)}, bf16[512,384]{1,0:T(8,128)(2,1)S(1)}, u32[]{:S(2)}, u32[]{:S(2)}) %collective-permute-start.45) | collective-permute-done | bytes 393248 | tf_op jit(solution)/shard_map/ppermute | solution.py:464
  332.7 8.6 %collective-permute-done.27 = bf16[2,272,128]{2,1,0:T(8,128)(2,1)S(1)} collective-permute-done((bf16[2,272,128]{2,1,0:T(8,128)(2,1)}, bf16[2,272,128]{2,1,0:T(8,128)(2,1)S(1)}, u32[]{:S(2)}, u32[]{:S(2)}) %collective-permute-start.27) | collective-permute-done | bytes 139296 | tf_op jit(solution)/shard_map/ppermute | solution.py:1145
  342.3 4.5 %collective-permute-start.28 = (bf16[2,272,128]{2,1,0:T(8,128)(2,1)S(1)}, bf16[2,272,128]{2,1,0:T(8,128)(2,1)S(1)}, u32[]{:S(2)}, u32[]{:S(2)}) collective-permute-start(bf16[2,272,128]{2,1,0:T(8,128)(2,1)S(1)} %add_convert_fusion.1), channel_id=1, source_target_pairs={{0,2},{2,0},{1,3},{3,1},{4,6},{6,4},{5,7},{7,5},{8,10},{10,8},{9,1... | collective-permute-start | bytes 417800 | tf_op jit(solution)/shard_map/ppermute | solution.py:1146
  347.1 13.3 %collective-permute-done.28 = bf16[2,272,128]{2,1,0:T(8,128)(2,1)S(1)} collective-permute-done((bf16[2,272,128]{2,1,0:T(8,128)(2,1)S(1)}, bf16[2,272,128]{2,1,0:T(8,128)(2,1)S(1)}, u32[]{:S(2)}, u32[]{:S(2)}) %collective-permute-start.28) | collective-permute-done | bytes 139296 | tf_op jit(solution)/shard_map/ppermute | solution.py:1146
  374.4 5.0 %collective-permute-done.25 = f32[128,512]{1,0:T(8,128)} collective-permute-done((f32[128,512]{1,0:T(8,128)}, f32[128,512]{1,0:T(8,128)}, u32[]{:S(2)}, u32[]{:S(2)}) %collective-permute-start.25) | collective-permute-done | bytes 262176 | tf_op jit(solution)/shard_map/ppermute | solution.py:464
  381.3 6.2 %shard_map.382 = (f32[512,256]{1,0:T(8,128)}, f32[261,1024]{1,0:T(8,128)}, f32[256,512]{1,0:T(8,128)}, f32[261,1024]{1,0:T(8,128)}, f32[5,1024]{1,0:T(8,128)}) custom-call(s32[4]{0:T(128)} %pad_add_fusion.scalars, bf16[4,2,272,128]{3,2,1,0:T(8,128)(2,1)} %pad_maximum_fusion.2.near, bf16[4,2,272,128]{3,2,1,0:T(8,128)(2,1)} %collective-permute-done.32.far, ...), custom_call_target="tpu_custom_call" | custom-call | tf_op jit(solution)/shard_map/pallas_call | solution.py:492
  390.3 30.4 %all-reduce.6.cloned.1.call-done = (bf16[512,384]{1,0:T(8,128)(2,1)}, bf16[512,384]{1,0:T(8,128)(2,1)}, bf16[512,256]{1,0:T(8,128)(2,1)}, bf16[256,512]{1,0:T(8,...) async-done(((bf16[512,384]{1,0:T(8,128)(2,1)}, bf16[512,384]{1,0:T(8,128)(2,1)}, bf16[512,256]{1,0:T(8,128)(2,1)}, ...) | async-done | bytes 2097168 | tf_op jit(solution)/shard_map/psum | solution.py:1173
  (367 shorter events, 140.3 us)
Async XLA Ops:
  7.2 92.1 %all-gather.7.cloned.1.call-start = ((), (), s32[]{:S(2)}) async-start(), calls=%async_computation.6 | async-start | bytes 4718592 | tf_op jit(solution)/shard_map/all_gather | solution.py:998
  10.2 161.7 %all-gather.9.cloned.1.call-start = ((), (), s32[]{:S(2)}) async-start(), calls=%async_computation.7 | async-start | bytes 7077888 | tf_op jit(solution)/shard_map/all_gather | solution.py:998
  14.5 18.6 %all-to-all-start = ((bf16[4,2,272,128]{3,2,1,0:T(8,128)(2,1)}), bf16[4,2,272,128]{3,2,1,0:T(8,128)(2,1)S(1)}, u32[]{:S(2)}, u32[]{:S(2)}) async-start(bf16[4,2,272,128]{3,2,1,0:T(8,128)(2,1)} %shard_map.368), calls=%async_computation | async-start | bytes 1114112 | tf_op jit(solution)/shard_map/all_to_all | solution.py:1029
  18.9 362.4 %all-gather.11.cloned.1.call-start = ((), (), s32[]{:S(2)}) async-start(), calls=%async_computation.8 | async-start | bytes 4718592 | tf_op jit(solution)/shard_map/all_gather | solution.py:998
  18.9 30.8 %collective-permute-start.4 = (bf16[128,512]{1,0:T(8,128)(2,1)S(1)}, bf16[128,512]{1,0:T(8,128)(2,1)S(1)}, u32[]{:S(2)}, u32[]{:S(2)}) collective-permute-start(bf16[128,512]{1,0:T(8,128)(2,1)S(1)} %get-tuple-element.290), channel_id=1, source_target_pairs={{0,16},{16,0},{1,17},{17,1},{2,18},{18,2},{3,19},{19,3},{4,20},{20... | collective-permute-start | bytes 393224 | tf_op jit(solution)/shard_map/ppermute | solution.py:464
  21.3 27.7 %collective-permute-start.5 = (f32[4,512]{1,0:T(4,128)S(1)}, f32[4,512]{1,0:T(4,128)S(1)}, u32[]{:S(2)}, u32[]{:S(2)}) collective-permute-start(f32[4,512]{1,0:T(4,128)S(1)} %pad_maximum_fusion.23), channel_id=1, source_target_pairs={{0,16},{16,0},{1,17},{17,1},{2,18},{18,2},{3,19},{19,3},{4,20},{20... | collective-permute-start | bytes 24584 | tf_op jit(solution)/shard_map/ppermute | solution.py:464
  38.3 10.5 %collective-permute-start.1 = (bf16[2,272,128]{2,1,0:T(8,128)(2,1)}, bf16[2,272,128]{2,1,0:T(8,128)(2,1)S(1)}, u32[]{:S(2)}, u32[]{:S(2)}) collective-permute-start(bf16[2,272,128]{2,1,0:T(8,128)(2,1)} %shard_map.369), channel_id=1, source_target_pairs={{0,8},{4,12},{8,0},{12,4},{1,9},{5,13},{9,1},{13,5},{2,10},{6,14},... | collective-permute-start | bytes 417800 | tf_op jit(solution)/shard_map/ppermute | solution.py:468
  38.3 10.5 %collective-permute-start.2 = (bf16[2,272,128]{2,1,0:T(8,128)(2,1)}, bf16[2,272,128]{2,1,0:T(8,128)(2,1)S(1)}, u32[]{:S(2)}, u32[]{:S(2)}) collective-permute-start(bf16[2,272,128]{2,1,0:T(8,128)(2,1)} %shard_map.369), channel_id=1, source_target_pairs={{0,24},{4,28},{8,16},{12,20},{16,8},{20,12},{24,0},{28,4},{1,25},{... | collective-permute-start | bytes 417800 | tf_op jit(solution)/shard_map/ppermute | solution.py:476
  104.5 10.8 %collective-permute-start.10 = (bf16[128,1024]{1,0:T(8,128)(2,1)}, bf16[128,1024]{1,0:T(8,128)(2,1)S(1)}, u32[]{:S(2)}, u32[]{:S(2)}) collective-permute-start(bf16[128,1024]{1,0:T(8,128)(2,1)} %get-tuple-element.72), channel_id=1, source_target_pairs={{0,16},{16,0},{1,17},{17,1},{2,18},{18,2},{3,19},{19,3},{4,20},{20... | collective-permute-start | bytes 786440 | tf_op jit(solution)/shard_map/ppermute | solution.py:464
  105.3 10.1 %collective-permute-start.11 = (bf16[128,1024]{1,0:T(8,128)(2,1)}, bf16[128,1024]{1,0:T(8,128)(2,1)S(1)}, u32[]{:S(2)}, u32[]{:S(2)}) collective-permute-start(bf16[128,1024]{1,0:T(8,128)(2,1)} %get-tuple-element.72), channel_id=1, source_target_pairs={{0,8},{4,12},{8,0},{12,4},{1,9},{5,13},{9,1},{13,5},{2,10},{6,14},... | collective-permute-start | bytes 786440 | tf_op jit(solution)/shard_map/ppermute | solution.py:468
  106.0 15.8 %collective-permute-start.12 = (bf16[128,1024]{1,0:T(8,128)(2,1)}, bf16[128,1024]{1,0:T(8,128)(2,1)S(1)}, u32[]{:S(2)}, u32[]{:S(2)}) collective-permute-start(bf16[128,1024]{1,0:T(8,128)(2,1)} %get-tuple-element.72), channel_id=1, source_target_pairs={{0,24},{4,28},{8,16},{12,20},{16,8},{20,12},{24,0},{28,4},{1,25},{... | collective-permute-start | bytes 786440 | tf_op jit(solution)/shard_map/ppermute | solution.py:476
  108.8 17.2 %collective-permute-start.15 = (bf16[128,512]{1,0:T(8,128)(2,1)}, bf16[128,512]{1,0:T(8,128)(2,1)}, u32[]{:S(2)}, u32[]{:S(2)}) collective-permute-start(bf16[128,512]{1,0:T(8,128)(2,1)} %get-tuple-element.280), channel_id=1, source_target_pairs={{0,16},{16,0},{1,17},{17,1},{2,18},{18,2},{3,19},{19,3},{4,20},{20... | collective-permute-start | bytes 393224 | tf_op jit(solution)/shard_map/ppermute | solution.py:464
  121.9 31.5 %collective-permute-start.13 = (bf16[4,128,1024]{2,1,0:T(8,128)(2,1)S(1)}, bf16[4,128,1024]{2,1,0:T(8,128)(2,1)S(1)}, u32[]{:S(2)}, u32[]{:S(2)}) collective-permute-start(bf16[4,128,1024]{2,1,0:T(8,128)(2,1)S(1)} %pad_maximum_fusion.near), channel_id=1, source_target_pairs={{0,4},{4,0},{8,12},{12,8},{1,5},{5,1},{9,13},{13,9},{2,6},{6,2},{1... | collective-permute-start | bytes 3145736 | tf_op jit(solution)/shard_map/ppermute | solution.py:472
  130.4 15.5 %collective-permute-start.14 = (bf16[512,384]{1,0:T(8,128)(2,1)}, bf16[512,384]{1,0:T(8,128)(2,1)}, u32[]{:S(2)}, u32[]{:S(2)}) collective-permute-start(bf16[512,384]{1,0:T(8,128)(2,1)} %pad_maximum_fusion.10), channel_id=1, source_target_pairs={{0,16},{16,0},{1,17},{17,1},{2,18},{18,2},{3,19},{19,3},{4,20},{20... | collective-permute-start | bytes 1179656 | tf_op jit(solution)/shard_map/ppermute | solution.py:464
  136.9 30.1 %collective-permute-start.62 = (bf16[2,128,512]{2,1,0:T(8,128)(2,1)}, bf16[2,128,512]{2,1,0:T(8,128)(2,1)S(1)}, u32[]{:S(2)}, u32[]{:S(2)}) collective-permute-start(bf16[2,128,512]{2,1,0:T(8,128)(2,1)} %get-tuple-element.232), channel_id=1, source_target_pairs={{0,8},{4,12},{8,0},{12,4},{1,9},{5,13},{9,1},{13,5},{2,10},{6,14},... | collective-permute-start | bytes 786440 | tf_op jit(solution)/shard_map/ppermute | solution.py:468
  140.1 25.5 %collective-permute-start.39 = (bf16[128,512]{1,0:T(8,128)(2,1)}, bf16[128,512]{1,0:T(8,128)(2,1)}, u32[]{:S(2)}, u32[]{:S(2)}) collective-permute-start(bf16[128,512]{1,0:T(8,128)(2,1)} %get-tuple-element.259), channel_id=1, source_target_pairs={{0,8},{4,12},{8,0},{12,4},{1,9},{5,13},{9,1},{13,5},{2,10},{6,14},... | collective-permute-start | bytes 393224 | tf_op jit(solution)/shard_map/ppermute | solution.py:468
  152.0 32.5 %collective-permute-start.34 = (bf16[2,128,512]{2,1,0:T(8,128)(2,1)}, bf16[2,128,512]{2,1,0:T(8,128)(2,1)}, u32[]{:S(2)}, u32[]{:S(2)}) collective-permute-start(bf16[2,128,512]{2,1,0:T(8,128)(2,1)} %get-tuple-element.272), channel_id=1, source_target_pairs={{0,8},{4,12},{8,0},{12,4},{1,9},{5,13},{9,1},{13,5},{2,10},{6,14},... | collective-permute-start | bytes 786440 | tf_op jit(solution)/shard_map/ppermute | solution.py:468
  166.5 17.1 %collective-permute-start.40 = (bf16[2,128,256]{2,1,0:T(8,128)(2,1)S(1)}, bf16[2,128,256]{2,1,0:T(8,128)(2,1)S(1)}, u32[]{:S(2)}, u32[]{:S(2)}) collective-permute-start(bf16[2,128,256]{2,1,0:T(8,128)(2,1)S(1)} %get-tuple-element.258), channel_id=1, source_target_pairs={{0,4},{4,0},{8,12},{12,8},{1,5},{5,1},{9,13},{13,9},{2,6},{6,2},{1... | collective-permute-start | bytes 393224 | tf_op jit(solution)/shard_map/ppermute | solution.py:472
  180.1 9.8 %all-to-all-start.3 = ((bf16[8,128,128]{2,1,0:T(8,128)(2,1)}), bf16[8,128,128]{2,1,0:T(8,128)(2,1)S(1)}, u32[]{:S(2)}, u32[]{:S(2)}) async-start(bf16[8,128,128]{2,1,0:T(8,128)(2,1)} %get-tuple-element.76), calls=%async_computation.3 | async-start | bytes 524288 | tf_op jit(solution)/shard_map/all_to_all | solution.py:485
  202.1 12.5 %collective-permute-start.17 = (bf16[4,128,1024]{2,1,0:T(8,128)(2,1)S(1)}, bf16[4,128,1024]{2,1,0:T(8,128)(2,1)S(1)}, u32[]{:S(2)}, u32[]{:S(2)}) collective-permute-start(bf16[4,128,1024]{2,1,0:T(8,128)(2,1)S(1)} %slice_bitcast_fusion), channel_id=1, source_target_pairs={{0,4},{4,0},{8,12},{12,8},{1,5},{5,1},{9,13},{13,9},{2,6},{6,2},{1... | collective-permute-start | bytes 3145736 | tf_op jit(solution)/shard_map/ppermute | solution.py:472
  211.6 10.1 %collective-permute-start.59 = (bf16[2,128,256]{2,1,0:T(8,128)(2,1)S(1)}, bf16[2,128,256]{2,1,0:T(8,128)(2,1)S(1)}, u32[]{:S(2)}, u32[]{:S(2)}) collective-permute-start(bf16[2,128,256]{2,1,0:T(8,128)(2,1)S(1)} %get-tuple-element.228), channel_id=1, source_target_pairs={{0,4},{4,0},{8,12},{12,8},{1,5},{5,1},{9,13},{13,9},{2,6},{6,2},{1... | collective-permute-start | bytes 393224 | tf_op jit(solution)/shard_map/ppermute | solution.py:472
  213.8 26.2 %collective-permute-start.56 = (bf16[2,128,256]{2,1,0:T(8,128)(2,1)S(1)}, bf16[2,128,256]{2,1,0:T(8,128)(2,1)S(1)}, u32[]{:S(2)}, u32[]{:S(2)}) collective-permute-start(bf16[2,128,256]{2,1,0:T(8,128)(2,1)S(1)} %get-tuple-element.238), channel_id=1, source_target_pairs={{0,4},{4,0},{8,12},{12,8},{1,5},{5,1},{9,13},{13,9},{2,6},{6,2},{1... | collective-permute-start | bytes 393224 | tf_op jit(solution)/shard_map/ppermute | solution.py:472
  217.0 14.1 %collective-permute-start.19 = (bf16[128,1024]{1,0:T(8,128)(2,1)S(1)}, bf16[128,1024]{1,0:T(8,128)(2,1)S(1)}, u32[]{:S(2)}, u32[]{:S(2)}) collective-permute-start(bf16[128,1024]{1,0:T(8,128)(2,1)S(1)} %get-tuple-element.202), channel_id=1, source_target_pairs={{0,8},{4,12},{8,0},{12,4},{1,9},{5,13},{9,1},{13,5},{2,10},{6,14},... | collective-permute-start | bytes 786440 | tf_op jit(solution)/shard_map/ppermute | solution.py:468
  217.5 13.5 %collective-permute-start.20 = (bf16[128,1024]{1,0:T(8,128)(2,1)S(1)}, bf16[128,1024]{1,0:T(8,128)(2,1)S(1)}, u32[]{:S(2)}, u32[]{:S(2)}) collective-permute-start(bf16[128,1024]{1,0:T(8,128)(2,1)S(1)} %get-tuple-element.201), channel_id=1, source_target_pairs={{0,24},{4,28},{8,16},{12,20},{16,8},{20,12},{24,0},{28,4},{1,25},{... | collective-permute-start | bytes 786440 | tf_op jit(solution)/shard_map/ppermute | solution.py:476
  221.6 52.1 %collective-permute-start.63 = (bf16[2,2,128,512]{3,2,1,0:T(8,128)(2,1)S(1)}, bf16[2,2,128,512]{3,2,1,0:T(8,128)(2,1)}, u32[]{:S(2)}, u32[]{:S(2)}) collective-permute-start(bf16[2,2,128,512]{3,2,1,0:T(8,128)(2,1)S(1)} %get-tuple-element.208), channel_id=1, source_target_pairs={{0,4},{4,0},{8,12},{12,8},{1,5},{5,1},{9,13},{13,9},{2,6},{6,2},{1... | collective-permute-start | bytes 1572872 | tf_op jit(solution)/shard_map/ppermute | solution.py:472
  225.0 22.7 %collective-permute-start.47 = (bf16[2,128,256]{2,1,0:T(8,128)(2,1)S(1)}, bf16[2,128,256]{2,1,0:T(8,128)(2,1)S(1)}, u32[]{:S(2)}, u32[]{:S(2)}) collective-permute-start(bf16[2,128,256]{2,1,0:T(8,128)(2,1)S(1)} %get-tuple-element.248), channel_id=1, source_target_pairs={{0,4},{4,0},{8,12},{12,8},{1,5},{5,1},{9,13},{13,9},{2,6},{6,2},{1... | collective-permute-start | bytes 393224 | tf_op jit(solution)/shard_map/ppermute | solution.py:472
  244.8 27.9 %collective-permute-start.50 = (bf16[2,128,512]{2,1,0:T(8,128)(2,1)}, bf16[2,128,512]{2,1,0:T(8,128)(2,1)S(1)}, u32[]{:S(2)}, u32[]{:S(2)}) collective-permute-start(bf16[2,128,512]{2,1,0:T(8,128)(2,1)} %get-tuple-element.252), channel_id=1, source_target_pairs={{0,8},{4,12},{8,0},{12,4},{1,9},{5,13},{9,1},{13,5},{2,10},{6,14},... | collective-permute-start | bytes 786440 | tf_op jit(solution)/shard_map/ppermute | solution.py:468
  245.5 36.7 %collective-permute-start.60 = (bf16[2,2,128,256]{3,2,1,0:T(8,128)(2,1)}, bf16[2,2,128,256]{3,2,1,0:T(8,128)(2,1)}, u32[]{:S(2)}, u32[]{:S(2)}) collective-permute-start(bf16[2,2,128,256]{3,2,1,0:T(8,128)(2,1)} %get-tuple-element.226), channel_id=1, source_target_pairs={{0,16},{16,0},{1,17},{17,1},{2,18},{18,2},{3,19},{19,3},{4,20},{20... | collective-permute-start | bytes 786440 | tf_op jit(solution)/shard_map/ppermute | solution.py:464
  252.6 17.2 %collective-permute-start.42 = (bf16[128,512]{1,0:T(8,128)(2,1)S(1)}, bf16[128,512]{1,0:T(8,128)(2,1)S(1)}, u32[]{:S(2)}, u32[]{:S(2)}) collective-permute-start(bf16[128,512]{1,0:T(8,128)(2,1)S(1)} %get-tuple-element.264), channel_id=1, source_target_pairs={{0,16},{16,0},{1,17},{17,1},{2,18},{18,2},{3,19},{19,3},{4,20},{20... | collective-permute-start | bytes 393224 | tf_op jit(solution)/shard_map/ppermute | solution.py:464
  254.3 29.5 %collective-permute-start.57 = (bf16[2,2,128,256]{3,2,1,0:T(8,128)(2,1)}, bf16[2,2,128,256]{3,2,1,0:T(8,128)(2,1)}, u32[]{:S(2)}, u32[]{:S(2)}) collective-permute-start(bf16[2,2,128,256]{3,2,1,0:T(8,128)(2,1)} %get-tuple-element.236), channel_id=1, source_target_pairs={{0,16},{16,0},{1,17},{17,1},{2,18},{18,2},{3,19},{19,3},{4,20},{20... | collective-permute-start | bytes 786440 | tf_op jit(solution)/shard_map/ppermute | solution.py:464
  266.0 18.6 %all-to-all-start.4 = ((bf16[8,272,128]{2,1,0:T(8,128)(2,1)}), bf16[8,272,128]{2,1,0:T(8,128)(2,1)S(1)}, u32[]{:S(2)}, u32[]{:S(2)}) async-start(bf16[8,272,128]{2,1,0:T(8,128)(2,1)} %get-tuple-element.88), calls=%async_computation.4 | async-start | bytes 1114112 | tf_op jit(solution)/shard_map/all_to_all | solution.py:485
  269.9 12.4 %collective-permute-start.36 = (bf16[128,512]{1,0:T(8,128)(2,1)S(1)}, bf16[128,512]{1,0:T(8,128)(2,1)S(1)}, u32[]{:S(2)}, u32[]{:S(2)}) collective-permute-start(bf16[128,512]{1,0:T(8,128)(2,1)S(1)} %get-tuple-element.269), channel_id=1, source_target_pairs={{0,8},{4,12},{8,0},{12,4},{1,9},{5,13},{9,1},{13,5},{2,10},{6,14},... | collective-permute-start | bytes 393224 | tf_op jit(solution)/shard_map/ppermute | solution.py:468
  272.6 20.0 %collective-permute-start.43 = (bf16[2,128,512]{2,1,0:T(8,128)(2,1)}, bf16[2,128,512]{2,1,0:T(8,128)(2,1)}, u32[]{:S(2)}, u32[]{:S(2)}) collective-permute-start(bf16[2,128,512]{2,1,0:T(8,128)(2,1)} %get-tuple-element.262), channel_id=1, source_target_pairs={{0,8},{4,12},{8,0},{12,4},{1,9},{5,13},{9,1},{13,5},{2,10},{6,14},... | collective-permute-start | bytes 786440 | tf_op jit(solution)/shard_map/ppermute | solution.py:468
  273.7 25.0 %collective-permute-start.54 = (bf16[2,2,128,512]{3,2,1,0:T(8,128)(2,1)}, bf16[2,2,128,512]{3,2,1,0:T(8,128)(2,1)}, u32[]{:S(2)}, u32[]{:S(2)}) collective-permute-start(bf16[2,2,128,512]{3,2,1,0:T(8,128)(2,1)} %get-tuple-element.210), channel_id=1, source_target_pairs={{0,4},{4,0},{8,12},{12,8},{1,5},{5,1},{9,13},{13,9},{2,6},{6,2},{1... | collective-permute-start | bytes 1572872 | tf_op jit(solution)/shard_map/ppermute | solution.py:472
  282.2 16.7 %collective-permute-start.51 = (bf16[2,2,128,512]{3,2,1,0:T(8,128)(2,1)}, bf16[2,2,128,512]{3,2,1,0:T(8,128)(2,1)}, u32[]{:S(2)}, u32[]{:S(2)}) collective-permute-start(bf16[2,2,128,512]{3,2,1,0:T(8,128)(2,1)} %get-tuple-element.212), channel_id=1, source_target_pairs={{0,4},{4,0},{8,12},{12,8},{1,5},{5,1},{9,13},{13,9},{2,6},{6,2},{1... | collective-permute-start | bytes 1572872 | tf_op jit(solution)/shard_map/ppermute | solution.py:472
  282.3 12.1 %collective-permute-start.48 = (bf16[2,2,128,256]{3,2,1,0:T(8,128)(2,1)}, bf16[2,2,128,256]{3,2,1,0:T(8,128)(2,1)}, u32[]{:S(2)}, u32[]{:S(2)}) collective-permute-start(bf16[2,2,128,256]{3,2,1,0:T(8,128)(2,1)} %get-tuple-element.246), channel_id=1, source_target_pairs={{0,16},{16,0},{1,17},{17,1},{2,18},{18,2},{3,19},{19,3},{4,20},{20... | collective-permute-start | bytes 786440 | tf_op jit(solution)/shard_map/ppermute | solution.py:464
  283.8 10.3 %collective-permute-start.37 = (bf16[2,128,256]{2,1,0:T(8,128)(2,1)S(1)}, bf16[2,128,256]{2,1,0:T(8,128)(2,1)S(1)}, u32[]{:S(2)}, u32[]{:S(2)}) collective-permute-start(bf16[2,128,256]{2,1,0:T(8,128)(2,1)S(1)} %get-tuple-element.268), channel_id=1, source_target_pairs={{0,4},{4,0},{8,12},{12,8},{1,5},{5,1},{9,13},{13,9},{2,6},{6,2},{1... | collective-permute-start | bytes 393224 | tf_op jit(solution)/shard_map/ppermute | solution.py:472
  289.1 39.1 %all-to-all-start.5 = ((bf16[8,2,272,128]{3,2,1,0:T(8,128)(2,1)}), bf16[8,2,272,128]{3,2,1,0:T(8,128)(2,1)S(1)}, u32[]{:S(2)}, u32[]{:S(2)}) async-start(bf16[8,2,272,128]{3,2,1,0:T(8,128)(2,1)} %get-tuple-element.97), calls=%async_computation.5 | async-start | bytes 2228224 | tf_op jit(solution)/shard_map/all_to_all | solution.py:485
  292.6 128.1 %all-reduce.6.cloned.1.call-start = ((), (), s32[]{:S(2)}) async-start(), calls=%async_computation.9 | async-start | bytes 4194304 | tf_op jit(solution)/shard_map/psum | solution.py:1173
  292.7 12.9 %collective-permute-start.35 = (bf16[2,2,128,512]{3,2,1,0:T(8,128)(2,1)}, bf16[2,2,128,512]{3,2,1,0:T(8,128)(2,1)S(1)}, u32[]{:S(2)}, u32[]{:S(2)}) collective-permute-start(bf16[2,2,128,512]{3,2,1,0:T(8,128)(2,1)} %get-tuple-element.216), channel_id=1, source_target_pairs={{0,4},{4,0},{8,12},{12,8},{1,5},{5,1},{9,13},{13,9},{2,6},{6,2},{1... | collective-permute-start | bytes 1572872 | tf_op jit(solution)/shard_map/ppermute | solution.py:472
  294.1 25.4 %collective-permute-start.44 = (bf16[2,2,128,512]{3,2,1,0:T(8,128)(2,1)S(1)}, bf16[2,2,128,512]{3,2,1,0:T(8,128)(2,1)S(1)}, u32[]{:S(2)}, u32[]{:S(2)}) collective-permute-start(bf16[2,2,128,512]{3,2,1,0:T(8,128)(2,1)S(1)} %get-tuple-element.214), channel_id=1, source_target_pairs={{0,4},{4,0},{8,12},{12,8},{1,5},{5,1},{9,13},{13,9},{2,6},{6,2},{1... | collective-permute-start | bytes 1572872 | tf_op jit(solution)/shard_map/ppermute | solution.py:472
  294.4 19.5 %collective-permute-start.38 = (bf16[2,2,128,256]{3,2,1,0:T(8,128)(2,1)S(1)}, bf16[2,2,128,256]{3,2,1,0:T(8,128)(2,1)S(1)}, u32[]{:S(2)}, u32[]{:S(2)}) collective-permute-start(bf16[2,2,128,256]{3,2,1,0:T(8,128)(2,1)S(1)} %get-tuple-element.266), channel_id=1, source_target_pairs={{0,16},{16,0},{1,17},{17,1},{2,18},{18,2},{3,19},{19,3},{4,20},{20... | collective-permute-start | bytes 786440 | tf_op jit(solution)/shard_map/ppermute | solution.py:464
  298.8 20.7 %collective-permute-start.41 = (bf16[2,2,128,256]{3,2,1,0:T(8,128)(2,1)S(1)}, bf16[2,2,128,256]{3,2,1,0:T(8,128)(2,1)S(1)}, u32[]{:S(2)}, u32[]{:S(2)}) collective-permute-start(bf16[2,2,128,256]{3,2,1,0:T(8,128)(2,1)S(1)} %copy-done.30), channel_id=1, source_target_pairs={{0,16},{16,0},{1,17},{17,1},{2,18},{18,2},{3,19},{19,3},{4,20},{20... | collective-permute-start | bytes 786440 | tf_op jit(solution)/shard_map/ppermute | solution.py:464
  298.9 28.4 %collective-permute-start.45 = (bf16[512,384]{1,0:T(8,128)(2,1)S(1)}, bf16[512,384]{1,0:T(8,128)(2,1)S(1)}, u32[]{:S(2)}, u32[]{:S(2)}) collective-permute-start(bf16[512,384]{1,0:T(8,128)(2,1)S(1)} %copy-done.26), channel_id=1, source_target_pairs={{0,16},{16,0},{1,17},{17,1},{2,18},{18,2},{3,19},{19,3},{4,20},{20... | collective-permute-start | bytes 1179656 | tf_op jit(solution)/shard_map/ppermute | solution.py:464
  331.2 10.1 %collective-permute-start.27 = (bf16[2,272,128]{2,1,0:T(8,128)(2,1)}, bf16[2,272,128]{2,1,0:T(8,128)(2,1)S(1)}, u32[]{:S(2)}, u32[]{:S(2)}) collective-permute-start(bf16[2,272,128]{2,1,0:T(8,128)(2,1)} %shard_map.381), channel_id=1, source_target_pairs={{0,1},{1,0},{2,3},{3,2},{4,5},{5,4},{6,7},{7,6},{8,9},{9,8},{10,11... | collective-permute-start | bytes 417800 | tf_op jit(solution)/shard_map/ppermute | solution.py:1145
  342.3 18.1 %collective-permute-start.28 = (bf16[2,272,128]{2,1,0:T(8,128)(2,1)S(1)}, bf16[2,272,128]{2,1,0:T(8,128)(2,1)S(1)}, u32[]{:S(2)}, u32[]{:S(2)}) collective-permute-start(bf16[2,272,128]{2,1,0:T(8,128)(2,1)S(1)} %add_convert_fusion.1), channel_id=1, source_target_pairs={{0,2},{2,0},{1,3},{3,1},{4,6},{6,4},{5,7},{7,5},{8,10},{10,8},{9,1... | collective-permute-start | bytes 417800 | tf_op jit(solution)/shard_map/ppermute | solution.py:1146
  347.0 25.1 %collective-permute-start.26 = (bf16[1024,261]{0,1:T(8,128)(2,1)S(1)}, bf16[1024,261]{0,1:T(8,128)(2,1)S(1)}, u32[]{:S(2)}, u32[]{:S(2)}) collective-permute-start(bf16[1024,261]{0,1:T(8,128)(2,1)S(1)} %copy.102), channel_id=1, source_target_pairs={{0,16},{16,0},{1,17},{17,1},{2,18},{18,2},{3,19},{19,3},{4,20},{20... | collective-permute-start | bytes 1603592 | tf_op jit(solution)/shard_map/ppermute | solution.py:464
  368.6 12.6 %collective-permute-start.32 = (bf16[4,2,272,128]{3,2,1,0:T(8,128)(2,1)}, bf16[4,2,272,128]{3,2,1,0:T(8,128)(2,1)}, u32[]{:S(2)}, u32[]{:S(2)}) collective-permute-start(bf16[4,2,272,128]{3,2,1,0:T(8,128)(2,1)} %pad_maximum_fusion.2.near), channel_id=1, source_target_pairs={{0,4},{4,0},{8,12},{12,8},{1,5},{5,1},{9,13},{13,9},{2,6},{6,2},{1... | collective-permute-start | bytes 1671176 | tf_op jit(solution)/shard_map/ppermute | solution.py:472
  (96 other events, 712.3 us)
Sparse Core Ops, SparseCore 0:
  10.5 48.1 all-gather.6
  60.6 52.2 all-gather.8
  115.4 49.3 all-gather.10
  328.3 92.3 all-reduce.5

commit v2 on v1

--- a/solution.py
+++ b/solution.py
@@ -477,26 +477,105 @@
 
 
 def gather_eight(value):
-    near = jnp.stack([value, swap_row(value), swap_chip(value), swap_both(value)])
-    return near, swap_core(near)
+    near = [value, swap_row(value), swap_chip(value), swap_both(value)]
+    return near + [swap_core(part) for part in near]
 
 
 def exchange(value):
     return lax.all_to_all(value, GROUP, 0, 0, tiled=True)
 
 
-def kernel(body, outs, *args, scratch=(), scalars=True, cost=None):
-    vmem = pl.BlockSpec(memory_space=pltpu.VMEM)
-    smem = pl.BlockSpec(memory_space=pltpu.SMEM)
-    specs = [smem if scalars and i == 0 else vmem for i in range(len(args))]
+def hold(values, *others):
+    return lax.optimization_barrier(tuple(values) + others)[: len(values)]
+
+
+def after(value, *others):
+    return lax.optimization_barrier((value,) + others)[0]
+
+
+class Any:
+    def __init__(self, value):
+        self.value = value
+
+
+class Small:
+    def __init__(self, value):
+        self.value = value
+
+
+def kernel(body, outs, *args, scratch=()):
+    spaces = {Any: pl.ANY, Small: pltpu.SMEM}
+    specs = [pl.BlockSpec(memory_space=spaces.get(type(arg), pltpu.VMEM)) for arg in args]
+    values = [arg.value if type(arg) in spaces else arg for arg in args]
     return pl.pallas_call(
         body,
         out_shape=tuple(jax.ShapeDtypeStruct(shape, kind) for shape, kind in outs),
         in_specs=specs,
-        out_specs=tuple(vmem for _ in outs),
+        out_specs=tuple(pl.BlockSpec(memory_space=pltpu.VMEM) for _ in outs),
         scratch_shapes=list(scratch),
         compiler_params=pltpu.CompilerParams(vmem_limit_bytes=56 * 1024 * 1024),
-    )(*args)
+    )(*values)
+
+
+def from_plane(half, *others):
+    half = after(half, *others)
+    return [swap_row(half), swap_chip(half), swap_both(half)]
+
+
+def from_next(parts, *others):
+    parts = lax.optimization_barrier(tuple(parts) + others)[: len(parts)]
+    return [lax.ppermute(part, "dp", SEQ_NEAR) for part in parts]
+
+
+def from_core(parts, *others):
+    parts = lax.optimization_barrier(tuple(parts) + others)[: len(parts)]
+    return [swap_core(part) for part in parts]
+
+
+def weight_buffer(count):
+    return [pltpu.VMEM((8, 2, count * WIDE, WIDE), jnp.bfloat16), pltpu.SemaphoreType.DMA((16,))]
+
+
+def load_weights(scalars, blocks, buffer, sems, first):
+    height = buffer.shape[2]
+    rows = pl.ds(first * WIDE, height)
+    plane = scalars[4]
+    copies = []
+    for core in range(2):
+        for half in range(2):
+            copies.append((blocks[core].at[half, rows, :], block_of(scalars, 0, core), half))
+    for k, block in enumerate(blocks[2:]):
+        core, other, step = k // 6, k // 3 % 2, k % 3 + 1
+        half = 1 - plane if other else plane
+        copies.append((block.at[rows, :], block_of(scalars, step, core), half))
+    copies = [
+        pltpu.make_async_copy(source, buffer.at[block, half], sems.at[k])
+        for k, (source, block, half) in enumerate(copies)
+    ]
+    for copy in copies:
+        copy.start()
+    return copies
+
+
+def load_plain(scalars, blocks, buffer, sems):
+    copies = [
+        pltpu.make_async_copy(
+            block, buffer.at[block_of(scalars, j % 4, j // 4)], sems.at[j]
+        )
+        for j, block in enumerate(blocks)
+    ]
+    for copy in copies:
+        copy.start()
+    return copies
+
+
+def plain_buffer():
+    return [pltpu.VMEM((8, 512, WIDE), jnp.bfloat16), pltpu.SemaphoreType.DMA((8,))]
+
+
+def wait_all(copies):
+    for copy in copies:
+        copy.wait()
 
 
 def mm(a, b):
@@ -559,17 +638,6 @@
     return lax.broadcasted_iota(jnp.int32, (count, lanes), 0)
 
 
-def fold_kernel(scalars, key, value, query, out, parts):
-    at = pl.multiple_of(scalars[2] * WIDE, WIDE)
-    channels = key.shape[0]
-    parts[...] = jnp.zeros_like(parts)
-    first = low(mt(key[:, pl.ds(at, WIDE)], query[...]))
-    second = low(mm(value[:, pl.ds(at, WIDE)], out[...]))
-    for b in range(4):
-        parts[b, 0, 0:channels, :] = first[:, b * BLOCK : (b + 1) * BLOCK]
-        parts[b, 1, 0:channels, :] = second[:, b * BLOCK : (b + 1) * BLOCK]
-
-
 def add_kernel(parts, total):
     acc = full(parts[0])
     for b in range(1, parts.shape[0]):
@@ -577,37 +645,81 @@
     total[...] = low(acc)
 
 
-def input_kernel(rows, gain, plain, turned, *, channels):
-    value = full(rows[...])
-    lanes = lax.broadcasted_iota(jnp.int32, value.shape, 1)
-    center = jnp.sum(value, axis=-1, keepdims=True) / channels
-    shifted = jnp.where(lanes < channels, value - center, 0.0)
-    spread = jnp.sum(shifted * shifted, axis=-1, keepdims=True) / channels
-    result = shifted * lax.rsqrt(spread + EPS) * gain[...]
-    plain[...] = low(result)
-    turned[...] = low(result.T)
-
-
-def first_kernel(latents, gain, normed):
-    value, _ = norm_parts(full(latents[...]))
-    normed[...] = low(value * gain[...])
-
-
-def query_kernel(scalars, near, far, normed, folded_query, folded_out, query):
-    row, col = scalars[1], scalars[2]
-    for step in range(4):
-        for core, source in ((0, near), (1, far)):
-            block = 4 * (row ^ (step % 2)) + (col ^ (2 * (step // 2) + core))
-            at = pl.multiple_of(block * BLOCK, BLOCK)
-            folded_query[:, pl.ds(at, BLOCK)] = source[step, 0]
-            folded_out[:, pl.ds(at, BLOCK)] = source[step, 1]
-    query[...] = low(mt(folded_query[...], normed[...]) * (1.0 / math.sqrt(D)))
-
-
-def cross_kernel(scalars, near, far, limits, plain, turned, queries, result, *, channels):
-    for step in range(4):
-        for core, source in ((0, near), (1, far)):
-            queries[block_of(scalars, step, core)] = source[step]
+def input_kernel(scalars, inputs, gain, plain, turned, rows, sem):
+    count, channels = rows.shape
+    at = pl.multiple_of(scalars[1] * count, count)
+    copy = pltpu.make_async_copy(inputs.at[pl.ds(at, count), :], rows, sem)
+    copy.start()
+    plain[...] = jnp.zeros_like(plain)
+    turned[...] = jnp.zeros_like(turned)
+    copy.wait()
+    normed, _ = norm_parts(full(rows[...]))
+    result = normed * gain[...]
+    plain[:, 0:channels] = low(result)
+    turned[0:channels, :] = low(result.T)
+
+
+def pack_kernel(scalars, query, key, value, *rest):
+    weights, (mine, theirs, first, first_half, second, second_half) = rest[:6], rest[7:]
+    for k, weight in enumerate((query, key, value)):
+        for place, row in ((mine, scalars[1]), (theirs, 1 - scalars[1])):
+            at = pl.multiple_of(row * HEAD, HEAD)
+            place[:, k * HEAD : (k + 1) * HEAD] = weight[:, pl.ds(at, HEAD)]
+    for k, weight in enumerate(weights):
+        whole, half = ((first, first_half), (second, second_half))[k // 3]
+        rows = slice(k % 3 * WIDE, (k % 3 + 1) * WIDE)
+        at = pl.multiple_of(scalars[4] * WIDE, WIDE)
+        if weight.shape[0] == WIDE:
+            whole[0, rows, :] = weight[:, :WIDE]
+            whole[1, rows, :] = weight[:, WIDE:]
+            half[rows, :] = weight[:, pl.ds(at, WIDE)]
+        else:
+            whole[0, rows, :] = weight[:WIDE, :]
+            whole[1, rows, :] = weight[WIDE:, :]
+            half[rows, :] = weight[pl.ds(at, WIDE), :]
+
+
+def query_kernel(
+    scalars, latents, other, gains, key, *rest
+):
+    blocks, (state, normed_in, folded, query, wide, buffer, sems) = rest[1:9], rest[9:]
+    copies = load_plain(scalars, blocks, buffer, sems)
+    row = scalars[1]
+    rows = pl.multiple_of(row * BLOCK, BLOCK)
+    mine = pl.multiple_of(row * 512, 512)
+    theirs = pl.multiple_of((1 - row) * 512, 512)
+    state[:, pl.ds(mine, 512)] = latents[pl.ds(rows, BLOCK), :]
+    state[:, pl.ds(theirs, 512)] = other[...]
+    value, _ = norm_parts(full(state[...]))
+    normed_in[...] = low(value * gains[0:1, :])
+    channels = key.shape[0]
+    folded[...] = jnp.zeros_like(folded)
+    wait_all(copies)
+    for r in range(2):
+        acc = None
+        for c in range(4):
+            part = mt(key[:, c * WIDE : (c + 1) * WIDE], buffer[2 * c + r])
+            acc = part if acc is None else acc + part
+        folded[0:channels, r * 512 : (r + 1) * 512] = low(acc)
+    query[...] = low(mt(folded[...], normed_in[...]) * (1.0 / math.sqrt(D)))
+
+
+BULK = 14
+
+
+def fold_out_kernel(scalars, value, *rest):
+    blocks, (folded, buffer, sems) = rest[:BULK], rest[BULK:]
+    copies = load_weights(scalars, blocks, buffer, sems, 0)
+    channels = value.shape[0]
+    folded[...] = jnp.zeros_like(folded)
+    wait_all(copies)
+    folded[0:channels, :] = low(shrink_tiles(value[...], buffer, 0))
+
+
+def cross_kernel(scalars, limits, plain, turned, *rest, channels):
+    blocks, (queries, result) = rest[:8], rest[8:]
+    for j, block in enumerate(blocks):
+        queries[block_of(scalars, j % 4, j // 4)] = block[...]
     base = scalars[3]
     count, padded = plain.shape
 
@@ -635,59 +747,80 @@
     lax.fori_loop(0, 4, pair, 0)
 
 
+def tile_of(packed, c, r, half, at):
+    return packed[2 * c + r, half, at * WIDE : (at + 1) * WIDE, :]
+
+
+def part_of(value, index):
+    return value[:, index * WIDE : (index + 1) * WIDE]
+
+
+def summed(parts):
+    acc = parts[0]
+    for part in parts[1:]:
+        acc = acc + part
+    return acc
+
+
 def expand_tiles(value, packed, at):
-    outs = []
-    for c in range(4):
-        acc = None
-        for r in range(2):
-            part = mm(value[:, r * 512 : (r + 1) * 512], packed[2 * c + r, at : at + 512, :])
-            acc = part if acc is None else acc + part
-        outs.append(acc)
-    return jnp.concatenate(outs, axis=1)
+    return jnp.concatenate(
+        [
+            summed(
+                [
+                    mm(part_of(value, 2 * r + h), tile_of(packed, c, r, h, at))
+                    for r in range(2)
+                    for h in range(2)
+                ]
+            )
+            for c in range(4)
+        ],
+        axis=1,
+    )
 
 
 def shrink_tiles(value, packed, at):
-    outs = []
-    for r in range(2):
-        for j in range(2):
-            acc = None
-            for c in range(4):
-                tile = packed[2 * c + r, at + j * WIDE : at + (j + 1) * WIDE, :]
-                part = mm(value[:, c * WIDE : (c + 1) * WIDE], tile)
-                acc = part if acc is None else acc + part
-            outs.append(acc)
-    return jnp.concatenate(outs, axis=1)
+    return jnp.concatenate(
+        [
+            summed([mm(part_of(value, c), tile_of(packed, c, r, h, at)) for c in range(4)])
+            for r in range(2)
+            for h in range(2)
+        ],
+        axis=1,
+    )
 
 
 def expand_back(value, packed, at):
-    outs = []
-    for r in range(2):
-        acc = None
-        for c in range(4):
-            part = mt(value[:, c * WIDE : (c + 1) * WIDE], packed[2 * c + r, at : at + 512, :])
-            acc = part if acc is None else acc + part
-        outs.append(acc)
-    return jnp.concatenate(outs, axis=1)
+    return jnp.concatenate(
+        [
+            summed([mt(part_of(value, c), tile_of(packed, c, r, h, at)) for c in range(4)])
+            for r in range(2)
+            for h in range(2)
+        ],
+        axis=1,
+    )
 
 
 def shrink_back(value, packed, at):
-    outs = []
-    for c in range(4):
-        acc = None
-        for r in range(2):
-            for j in range(2):
-                tile = packed[2 * c + r, at + j * WIDE : at + (j + 1) * WIDE, :]
-                start = r * 512 + j * WIDE
-                part = mt(value[:, start : start + WIDE], tile)
-                acc = part if acc is None else acc + part
-        outs.append(acc)
-    return jnp.concatenate(outs, axis=1)
-
-
-def merge_kernel(
-    parts, latents, folded_out, packed, gains,
-    mixed_out, lse_out, after_cross, hidden, upward, active, after_first, self_in, *, channels
-):
+    return jnp.concatenate(
+        [
+            summed(
+                [
+                    mt(part_of(value, 2 * r + h), tile_of(packed, c, r, h, at))
+                    for r in range(2)
+                    for h in range(2)
+                ]
+            )
+            for c in range(4)
+        ],
+        axis=1,
+    )
+
+
+def merge_kernel(scalars, parts, latents, folded_out, gains, *rest, channels):
+    blocks, rest = rest[:BULK], rest[BULK:]
+    mixed_out, lse_out, after_cross, hidden, upward, active, after_first, self_in = rest[:8]
+    packed, sems = rest[8:]
+    copies = load_weights(scalars, blocks, packed, sems, 1)
     lses = []
     for d in range(8):
         rows = full(parts[d, channels : channels + 3, :])
@@ -710,24 +843,25 @@
     normed, _ = norm_parts(state)
     hid = low(normed * gains[1:2, :])
     hidden[...] = hid
+    wait_all(copies)
     up = expand_tiles(hid, packed, 0)
     upward[...] = up
     act = low(gelu_value(up))
     active[...] = act
-    state = state + shrink_tiles(act, packed, 512)
+    state = state + shrink_tiles(act, packed, 1)
     after_first[...] = state
     normed, _ = norm_parts(state)
     self_in[...] = low(normed * gains[2:3, :])
 
 
-def attend_kernel(
-    scalars, near, far, weights, limits, places, rows_out, qkv_out, mixed_out, lse_out, sent
-):
-    for core, source in ((0, near), (1, far)):
-        for step in range(4):
-            at = pl.multiple_of(block_of(scalars, step, core) * BLOCK, BLOCK)
-            rows = source[step]
-            rows_out[pl.ds(at, BLOCK), :] = rows
+def attend_kernel(scalars, mine, theirs, limits, places, *rest):
+    blocks, (rows_out, weights, qkv_out, mixed_out, lse_out, sent) = rest[:8], rest[8:]
+    row = scalars[1]
+    weights[pl.ds(pl.multiple_of(row * 512, 512), 512), :] = mine[...]
+    weights[pl.ds(pl.multiple_of((1 - row) * 512, 512), 512), :] = theirs[...]
+    for j, block in enumerate(blocks):
+        at = pl.multiple_of(block_of(scalars, j % 4, j // 4) * BLOCK, BLOCK)
+        rows_out[pl.ds(at, BLOCK), :] = block[...]
     qkv_out[...] = low(mm(rows_out[...], weights[...]))
     scale = 1.0 / math.sqrt(HEAD)
     turned = low(full(qkv_out[:, 2 * HEAD :]).T)
@@ -752,35 +886,153 @@
     lax.fori_loop(0, 4, pair, 0)
 
 
-def second_kernel(
-    parts, after_first, cotangent, gain, packed,
-    out, joined, hidden, active, grad_up, grad_gain, branch_grad, state_grad, sent
-):
-    att = jnp.concatenate([full(parts[h]).T for h in range(8)], axis=1)
-    att = low(att)
-    joined[...] = att
+def split_halves(scalars, values, keep, give):
+    row = scalars[1]
+    for k, value in enumerate(values):
+        low_half, high_half = value[:, :512], value[:, 512:]
+        keep[k] = jnp.where(row == 0, low_half, high_half)
+        give[k] = jnp.where(row == 0, high_half, low_half)
+
+
+def split_quarters(scalars, values, quarters):
+    for k, value in enumerate(values):
+        for c in range(4):
+            quarters[scalars[2] ^ c, k] = part_of(value, c)
+
+
+def second_kernel(scalars, parts, after_first, cotangent, gains, early_hidden, early_active, *rest):
+    blocks, rest = rest[:BULK], rest[BULK:]
+    out, keep, give, quarters, grad_gain, state_grad, sent = rest[:7]
+    packed, sems = rest[7:]
+    gain = gains[3:4, :]
+    copies = load_weights(scalars, blocks, packed, sems, 0)
+    att = low(jnp.concatenate([full(parts[h]).T for h in range(8)], axis=1))
+    wait_all(copies)
     state = after_first[...] + shrink_tiles(att, packed, 0)
     normed, inv = norm_parts(state)
-    hid = low(normed * gain[...])
-    hidden[...] = hid
-    up = expand_tiles(hid, packed, 512)
+    hid = low(normed * gain)
+    up = expand_tiles(hid, packed, 1)
     act = low(gelu_value(up))
-    active[...] = act
-    final = state + shrink_tiles(act, packed, 1024)
-    out[...] = low(final)
+    out[...] = low(state + shrink_tiles(act, packed, 2))
     grad = cotangent[...]
-    grad_act = shrink_back(grad, packed, 1024)
-    gu = low(grad_act * gelu_slope(up))
-    grad_up[...] = gu
-    grad_hid = expand_back(gu, packed, 512)
-    back, grad_gain[...] = norm_back(grad_hid, gain[...], normed, inv)
+    gu = low(shrink_back(grad, packed, 2) * gelu_slope(up))
+    back, grad_gain[...] = norm_back(expand_back(gu, packed, 1), gain, normed, inv)
     total = full(grad) + back
     state_grad[...] = total
     lower = low(total)
-    branch_grad[...] = lower
     grad_att = shrink_back(lower, packed, 0)
     for h in range(8):
         sent[h] = low(grad_att[:, h * BLOCK : (h + 1) * BLOCK].T)
+    split_halves(scalars, (hid, grad, lower, early_hidden[...]), keep, give)
+    split_quarters(scalars, (gu, act, att, early_active[...]), quarters)
+
+
+def put_chunk(scalars, keep, give, index, value):
+    here = scalars[4] == index // 2
+    at = scalars[5] ^ (index % 2)
+
+    @pl.when(here)
+    def _():
+        keep[at] = value
+
+    @pl.when(jnp.logical_not(here))
+    def _():
+        give[at] = value
+
+
+def read_chunk(scalars, mine, theirs, index):
+    at = scalars[5] ^ (index % 2)
+    return jnp.where(scalars[4] == index // 2, full(mine[at]), full(theirs[at]))
+
+
+def columns(value, index):
+    return value[:, index * BLOCK : (index + 1) * BLOCK]
+
+
+def row_block(value, index):
+    return value[index * BLOCK : (index + 1) * BLOCK, :]
+
+
+def weight_kernel(scalars, *refs):
+    halves, quarters, rest = refs[:8], refs[8:16], refs[16:]
+    keep, give, halves_turned, quarters_all, quarters_turned = rest
+    for k in range(3):
+        for j in range(8):
+            at = slice(j * BLOCK, (j + 1) * BLOCK)
+            if k == 0:
+                halves_turned[:, at] = low(full(halves[j][k]).T)
+                quarters_all[at, :] = quarters[j][k]
+            else:
+                quarters_turned[k - 1, :, at] = low(full(quarters[j][k]).T)
+    expand = low(mm(halves_turned[...], quarters_all[...]))
+    shrinks = [
+        low(summed([
+            mm(quarters_turned[k - 1, :, j * BLOCK : (j + 1) * BLOCK], halves[j][k])
+            for j in range(8)
+        ]))
+        for k in (1, 2)
+    ]
+    for t in range(4):
+        parts = jnp.concatenate([columns(value, t) for value in shrinks], axis=1)
+        put_chunk(scalars, keep, give, t, jnp.concatenate([row_block(expand, t), parts], axis=0))
+
+
+def weight_out_kernel(scalars, mine, theirs, expand, first_shrink, second_shrink):
+    for t in range(4):
+        chunk = read_chunk(scalars, mine, theirs, t)
+        at = slice(t * BLOCK, (t + 1) * BLOCK)
+        expand[at, :] = chunk[:BLOCK]
+        first_shrink[:, at] = chunk[BLOCK:, :BLOCK]
+        second_shrink[:, at] = chunk[BLOCK:, BLOCK:]
+
+
+def last_weight_kernel(scalars, *refs):
+    early_halves, early_quarters, halves, quarters = refs[:8], refs[8:16], refs[16:24], refs[24:32]
+    keep, give, halves_turned, quarters_all, quarters_turned = refs[32:]
+    for j in range(8):
+        at = slice(j * BLOCK, (j + 1) * BLOCK)
+        halves_turned[:, at] = low(full(early_halves[j][3]).T)
+        quarters_all[at, :] = quarters[j][0]
+        quarters_turned[:, at] = low(full(early_quarters[j][3]).T)
+    expand = low(mm(halves_turned[...], quarters_all[...]))
+    shrink = low(summed([
+        mm(quarters_turned[:, j * BLOCK : (j + 1) * BLOCK], halves[j][0]) for j in range(8)
+    ]))
+    for t in range(4):
+        part = columns(shrink, t)
+        parts = jnp.concatenate([part[:BLOCK], part[BLOCK:]], axis=1)
+        put_chunk(scalars, keep, give, t, jnp.concatenate([row_block(expand, t), parts], axis=0))
+
+
+def last_weight_out_kernel(scalars, mine, theirs, expand, shrink):
+    for t in range(4):
+        chunk = read_chunk(scalars, mine, theirs, t)
+        at = slice(t * BLOCK, (t + 1) * BLOCK)
+        expand[at, :] = chunk[:BLOCK]
+        shrink[:BLOCK, at] = chunk[BLOCK:, :BLOCK]
+        shrink[BLOCK:, at] = chunk[BLOCK:, BLOCK:]
+
+
+def head_weight_kernel(scalars, rows, grads, keep, give):
+    turned = low(full(grads[...]).T)
+    total = mm(turned, rows[...]).T
+    row = scalars[1]
+    mine = low(jnp.where(row == 0, total[:512], total[512:]))
+    theirs = low(jnp.where(row == 0, total[512:], total[:512]))
+    for t in range(4):
+        put_chunk(
+            scalars, keep, give, t,
+            jnp.concatenate([row_block(mine, t), row_block(theirs, t)], axis=1),
+        )
+
+
+def head_out_kernel(scalars, mine, theirs, keep, give):
+    width = keep.shape[1]
+    for t in range(4):
+        chunk = low(read_chunk(scalars, mine, theirs, t))
+        at = slice(t * BLOCK, (t + 1) * BLOCK)
+        keep[at, :] = chunk[:, :width]
+        give[at, :] = chunk[:, width:]
 
 
 def attend_back_kernel(
@@ -818,18 +1070,22 @@
 
 
 def first_back_kernel(
-    own, by_row, by_chip, by_both, state_grad, after_first, after_cross, upward, packed, gains,
-    folded_out, mixed, lse,
-    gain_grads, first_branch, grad_up, cross_branch, cross_grad, value_part, sent, *, channels
+    scalars, own, by_row, by_chip, by_both, state_grad, after_first, after_cross, upward, gains,
+    folded_out, mixed, lse, *rest, channels
 ):
+    blocks, rest = rest[:BULK], rest[BULK:]
+    gain_grads, keep, give, quarters, cross_grad, value_part, sent = rest[:7]
+    packed, sems = rest[7:]
+    copies = load_weights(scalars, blocks, packed, sems, 1)
     grad_in = full(own[...]) + full(by_row[...]) + full(by_chip[...]) + full(by_both[...])
     normed, inv = norm_parts(after_first[...])
     back, self_gain = norm_back(grad_in, gains[2:3, :], normed, inv)
     grad = state_grad[...] + back
     lower = low(grad)
-    first_branch[...] = lower
-    gu = low(shrink_back(lower, packed, 512) * gelu_slope(upward[...]))
-    grad_up[...] = gu
+    wait_all(copies)
+    gu = low(shrink_back(lower, packed, 1) * gelu_slope(upward[...]))
+    split_halves(scalars, (lower,), keep, give)
+    split_quarters(scalars, (gu,), quarters)
     grad_hid = expand_back(gu, packed, 0)
     normed, inv = norm_parts(after_cross[...])
     back, first_gain = norm_back(grad_hid, gains[1:2, :], normed, inv)
@@ -838,7 +1094,6 @@
     grad = grad + back
     cross_grad[...] = grad
     lower = low(grad)
-    cross_branch[...] = lower
     value_part[...] = low(mm(mixed[...], lower))
     grad_mixed = mt(folded_out[...], lower)
     padded = grad_mixed.shape[0]
@@ -851,13 +1106,13 @@
     sent[...] = low(grad_mixed)
 
 
-def cross_back_kernel(
-    scalars, near, far, queries, limits, plain, turned, rows, gain,
-    grad_rows, grad_gain, sent, grads, total, *, channels
-):
-    for step in range(4):
-        for core, source in ((0, near), (1, far)):
-            grads[block_of(scalars, step, core)] = source[step]
+def cross_back_kernel(scalars, queries, limits, plain, turned, inputs, gain, *rest, channels):
+    blocks, (grad_rows, grad_gain, sent, grads, total, rows, sem) = rest[:8], rest[8:]
+    at = pl.multiple_of(scalars[1] * rows.shape[0], rows.shape[0])
+    copy = pltpu.make_async_copy(inputs.at[pl.ds(at, rows.shape[0]), :], rows, sem)
+    copy.start()
+    for j, block in enumerate(blocks):
+        grads[block_of(scalars, j % 4, j // 4)] = block[...]
     base = scalars[3]
     count, padded = plain.shape
     total[...] = jnp.zeros_like(total)
@@ -881,20 +1136,11 @@
         return carry
 
     lax.fori_loop(0, 4, pair, 0)
-    value = full(rows[...])
-    lanes = lax.broadcasted_iota(jnp.int32, value.shape, 1)
-    inside = lanes < channels
-    center = jnp.sum(value, axis=-1, keepdims=True) / channels
-    shifted = jnp.where(inside, value - center, 0.0)
-    inv = lax.rsqrt(jnp.sum(shifted * shifted, axis=-1, keepdims=True) / channels + EPS)
-    normed = shifted * inv
-    grad = jnp.where(inside, total[...], 0.0)
-    grad_gain[...] = jnp.sum(grad * normed, axis=0, keepdims=True)
-    scaled = grad * gain[...]
-    first = jnp.sum(scaled, axis=-1, keepdims=True) / channels
-    second = jnp.sum(scaled * normed, axis=-1, keepdims=True) / channels
-    result = inv * (scaled - first - normed * second)
-    grad_rows[...] = low(result[:, :channels])
+    copy.wait()
+    normed, inv = norm_parts(full(rows[...]))
+    back, wide = norm_back(total[:, 0:channels], gain[...], normed, inv)
+    grad_gain[...] = wide
+    grad_rows[...] = low(back)
 
 
 def last_kernel(
@@ -925,15 +1171,17 @@
         sent[b, 1] = value_part[:, b * BLOCK : (b + 1) * BLOCK]
 
 
-def finish_kernel(
-    scalars, near, far, key, value, packed,
-    grad_query, grad_key, grad_out, grad_value, gain_grads, key_sum, value_sum, *, channels
-):
-    for step in range(4):
-        for core, source in ((0, near), (1, far)):
-            at = pl.multiple_of(block_of(scalars, step, core) * BLOCK, BLOCK)
-            key_sum[:, pl.ds(at, BLOCK)] = source[step, 0]
-            value_sum[:, pl.ds(at, BLOCK)] = source[step, 1]
+def finish_kernel(scalars, key, value, *rest, channels):
+    blocks, query_blocks, rest = rest[:8], rest[8:16], rest[16:]
+    out_blocks, rest = rest[:BULK], rest[BULK:]
+    grad_query, grad_key, grad_out, grad_value, gain_grads = rest[:5]
+    key_sum, value_sum, packed, sems, packed_out, out_sems = rest[5:]
+    copies = load_plain(scalars, query_blocks, packed, sems)
+    copies += load_weights(scalars, out_blocks, packed_out, out_sems, 0)
+    for j, block in enumerate(blocks):
+        at = pl.multiple_of(block_of(scalars, j % 4, j // 4) * BLOCK, BLOCK)
+        key_sum[:, pl.ds(at, BLOCK)] = block[0]
+        value_sum[:, pl.ds(at, BLOCK)] = block[1]
     extra = full(key_sum[channels : channels + 10, :])
     for k in range(5):
         gain_grads[k : k + 1, :] = extra[2 * k : 2 * k + 1] + extra[2 * k + 1 : 2 * k + 2]
@@ -943,8 +1191,11 @@
     grad_query[...] = mm(low(turned[:, :channels]), key[:, pl.ds(at, WIDE)])
     turned = full(value[:, pl.ds(at, WIDE)]).T
     grad_out[...] = mm(low(turned), value_sum[0:channels, pl.ds(half, 512)])
-    grad_key[...] = expand_tiles(key_sum[...], packed, 0)[:channels]
-    grad_value[...] = shrink_back(value_sum[...], packed, 512)[:channels]
+    wait_all(copies)
+    for c in range(4):
+        acc = mm(key_sum[:, 0:512], packed[2 * c]) + mm(key_sum[:, 512:1024], packed[2 * c + 1])
+        grad_key[:, c * WIDE : (c + 1) * WIDE] = acc[:channels]
+    grad_value[...] = shrink_back(value_sum[...], packed_out, 0)[:channels]
 
 
 def wide_rows(value, row):
@@ -954,31 +1205,40 @@
     return keep, give
 
 
-def for_rows(value, row):
-    keep, give = wide_rows(value, row)
-    pair = jnp.stack([keep, swap_row(give)])
-    both = jnp.stack([pair, swap_chip(pair)])
-    return jnp.stack([both, swap_core(both)])
-
-
-def for_cols(value, chip, core):
-    keep, give = wide_rows(value, chip)
-    pair = jnp.stack([keep, swap_chip(give)])
-    half = pair.shape[2] // 2
-    mine = lax.dynamic_slice_in_dim(pair, core * half, half, 2)
-    theirs = lax.dynamic_slice_in_dim(pair, (1 - core) * half, half, 2)
-    both = jnp.stack([mine, swap_core(theirs)])
-    every = jnp.stack([both, swap_row(both)])
-    return jnp.transpose(every, (1, 2, 0, 3, 4))
-
-
-def over_rows(first, second):
-    return lax.dot_general(
-        first.reshape(-1, first.shape[-1]),
-        second.reshape(-1, second.shape[-1]),
-        (((0,), (0,)), ((), ())),
-        preferred_element_type=jnp.float32,
-    )
+def swap_near(value):
+    return lax.ppermute(value, "dp", SEQ_NEAR)
+
+
+def swap_far(value):
+    return lax.ppermute(value, "dp", SEQ_FAR)
+
+
+def plus(a, b):
+    return low(full(a) + full(b))
+
+
+def swap_cross(value):
+    return lax.ppermute(value, "col", col_step(3))
+
+
+def spread_halves(keep, give):
+    mine = [keep, swap_row(give)]
+    mine = mine + [swap_chip(part) for part in mine]
+    return mine + [swap_core(part) for part in mine]
+
+
+def spread_quarters(quarters):
+    mine = [quarters[0], swap_chip(quarters[2]), swap_core(quarters[1]), swap_cross(quarters[3])]
+    theirs = [swap_row(part) for part in mine]
+    return [mine[0], theirs[0], mine[1], theirs[1], mine[2], theirs[2], mine[3], theirs[3]]
+
+
+def over_planes(parts):
+    count = parts.shape[0] // 4
+    at = lax.axis_index("dp")
+    pieces = parts.reshape(4, count, parts.shape[1])
+    total = low(jnp.sum(full(lax.all_to_all(pieces, "dp", 0, 0, tiled=True)), axis=0))
+    return lax.all_gather(total, "dp", axis=0, tiled=True)
 
 
 def in_order(row, own, other, axis):
@@ -991,11 +1251,6 @@
 
 def tiles_of(weight):
     return [weight[:, :WIDE], weight[:, WIDE:]]
-
-
-def all_of(parts):
-    packed = jnp.concatenate(parts, axis=0)
-    return lax.all_gather(packed, GROUP, axis=0, tiled=False)
 
 
 def fast_device(
@@ -1010,7 +1265,9 @@
     padded = -(-(channels + 11) // 16) * 16
     keys_here = inputs.shape[1] // 2
     base = col * inputs.shape[1] + row * keys_here
-    scalars = jnp.stack([2 * col + row, row, col, base]).astype(jnp.int32)
+    plane = lax.axis_index("dp") % 2
+    far_plane = lax.axis_index("dp") // 2
+    scalars = jnp.stack([2 * col + row, row, col, base, plane, far_plane]).astype(jnp.int32)
     rows = BLOCK
 
     def swap_half(block):
@@ -1022,162 +1279,250 @@
         keep, give = wide_rows(value, row)
         return in_order(row, keep, swap_row(give), 0)
 
-    parts = kernel(
-        fold_kernel, [((4, 2, padded, BLOCK), bf)], scalars, cross_key, cross_value, cross_query,
-        cross_out,
-    )[0]
-    parts = lax.all_to_all(parts, "col", 0, 0, tiled=True)
-    folded = kernel(add_kernel, [((2, padded, BLOCK), bf)], parts, scalars=False)[0]
-    fold_near, fold_far = gather_eight(folded)
-
+    small = Small(scalars)
+    inputs_here = inputs[0]
+    gain_here = input_gain[None]
     gains_here = jnp.stack([cross_gain, first_gain, self_gain, second_gain])
+    other_rows = swap_row(
+        lax.dynamic_slice_in_dim(latents[0], (1 - row) * rows, rows, 0)
+    )
+    query_blocks = [cross_query] + from_plane(cross_query)
     gains = in_order(row, gains_here, swap_row(gains_here), 1)
-    state = swap_half(latents[0])
-    normed_in = kernel(
-        first_kernel, [((rows, D), bf)], state, gains[0:1], scalars=False
-    )[0]
-    own_rows = jnp.pad(
-        lax.dynamic_slice_in_dim(inputs[0], row * keys_here, keys_here, 0),
-        ((0, 0), (0, padded - channels)),
-    )
-    wide_gain = jnp.pad(input_gain, (0, padded - channels))[None]
     plain, turned = kernel(
-        functools.partial(input_kernel, channels=channels),
+        input_kernel,
         [((keys_here, padded), bf), ((padded, keys_here), bf)],
-        own_rows, wide_gain, scalars=False,
-    )
+        small, Any(inputs_here), gain_here,
+        scratch=[pltpu.VMEM((keys_here, channels), bf), pltpu.SemaphoreType.DMA(())],
+    )
+    whole, half = (2, 3 * WIDE, WIDE), (3 * WIDE, WIDE)
+    mine, theirs, first_whole, first_half, second_whole, second_half = kernel(
+        pack_kernel,
+        [((512, 3 * HEAD), bf), ((512, 3 * HEAD), bf), (whole, bf), (half, bf), (whole, bf),
+         (half, bf)],
+        small, self_query, self_key, self_value, cross_out, first_expand, first_shrink, self_out,
+        second_expand, second_shrink, Any(plain),
+    )
+    first_plane = from_plane(first_half, other_rows, gains)
     limits = view_limits(positions, piece_start)[0].reshape(8, 1, BLOCK)
     places = positions[0][:, None]
-
-    packed_first = all_of([first_expand] + tiles_of(first_shrink))
-    packed_second = all_of(tiles_of(self_out) + [second_expand] + tiles_of(second_shrink))
-    packed_cross = all_of([cross_query] + tiles_of(cross_out))
-    joined_weights = [
-        w.reshape(w.shape[0], 2, HEAD) for w in (self_query, self_key, self_value)
-    ]
-    mine = jnp.concatenate(
-        [lax.dynamic_index_in_dim(w, row, 1, False) for w in joined_weights], axis=1
-    )
-    theirs = jnp.concatenate(
-        [lax.dynamic_index_in_dim(w, 1 - row, 1, False) for w in joined_weights], axis=1
-    )
-    head_weights = in_order(row, mine, swap_row(theirs), 0)
-
-    folded_query, folded_out, query = kernel(
-        query_kernel, [((padded, D), bf), ((padded, D), bf), ((padded, rows), bf)],
-        scalars, fold_near, fold_far, normed_in,
-    )
-    query_near, query_far = gather_eight(query)
+    query_blocks = query_blocks + from_core(query_blocks, plain)
+    state, normed_in, folded_query, query = kernel(
+        query_kernel,
+        [((rows, D), bf), ((rows, D), bf), ((padded, D), bf), ((padded, rows), bf)],
+        small, latents[0], other_rows, gains, cross_key, Any(plain),
+        *[Any(block) for block in query_blocks],
+        scratch=[pltpu.VMEM((8, BLOCK), f32)] + plain_buffer(),
+    )
+    query_parts = gather_eight(query)
+    theirs = swap_row(after(theirs, query))
+    first_next = from_next(first_plane, query)
     queries, partial_mixed = kernel(
         functools.partial(cross_kernel, channels=channels),
         [((8, padded, BLOCK), bf), ((8, padded, BLOCK), bf)],
-        scalars, query_near, query_far, limits, plain, turned,
+        small, limits, plain, turned, *query_parts,
     )
     received = exchange(partial_mixed)
+    first_core = from_core([first_whole] + first_plane, partial_mixed)
+    second_plane = from_plane(second_half, received)
+    first_last = from_core(first_next, received)
+    first_blocks = [
+        Any(block)
+        for block in [first_whole, first_core[0]] + first_plane + first_next + first_core[1:]
+        + first_last
+    ]
+    folded_out = kernel(
+        fold_out_kernel, [((padded, D), bf)], small, cross_value,
+        *first_blocks, scratch=weight_buffer(1),
+    )[0]
     mixed, lse, after_cross, hidden, upward, active, after_first, self_in = kernel(
         functools.partial(merge_kernel, channels=channels),
         [
             ((padded, rows), bf), ((1, rows), f32), ((rows, D), f32), ((rows, D), bf),
             ((rows, D), f32), ((rows, D), bf), ((rows, D), f32), ((rows, D), bf),
         ],
-        received, state, folded_out, packed_first, gains, scalars=False,
-    )
-    self_near, self_far = gather_eight(self_in)
+        small, received, state, folded_out, gains, *first_blocks,
+        scratch=weight_buffer(2),
+    )
+    self_parts = gather_eight(self_in)
+    second_next = from_next(second_plane, self_in)
+    second_core = from_core([second_whole] + second_plane, self_in)
     total_rows = positions.shape[1]
-    self_rows, qkv, self_mixed, self_lse, sent = kernel(
+    self_rows, head_weights, qkv, self_mixed, self_lse, sent = kernel(
         attend_kernel,
         [
-            ((total_rows, D), bf), ((total_rows, 3 * HEAD), bf), ((HEAD, total_rows), f32),
-            ((1, total_rows), f32), ((8, HEAD, BLOCK), bf),
+            ((total_rows, D), bf), ((D, 3 * HEAD), bf), ((total_rows, 3 * HEAD), bf),
+            ((HEAD, total_rows), f32), ((1, total_rows), f32), ((8, HEAD, BLOCK), bf),
         ],
-        scalars, self_near, self_far, head_weights, limits, places,
-    )
+        small, mine, theirs, limits, places, *self_parts,
+    )
+    second_last = from_core(second_next, qkv)
+    second_blocks = [
+        Any(block)
+        for block in [second_whole, second_core[0]] + second_plane + second_next
+        + second_core[1:] + second_last
+    ]
     received = exchange(sent)
     grad_final = swap_half(cotangent[0])
-    (
-        out, joined, second_hidden, second_active, second_up, second_gain_part, self_branch,
-        state_grad, sent,
-    ) = kernel(
+    out, keep, give, quarters, second_gain_part, state_grad, sent = kernel(
         second_kernel,
         [
-            ((rows, D), bf), ((rows, D), bf), ((rows, D), bf), ((rows, D), bf), ((rows, D), bf),
-            ((1, D), f32), ((rows, D), bf), ((rows, D), f32), ((8, BLOCK, rows), bf),
+            ((rows, D), bf), ((4, rows, 512), bf), ((4, rows, 512), bf), ((4, 4, rows, WIDE), bf),
+            ((1, D), f32), ((rows, D), f32), ((8, BLOCK, rows), bf),
         ],
-        received, after_first, grad_final, gains[3:4], packed_second, scalars=False,
+        small, received, after_first, grad_final, gains, hidden, active,
+        *second_blocks, scratch=weight_buffer(3),
     )
     received = exchange(sent)
+    give, early = hold((give, quarters), received)
+    gave = swap_row(give)
+    early = [early[0], swap_core(early[1]), swap_chip(early[2]), swap_cross(early[3])]
     grad_qkv, sent = kernel(
         attend_back_kernel,
         [((total_rows, 3 * HEAD), bf), ((2, 4, rows, D), bf)],
-        scalars, received, qkv, self_mixed, self_lse, head_weights, limits, places,
-    )
+        small, received, qkv, self_mixed, self_lse, head_weights, limits, places,
+    )
+    chunk = (2, BLOCK, 6 * HEAD)
+    head_keep, head_give = kernel(
+        head_weight_kernel, [(chunk, bf), (chunk, bf)], small, self_rows, grad_qkv,
+    )
+    sent, head_give = hold((sent, head_give), gave, *early[1:])
+    head_near = swap_near(head_give)
     summed = low(full(sent[0]) + full(swap_core(sent[1])))
     by_row, by_chip, by_both = swap_row(summed[1]), swap_chip(summed[2]), swap_both(summed[3])
-    (
-        gain_rows, first_branch, first_up, cross_branch, cross_grad, value_part, sent,
-    ) = kernel(
+    keep, first_quarter, head_mine, head_next = hold(
+        (keep, early[0], plus(head_keep[0], head_near[0]), plus(head_keep[1], head_near[1])),
+        by_row, by_chip, by_both,
+    )
+    kept = swap_chip(keep)
+    first_quarter = swap_row(first_quarter)
+    head_far = swap_far(head_next)
+    gain_rows, last_keep, last_give, last_quarters, cross_grad, value_part, sent = kernel(
         functools.partial(first_back_kernel, channels=channels),
         [
-            ((2, D), f32), ((rows, D), bf), ((rows, D), bf), ((rows, D), bf), ((rows, D), f32),
-            ((padded, D), bf), ((padded, rows), bf),
+            ((2, D), f32), ((1, rows, 512), bf), ((1, rows, 512), bf), ((4, 1, rows, WIDE), bf),
+            ((rows, D), f32), ((padded, D), bf), ((padded, rows), bf),
         ],
-        summed[0], by_row, by_chip, by_both, state_grad, after_first, after_cross, upward,
-        packed_first, gains, folded_out, mixed, lse, scalars=False,
-    )
-    grad_near, grad_far = gather_eight(sent)
+        small, summed[0], by_row, by_chip, by_both, state_grad, after_first, after_cross, upward,
+        gains, folded_out, mixed, lse, *first_blocks,
+        scratch=weight_buffer(2),
+    )
+    sent, head_far = hold((sent, head_far), kept, first_quarter)
+    sent_parts = gather_eight(sent)
+    third = hold([gave] + early[1:] + [plus(head_mine, head_far)], *sent_parts[1:])
+    gave_chip = swap_chip(third[0])
+    other_quarters = [swap_row(part) for part in third[1:4]]
+    head_done = third[4]
+    head_other = swap_far(head_done)
     grad_rows, input_gain_part, sent = kernel(
         functools.partial(cross_back_kernel, channels=channels),
-        [((keys_here, channels), bf), ((1, padded), f32), ((8, padded, BLOCK), bf)],
-        scalars, grad_near, grad_far, queries, limits, plain, turned, own_rows, wide_gain,
-        scratch=[pltpu.VMEM((8, padded, BLOCK), bf), pltpu.VMEM((keys_here, padded), f32)],
+        [((keys_here, channels), bf), ((1, channels), f32), ((8, padded, BLOCK), bf)],
+        small, queries, limits, plain, turned, Any(inputs_here), gain_here, *sent_parts,
+        scratch=[
+            pltpu.VMEM((8, padded, BLOCK), bf), pltpu.VMEM((keys_here, padded), f32),
+            pltpu.VMEM((keys_here, channels), bf), pltpu.SemaphoreType.DMA(()),
+        ],
+    )
+    sent, head_half, gave_chip = hold(
+        (sent, jnp.stack([head_done, head_other]), gave_chip), *other_quarters
     )
     received = exchange(sent)
-    wide_part = jnp.pad(input_gain_part, ((0, 0), (0, D - padded)))
+    head_rest = swap_near(head_half)
+    early_halves = [keep, gave, kept, gave_chip]
+    early_halves = early_halves + from_core(early_halves)
+    theirs = [first_quarter] + other_quarters
+    early_quarters = [part for k in (0, 2, 1, 3) for part in (early[k], theirs[k])]
+    chunk = (2, 3 * BLOCK, WIDE)
+    early_keep, early_give = kernel(
+        weight_kernel, [(chunk, bf), (chunk, bf)],
+        small, *early_halves, *early_quarters,
+        scratch=[
+            pltpu.VMEM((512, D), bf), pltpu.VMEM((D, WIDE), bf), pltpu.VMEM((2, WIDE, D), bf)
+        ],
+    )
+    received, early_give, last_keep, last_give, last_quarters = hold(
+        (received, early_give, last_keep, last_give, last_quarters), head_rest
+    )
+    early_near = swap_near(early_give)
+    last_gave, last_kept = swap_row(last_give), swap_chip(last_keep)
+    last_own = [
+        last_quarters[0], swap_core(last_quarters[1]), swap_chip(last_quarters[2]),
+        swap_cross(last_quarters[3]),
+    ]
+    wide_part = jnp.pad(input_gain_part, ((0, 0), (0, D - channels)))
     extra = jnp.concatenate([gain_rows, second_gain_part, wide_part], axis=0)
     latents_grad, sent = kernel(
         functools.partial(last_kernel, channels=channels),
         [((rows, D), f32), ((8, 2, padded, BLOCK), bf)],
         received, folded_query, normed_in, state, gains, cross_grad, value_part, extra,
-        scalars=False,
-    )
-    received = exchange(sent)
-    total = kernel(add_kernel, [((2, padded, BLOCK), bf)], received, scalars=False)[0]
-    total = low(full(total) + full(lax.ppermute(total, "dp", SEQ_NEAR)))
-    total = low(full(total) + full(lax.ppermute(total, "dp", SEQ_FAR)))
-    sum_near, sum_far = gather_eight(total)
+    )
+    sent, last_gave, *last_own = hold([sent, last_gave] + last_own, last_kept)
+    received_last = exchange(sent)
+    last_halves = [last_keep, last_gave, last_kept, swap_chip(last_gave)]
+    last_theirs = [swap_row(part) for part in last_own]
+    last_parts = [part for k in (0, 2, 1, 3) for part in (last_own[k], last_theirs[k])]
+    received_last, *last_halves = hold([received_last] + last_halves, *last_theirs)
+    total = kernel(add_kernel, [((2, padded, BLOCK), bf)], received_last)[0]
+    last_halves = last_halves + from_core(last_halves, total)
+    near = swap_near(total)
+    out, latents_grad = hold((out, latents_grad), total)
+    chunk = (2, 2 * BLOCK, WIDE)
+    last_keep, last_give = kernel(
+        last_weight_kernel, [(chunk, bf), (chunk, bf)],
+        small, *early_halves, *early_quarters, *last_halves, *last_parts,
+        scratch=[pltpu.VMEM((512, D), bf), pltpu.VMEM((D, WIDE), bf), pltpu.VMEM((WIDE, D), bf)],
+    )
+    head_keep, head_give = kernel(
+        head_out_kernel, [((512, 3 * HEAD), bf), ((512, 3 * HEAD), bf)],
+        small, head_half, head_rest,
+    )
+    total, early_mine, early_next, last_give, head_give = hold(
+        (
+            plus(total, near), plus(early_keep[0], early_near[0]),
+            plus(early_keep[1], early_near[1]), last_give, head_give,
+        )
+    )
+    pair = swap_row(head_give)
+    far = swap_far(total)
+    early_far = swap_far(early_next)
+    last_near = swap_near(last_give)
+    total, early_done = hold((plus(total, far), plus(early_mine, early_far)), pair)
+    total_parts = gather_eight(total)
+    early_other = swap_far(early_done)
+    early_half, last_mine, last_next, *total_parts = hold(
+        [
+            jnp.stack([early_done, early_other]), plus(last_keep[0], last_near[0]),
+            plus(last_keep[1], last_near[1]),
+        ] + total_parts,
+    )
+    early_rest = swap_near(early_half)
+    grad_rows = after(grad_rows, *total_parts[1:])
+    last_far = swap_far(last_next)
     grad_cross_query, grad_cross_key, grad_cross_out, grad_cross_value, gain_grads = kernel(
         functools.partial(finish_kernel, channels=channels),
         [
             (cross_query.shape, f32), (cross_key.shape, f32), (cross_out.shape, f32),
             (cross_value.shape, f32), ((5, D), f32),
         ],
-        scalars, sum_near, sum_far, cross_key, cross_value, packed_cross,
-        scratch=[pltpu.VMEM((padded, D), bf), pltpu.VMEM((padded, D), bf)],
+        small, cross_key, cross_value, *total_parts,
+        *[Any(block) for block in query_blocks], *first_blocks,
+        scratch=[pltpu.VMEM((padded, D), bf), pltpu.VMEM((padded, D), bf)]
+        + plain_buffer() + weight_buffer(1),
     )
     half = D // 2
     gains_mine = lax.dynamic_slice_in_dim(gain_grads, row * half, half, 1)
 
-    grad_second_expand = over_rows(
-        for_rows(second_hidden, row), for_cols(second_up, chip, core)
-    )
-    grad_second_shrink = over_rows(
-        for_cols(second_active, chip, core), for_rows(grad_final, row)
-    )
-    grad_self_out = over_rows(for_cols(joined, chip, core), for_rows(self_branch, row))
-    grad_first_expand = over_rows(for_rows(hidden, row), for_cols(first_up, chip, core))
-    grad_first_shrink = over_rows(for_cols(active, chip, core), for_rows(first_branch, row))
-    grad_heads = low(over_rows(self_rows, grad_qkv))
-    keep = lax.dynamic_slice_in_dim(grad_heads, row * half, half, 0)
-    give = lax.dynamic_slice_in_dim(grad_heads, (1 - row) * half, half, 0)
-    pair = swap_row(give)
-    summed = lax.psum(
-        (
-            low(grad_second_expand), low(grad_second_shrink), low(grad_self_out),
-            keep, pair, low(grad_first_expand), low(grad_first_shrink),
-        ),
-        "dp",
-    )
-    keep, pair = full(summed[3]), full(summed[4])
+    last_done, grad_cross_query = hold((plus(last_mine, last_far), grad_cross_query), early_rest)
+    last_other = swap_far(last_done)
+    early_sums = kernel(
+        weight_out_kernel, [((512, WIDE), f32), ((WIDE, 512), f32), ((WIDE, 512), f32)],
+        small, early_half, early_rest,
+    )
+    last_half = jnp.stack([last_done, last_other])
+    last_total = kernel(
+        last_weight_out_kernel, [((512, WIDE), f32), ((WIDE, 512), f32)],
+        small, last_half, swap_near(last_half),
+    )
+    keep, pair = full(head_keep), full(pair)
     grad_qkv_weights = [
         in_order(row, keep[:, k * HEAD : (k + 1) * HEAD], pair[:, k * HEAD : (k + 1) * HEAD], 1)
         for k in range(3)
@@ -1194,16 +1539,16 @@
         grad_cross_value,
         grad_cross_out,
         gains_mine[1],
-        full(summed[5]),
-        full(summed[6]),
+        last_total[0],
+        last_total[1],
         gains_mine[2],
         grad_qkv_weights[0],
         grad_qkv_weights[1],
         grad_qkv_weights[2],
-        full(summed[2]),
+        early_sums[2],
         gains_mine[3],
-        full(summed[0]),
-        full(summed[1]),
+        early_sums[0],
+        early_sums[1],
     )
 
 

time: 441 us -> 381 us (0.86)
  waiting for transfers between devices: 162 us -> 114 us
  starting transfers between devices: 75.1 us -> 105 us
  Pallas kernels: 77.7 us -> 106 us
  other arithmetic: 38.2 us -> 11.6 us
  between operations: 14.9 us -> 2.44 us
  matrix products: 10.9 us -> 0 us
  blocking collectives: 20.3 us -> 10.6 us
  local copies, waits for them, and re-layouts: 35.7 us -> 26.2 us
    psum x1 -> x0, waiting for transfers between devices: 30.4 us -> none  [fast_device(): lax.psum((low(grad_second_expand), low(grad_second_shrink), low(grad_self...]
    pallas_call x15 -> x20, Pallas kernels: 77.7 us -> 106 us  [kernel(): pl.pallas_call(body, out_shape=tuple((jax.ShapeDtypeStruct(shape, kind) f...]
    ppermute x2 -> x22, waiting for transfers between devices: 21.9 us -> 48.9 us  [the longest x7 21 us: swap_far(): return lax.ppermute(value, 'dp', SEQ_FAR)]
    ppermute x24 -> x26, waiting for transfers between devices: 47.3 us -> 25.1 us  [swap_row(): return lax.ppermute(value, 'row', ROW_SWAP)]
    ppermute x2 -> x22, starting transfers between devices: 5.98 us -> 25.5 us  [the longest x7 10.8 us: swap_far(): return lax.ppermute(value, 'dp', SEQ_FAR)]
    another operation x26 -> x3, other arithmetic: 17.8 us -> 0.85 us  [the longest x1 0.78 us: fast_device(): jnp.stack([head_done, head_other])]
    ppermute x16 -> x14, waiting for transfers between devices: 33.4 us -> 19.3 us  [swap_chip(): return lax.ppermute(value, 'col', col_step(2))]
    all_to_all x1 -> x0, waiting for transfers between devices: 11.7 us -> none  [fast_device(): parts = lax.all_to_all(parts, 'col', 0, 0, tiled=True)]
  transfers between devices with their start and end apart: 73 -> 119, of which waited for: 34 -> 44; matrix products, arithmetic and copies ran while one was open for 15% -> 7% of each run, Pallas kernels for 18% -> 25%
where the time goes in v2:
time: 381 us; the launch traced here: 376 us
  waiting for transfers between devices  114 us (30%)
  Pallas kernels  106 us (28%)
  starting transfers between devices  105 us (28%)
  local copies, waits for them, and re-layouts  26.2 us (7%)
  other arithmetic  11.6 us (3%)
  blocking collectives  10.6 us (3%)
    pallas_call x20, Pallas kernels, kernel(): pl.pallas_call(body, out_shape=tuple((jax.ShapeDtypeStruct(shape, kind) f...  106 us
    ppermute x26, starting transfers between devices, swap_row(): return lax.ppermute(value, 'row', ROW_SWAP)  32.4 us
    ppermute x26, waiting for transfers between devices, swap_row(): return lax.ppermute(value, 'row', ROW_SWAP)  25.1 us
    ppermute x7, waiting for transfers between devices, swap_far(): return lax.ppermute(value, 'dp', SEQ_FAR)  21 us
    ppermute x14, waiting for transfers between devices, swap_chip(): return lax.ppermute(value, 'col', col_step(2))  19.3 us
    ppermute x7, waiting for transfers between devices, swap_near(): return lax.ppermute(value, 'dp', SEQ_NEAR)  17.4 us
    all_to_all x4, starting transfers between devices, exchange(): return lax.all_to_all(value, GROUP, 0, 0, tiled=True)  15.3 us
    unnamed x228, local copies, waits for them, and re-layouts  13.7 us
  transfers between devices with their start and end apart: 119, of which 44 were waited for; matrix products, arithmetic and copies ran while one was open for 7% of the time, Pallas kernels for 25%

profile of v2, /device:TPU:0, one launch (start us, length us, event | category | flops | bytes accessed | tf_op | source)
XLA Modules:
  0.0 375.6 jit_solution(955891322651957200)
XLA Ops:
  0.7 3.0 collective-permute-start.2
  8.2 2.6 copy.54
  12.0 3.5 shard_map.368
  20.3 3.4 shard_map.369
  25.6 2.2 collective-permute-start.19
  30.5 4.6 %shard_map.370 = (bf16[128,1024]{1,0:T(8,128)(2,1)}, bf16[128,1024]{1,0:T(8,128)(2,1)}, bf16[272,1024]{1,0:T(8,128)(2,1)}, bf16[272,128]{1,0:T(8,128)(2,1)}) custom-call(s32[6]{0:T(128)} %stack.69.scalars, bf16[256,512]{1,0:T(8,128)(2,1)} %bitcast.91, bf16[128,512]{1,0:T(8,128)(2,1)} %copy-done.77, f32[4,1024]{1,0:T(4,128)} %maximum_select_fusion.7.gains, ...), custom_call_target="tpu_custom_call" | custom-call | tf_op jit(solution)/shard_map/pallas_call | solution.py:510
  38.7 4.8 %collective-permute-done.18.rest_3_.rest_19_ = bf16[768,256]{1,0:T(8,128)(2,1)S(1)} collective-permute-done((bf16[768,256]{1,0:T(8,128)(2,1)}, bf16[768,256]{1,0:T(8,128)(2,1)S(1)}, u32[]{:S(2)}, u32[]{:S(2)}) %collective-permute-start.18) | collective-permute-done | bytes 393248 | tf_op jit(solution)/shard_map/ppermute | solution.py:468
  50.4 6.6 %shard_map.371 = (bf16[8,272,128]{2,1,0:T(8,128)(2,1)}, bf16[8,272,128]{2,1,0:T(8,128)(2,1)}) custom-call(s32[6]{0:T(128)} %stack.69.scalars, s32[8,1,128]{2,1,0:T(1,128)} %maximum_bitcast_fusion.limits, bf16[1024,272]{1,0:T(8,128)(2,1)} %get-tuple-element.179.rest_6_.rest_0_.plain, bf16[272,1024]{1,0:T(8,128)(2,1)} %get-tuple-element.188.turned, ...), custom_call_target="tpu_custom_call" | custom-call | tf_op jit(solution)/shard_map/pallas_call | solution.py:510
  57.0 4.4 %all-to-all-start = ((bf16[8,272,128]{2,1,0:T(8,128)(2,1)}), bf16[8,272,128]{2,1,0:T(8,128)(2,1)}, u32[]{:S(2)}, u32[]{:S(2)}) async-start(bf16[8,272,128]{2,1,0:T(8,128)(2,1)} %get-tuple-element.189), calls=%async_computation | async-start | bytes 1114112 | tf_op jit(solution)/shard_map/all_to_all | solution.py:485
  63.5 9.5 %collective-permute-done.23.rest_7_.rest_23_ = bf16[768,256]{1,0:T(8,128)(2,1)} collective-permute-done((bf16[768,256]{1,0:T(8,128)(2,1)S(1)}, bf16[768,256]{1,0:T(8,128)(2,1)}, u32[]{:S(2)}, u32[]{:S(2)}) %collective-permute-start.23) | collective-permute-done | bytes 393248 | tf_op jit(solution)/shard_map/ppermute | solution.py:527
  73.6 3.2 collective-permute-start.38
  81.2 4.4 %shard_map.372.folded_out = bf16[272,1024]{1,0:T(8,128)(2,1)} custom-call(s32[6]{0:T(128)} %stack.69.scalars, bf16[261,1024]{1,0:T(8,128)(2,1)} %value.5, bf16[2,768,256]{2,1,0:T(8,128)(2,1)} %get-tuple-element.194.rest_0_.rest_16_, bf16[2,768,256]{2,1,0:T(8,128)(2,1)} %copy-done.1, bf16[768,256]{1,0:T(8,128)(2,1)} %copy-done.2, bf16[768,256]{1,0:T(8,128)(2,1)} %copy-done.3, ...), custom_call_target="tpu_custom_call" | custom-call | tf_op jit(solution)/shard_map/pallas_call | solution.py:510
  85.6 5.5 %shard_map.373 = (bf16[272,128]{1,0:T(8,128)(2,1)}, f32[1,128]{1,0:T(1,128)}, f32[128,1024]{1,0:T(8,128)}, bf16[128,1024]{1,0:T(8,128)(2,1)}, f32[128,1024]{1,0:...) custom-call(s32[6]{0:T(128)} %stack.69.scalars, ...), custom_call_target="tpu_custom_call" | custom-call | tf_op jit(solution)/shard_map/pallas_call | solution.py:510
  92.2 5.4 %collective-permute-done.39.rest_3_ = bf16[768,256]{1,0:T(8,128)(2,1)} collective-permute-done((bf16[768,256]{1,0:T(8,128)(2,1)}, bf16[768,256]{1,0:T(8,128)(2,1)}, u32[]{:S(2)}, u32[]{:S(2)}) %collective-permute-start.39) | collective-permute-done | bytes 393248 | tf_op jit(solution)/shard_map/ppermute | solution.py:468
  99.2 4.8 %collective-permute-done.9.theirs = bf16[512,384]{1,0:T(8,128)(2,1)S(1)} collective-permute-done((bf16[512,384]{1,0:T(8,128)(2,1)}, bf16[512,384]{1,0:T(8,128)(2,1)S(1)}, u32[]{:S(2)}, u32[]{:S(2)}) %collective-permute-start.9) | collective-permute-done | bytes 393248 | tf_op jit(solution)/shard_map/ppermute | solution.py:464
  105.5 4.0 %collective-permute-done.30.rest_1_ = bf16[128,1024]{1,0:T(8,128)(2,1)S(1)} collective-permute-done((bf16[128,1024]{1,0:T(8,128)(2,1)}, bf16[128,1024]{1,0:T(8,128)(2,1)S(1)}, u32[]{:S(2)}, u32[]{:S(2)}) %collective-permute-start.30) | collective-permute-done | bytes 262176 | tf_op jit(solution)/shard_map/ppermute | solution.py:464
  110.1 4.6 %collective-permute-done.32.rest_3_ = bf16[128,1024]{1,0:T(8,128)(2,1)} collective-permute-done((bf16[128,1024]{1,0:T(8,128)(2,1)}, bf16[128,1024]{1,0:T(8,128)(2,1)}, u32[]{:S(2)}, u32[]{:S(2)}) %collective-permute-start.32) | collective-permute-done | bytes 262176 | tf_op jit(solution)/shard_map/ppermute | solution.py:476
  122.4 8.1 %shard_map.374 = (bf16[1024,1024]{1,0:T(8,128)(2,1)}, bf16[1024,384]{1,0:T(8,128)(2,1)}, bf16[1024,384]{1,0:T(8,128)(2,1)}, f32[128,1024]{1,0:T(8,128)}, f32[1,1...) custom-call(s32[6]{0:T(128)} %stack.69.scalars, bf16[512,384]{1,0:T(8,128)(2,1)} %get-tuple-element.180.mine, ...), custom_call_target="tpu_custom_call" | custom-call | tf_op jit(solution)/shard_map/pallas_call | solution.py:510
  131.7 3.6 all-to-all-start.1
  137.0 4.6 %all-to-all-done.1.parts = bf16[8,128,128]{2,1,0:T(8,128)(2,1)S(1)} async-done(((bf16[8,128,128]{2,1,0:T(8,128)(2,1)}), bf16[8,128,128]{2,1,0:T(8,128)(2,1)S(1)}, u32[]{:S(2)}, u32[]{:S(2)}) %all-to-all-start.1) | async-done | bytes 262176 | tf_op jit(solution)/shard_map/all_to_all | solution.py:485
  142.7 9.3 %shard_map.375 = (bf16[128,1024]{1,0:T(8,128)(2,1)}, bf16[4,128,512]{2,1,0:T(8,128)(2,1)}, bf16[4,128,512]{2,1,0:T(8,128)(2,1)}, bf16[4,4,128,256]{3,2,1,0:T(8,1...) custom-call(s32[6]{0:T(128)} %stack.69.scalars, bf16[8,128,128]{2,1,0:T(8,128)(2,1)} %copy-done.36, ...), custom_call_target="tpu_custom_call" | custom-call | tf_op jit(solution)/shard_map/pallas_call | solution.py:510
  152.0 10.6 %all_to_all.25.parts = bf16[8,128,128]{2,1,0:T(8,128)(2,1)} all-to-all(bf16[8,128,128]{2,1,0:T(8,128)(2,1)} %get-tuple-element.225), channel_id=1, replica_groups=mesh['row'=2,'col'=4,'dp'=4] {'col','row'}, dimensions={0} | all-to-all | bytes 524288 | tf_op jit(solution)/shard_map/all_to_all | solution.py:485
  167.0 10.1 %shard_map.376 = (bf16[1024,384]{1,0:T(8,128)(2,1)}, bf16[2,4,128,1024]{3,2,1,0:T(8,128)(2,1)}) custom-call(s32[6]{0:T(128)} %stack.69.scalars, bf16[8,128,128]{2,1,0:T(8,128)(2,1)} %all_to_all.25.parts, bf16[1024,384]{1,0:T(8,128)(2,1)} %get-tuple-element.219.qkv, f32[128,1024]{1,0:T(8,128)} %get-tuple-element.226.mixed, f32[1,1024]{1,0:T(1,128)} %get-tuple-element.227.lse, ...), custom_call_target="tpu_custom_call" | custom-call | tf_op jit(solution)/shard_map/pallas_call | solution.py:510
  177.0 4.1 %shard_map.377 = (bf16[2,128,768]{2,1,0:T(8,128)(2,1)}, bf16[2,128,768]{2,1,0:T(8,128)(2,1)}) custom-call(s32[6]{0:T(128)} %stack.69.scalars, bf16[1024,1024]{1,0:T(8,128)(2,1)} %get-tuple-element.230.rows, bf16[1024,384]{1,0:T(8,128)(2,1)} %get-tuple-element.231.grads), custom_call_target="tpu_custom_call" | custom-call | tf_op jit(solution)/shard_map/pallas_call | solution.py:510
  188.7 5.0 %collective-permute-done.59 = bf16[2,128,768]{2,1,0:T(8,128)(2,1)S(1)} collective-permute-done((bf16[2,128,768]{2,1,0:T(8,128)(2,1)S(1)}, bf16[2,128,768]{2,1,0:T(8,128)(2,1)S(1)}, u32[]{:S(2)}, u32[]{:S(2)}) %collective-permute-start.59) | collective-permute-done | bytes 393248 | tf_op jit(solution)/shard_map/ppermute | solution.py:1209
  194.4 5.6 %collective-permute-done.57.by_chip = bf16[128,1024]{1,0:T(8,128)(2,1)S(1)} collective-permute-done((bf16[128,1024]{1,0:T(8,128)(2,1)S(1)}, bf16[128,1024]{1,0:T(8,128)(2,1)S(1)}, u32[]{:S(2)}, u32[]{:S(2)}) %collective-permute-start.57) | collective-permute-done | bytes 262176 | tf_op jit(solution)/shard_map/ppermute | solution.py:468
  201.7 2.6 collective-permute-start.60
  204.3 7.3 %shard_map.378 = (f32[2,1024]{1,0:T(2,128)}, bf16[1,128,512]{2,1,0:T(8,128)(2,1)}, bf16[1,128,512]{2,1,0:T(8,128)(2,1)}, bf16[4,1,128,256]{3,2,1,0:T(8,128)(2,1)...) custom-call(s32[6]{0:T(128)} %stack.69.scalars, ...), custom_call_target="tpu_custom_call" | custom-call | tf_op jit(solution)/shard_map/pallas_call | solution.py:510
  222.5 2.5 collective-permute-start.70
  228.2 10.0 %shard_map.379 = (bf16[1024,261]{1,0:T(8,128)(2,1)}, f32[1,261]{1,0:T(1,128)}, bf16[8,272,128]{2,1,0:T(8,128)(2,1)}) custom-call(s32[6]{0:T(128)} %stack.69.scalars, bf16[8,272,128]{2,1,0:T(8,128)(2,1)} %get-tuple-element.224.queries, s32[8,1,128]{2,1,0:T(1,128)} %maximum_bitcast_fusion.limits, bf16[1024,272]{1,0:T(8,128)(2,1)} %get-tuple-element.179.rest_6_.rest_0_.plain, ...), custom_call_target="tpu_custom_call" | custom-call | tf_op jit(solution)/shard_map/pallas_call | solution.py:510
  239.8 4.2 %collective-permute-done.74.refs_15_ = bf16[4,128,256]{2,1,0:T(8,128)(2,1)S(1)} collective-permute-done((bf16[4,128,256]{2,1,0:T(8,128)(2,1)S(1)}, bf16[4,128,256]{2,1,0:T(8,128)(2,1)S(1)}, u32[]{:S(2)}, u32[]{:S(2)}) %collective-permute-start.74) | collective-permute-done | bytes 262176 | tf_op jit(solution)/shard_map/ppermute | solution.py:464
  245.1 3.8 %all-to-all-start.3 = ((bf16[8,272,128]{2,1,0:T(8,128)(2,1)}), bf16[8,272,128]{2,1,0:T(8,128)(2,1)S(1)}, u32[]{:S(2)}, u32[]{:S(2)}) async-start(bf16[8,272,128]{2,1,0:T(8,128)(2,1)} %get-tuple-element.259), calls=%async_computation.3 | async-start | bytes 1114112 | tf_op jit(solution)/shard_map/all_to_all | solution.py:485
  250.5 5.5 %shard_map.380 = (bf16[2,384,256]{2,1,0:T(8,128)(2,1)}, bf16[2,384,256]{2,1,0:T(8,128)(2,1)}) custom-call(s32[6]{0:T(128)} %stack.69.scalars, bf16[4,128,512]{2,1,0:T(8,128)(2,1)} %get-tuple-element.261.refs_0_, bf16[4,128,512]{2,1,0:T(8,128)(2,1)} %copy-done.15, bf16[4,128,512]{2,1,0:T(8,128)(2,1)} %copy-done.16, bf16[4,128,512]{2,1,0:T(8,128)(2,1)} %copy-done.17, ...), custom_call_target="tpu_custom_call" | custom-call | tf_op jit(solution)/shard_map/pallas_call | solution.py:510
  256.0 4.9 %collective-permute-done.79.theirs = bf16[2,128,768]{2,1,0:T(8,128)(2,1)} collective-permute-done((bf16[2,128,768]{2,1,0:T(8,128)(2,1)}, bf16[2,128,768]{2,1,0:T(8,128)(2,1)}, u32[]{:S(2)}, u32[]{:S(2)}) %collective-permute-start.79) | collective-permute-done | bytes 393248 | tf_op jit(solution)/shard_map/ppermute | solution.py:1209
  266.6 3.6 shard_map.381
  270.3 3.6 all-to-all-start.4
  274.6 2.2 shard_map.384
  287.9 3.0 collective-permute-done.86.refs_25_
  304.5 5.1 %shard_map.383 = (bf16[2,256,256]{2,1,0:T(8,128)(2,1)}, bf16[2,256,256]{2,1,0:T(8,128)(2,1)}) custom-call(s32[6]{0:T(128)} %stack.69.scalars, bf16[4,128,512]{2,1,0:T(8,128)(2,1)} %get-tuple-element.261.refs_0_, bf16[4,128,512]{2,1,0:T(8,128)(2,1)} %copy-done.15, bf16[4,128,512]{2,1,0:T(8,128)(2,1)} %copy-done.16, bf16[4,128,512]{2,1,0:T(8,128)(2,1)} %copy-done.17, ...), custom_call_target="tpu_custom_call" | custom-call | tf_op jit(solution)/shard_map/pallas_call | solution.py:510
  316.0 3.6 collective-permute-done.98
  319.7 7.4 %collective-permute-done.99 = bf16[384,256]{1,0:T(8,128)(2,1)S(1)} collective-permute-done((bf16[384,256]{1,0:T(8,128)(2,1)S(1)}, bf16[384,256]{1,0:T(8,128)(2,1)S(1)}, u32[]{:S(2)}, u32[]{:S(2)}) %collective-permute-start.99) | collective-permute-done | bytes 196640 | tf_op jit(solution)/shard_map/ppermute | solution.py:1213
  332.8 2.4 collective-permute-done.105.rest_3_
  335.3 7.9 %collective-permute-done.101 = bf16[384,256]{1,0:T(8,128)(2,1)S(1)} collective-permute-done((bf16[384,256]{1,0:T(8,128)(2,1)S(1)}, bf16[384,256]{1,0:T(8,128)(2,1)S(1)}, u32[]{:S(2)}, u32[]{:S(2)}) %collective-permute-start.101) | collective-permute-done | bytes 196640 | tf_op jit(solution)/shard_map/ppermute | solution.py:1213
  344.0 2.4 collective-permute-start.111
  349.0 6.7 %shard_map.385 = (f32[512,256]{1,0:T(8,128)}, f32[261,1024]{1,0:T(8,128)}, f32[256,512]{1,0:T(8,128)}, f32[261,1024]{1,0:T(8,128)}, f32[5,1024]{1,0:T(8,128)}) custom-call(s32[6]{0:T(128)} %stack.69.scalars, bf16[261,1024]{1,0:T(8,128)(2,1)} %key.5, bf16[261,1024]{1,0:T(8,128)(2,1)} %value.5, bf16[2,272,128]{2,1,0:T(8,128)(2,1)} %copy-done.41, ...), custom_call_target="tpu_custom_call" | custom-call | tf_op jit(solution)/shard_map/pallas_call | solution.py:510
  357.9 2.3 collective-permute-start.113
  363.1 2.4 shard_map.387
  368.8 4.3 %collective-permute-done.114.theirs = bf16[2,256,256]{2,1,0:T(8,128)(2,1)} collective-permute-done((bf16[2,256,256]{2,1,0:T(8,128)(2,1)S(1)}, bf16[2,256,256]{2,1,0:T(8,128)(2,1)}, u32[]{:S(2)}, u32[]{:S(2)}) %collective-permute-start.114) | collective-permute-done | bytes 262176 | tf_op jit(solution)/shard_map/ppermute | solution.py:1209
  (480 shorter events, 138.3 us)
Async XLA Ops:
  0.7 14.8 %collective-permute-start.2 = (bf16[512,256]{1,0:T(8,128)(2,1)}, bf16[512,256]{1,0:T(8,128)(2,1)S(1)}, u32[]{:S(2)}, u32[]{:S(2)}) collective-permute-start(bf16[512,256]{1,0:T(8,128)(2,1)} %rest_8_.1), channel_id=1, source_target_pairs={{0,16},{16,0},{1,17},{17,1},{2,18},{18,2},{3,19},{19,3},{4,20},{20... | collective-permute-start | bytes 786440 | tf_op jit(solution)/shard_map/ppermute | solution.py:464
  3.7 12.7 %collective-permute-start.3 = (bf16[512,256]{1,0:T(8,128)(2,1)}, bf16[512,256]{1,0:T(8,128)(2,1)S(1)}, u32[]{:S(2)}, u32[]{:S(2)}) collective-permute-start(bf16[512,256]{1,0:T(8,128)(2,1)} %rest_8_.1), channel_id=1, source_target_pairs={{0,8},{4,12},{8,0},{12,4},{1,9},{5,13},{9,1},{13,5},{2,10},{6,14},... | collective-permute-start | bytes 786440 | tf_op jit(solution)/shard_map/ppermute | solution.py:468
  5.2 13.0 %collective-permute-start.4 = (bf16[512,256]{1,0:T(8,128)(2,1)}, bf16[512,256]{1,0:T(8,128)(2,1)S(1)}, u32[]{:S(2)}, u32[]{:S(2)}) collective-permute-start(bf16[512,256]{1,0:T(8,128)(2,1)} %rest_8_.1), channel_id=1, source_target_pairs={{0,24},{4,28},{8,16},{12,20},{16,8},{20,12},{24,0},{28,4},{1,25},{... | collective-permute-start | bytes 786440 | tf_op jit(solution)/shard_map/ppermute | solution.py:476
  6.2 18.2 %collective-permute-start = (bf16[128,512]{1,0:T(8,128)(2,1)S(1)}, bf16[128,512]{1,0:T(8,128)(2,1)S(1)}, u32[]{:S(2)}, u32[]{:S(2)}) collective-permute-start(bf16[128,512]{1,0:T(8,128)(2,1)S(1)} %dynamic-slice_bitcast_fusion.4), channel_id=1, source_target_pairs={{0,16},{16,0},{1,17},{17,1},{2,18},{18,2},{3,19},{19,3},{4,20},{20... | collective-permute-start | bytes 393224 | tf_op jit(solution)/shard_map/ppermute | solution.py:464
  24.3 12.2 %collective-permute-start.17 = (bf16[768,256]{1,0:T(8,128)(2,1)}, bf16[768,256]{1,0:T(8,128)(2,1)S(1)}, u32[]{:S(2)}, u32[]{:S(2)}) collective-permute-start(bf16[768,256]{1,0:T(8,128)(2,1)} %get-tuple-element.193), channel_id=1, source_target_pairs={{0,16},{16,0},{1,17},{17,1},{2,18},{18,2},{3,19},{19,3},{4,20},{20... | collective-permute-start | bytes 1179656 | tf_op jit(solution)/shard_map/ppermute | solution.py:464
  24.9 18.7 %collective-permute-start.18 = (bf16[768,256]{1,0:T(8,128)(2,1)}, bf16[768,256]{1,0:T(8,128)(2,1)S(1)}, u32[]{:S(2)}, u32[]{:S(2)}) collective-permute-start(bf16[768,256]{1,0:T(8,128)(2,1)} %get-tuple-element.193), channel_id=1, source_target_pairs={{0,8},{4,12},{8,0},{12,4},{1,9},{5,13},{9,1},{13,5},{2,10},{6,14},... | collective-permute-start | bytes 1179656 | tf_op jit(solution)/shard_map/ppermute | solution.py:468
  25.6 19.4 %collective-permute-start.19 = (bf16[768,256]{1,0:T(8,128)(2,1)}, bf16[768,256]{1,0:T(8,128)(2,1)S(1)}, u32[]{:S(2)}, u32[]{:S(2)}) collective-permute-start(bf16[768,256]{1,0:T(8,128)(2,1)} %get-tuple-element.193), channel_id=1, source_target_pairs={{0,24},{4,28},{8,16},{12,20},{16,8},{20,12},{24,0},{28,4},{1,25},{... | collective-permute-start | bytes 1179656 | tf_op jit(solution)/shard_map/ppermute | solution.py:476
  45.0 17.2 %collective-permute-start.21 = (bf16[768,256]{1,0:T(8,128)(2,1)S(1)}, bf16[768,256]{1,0:T(8,128)(2,1)S(1)}, u32[]{:S(2)}, u32[]{:S(2)}) collective-permute-start(bf16[768,256]{1,0:T(8,128)(2,1)S(1)} %collective-permute-done.17.rest_2_.rest_18_), channel_id=1, source_target_pairs={{0,1},{1,0},{2,3},{3,2},{4,5},{5,4},{6,7},{7,6},{8,9},{9,8},{10,11... | collective-permute-start | bytes 1179656 | tf_op jit(solution)/shard_map/ppermute | solution.py:527
  48.2 15.4 %collective-permute-start.22 = (bf16[768,256]{1,0:T(8,128)(2,1)S(1)}, bf16[768,256]{1,0:T(8,128)(2,1)S(1)}, u32[]{:S(2)}, u32[]{:S(2)}) collective-permute-start(bf16[768,256]{1,0:T(8,128)(2,1)S(1)} %collective-permute-done.18.rest_3_.rest_19_), channel_id=1, source_target_pairs={{0,1},{1,0},{2,3},{3,2},{4,5},{5,4},{6,7},{7,6},{8,9},{9,8},{10,11... | collective-permute-start | bytes 1179656 | tf_op jit(solution)/shard_map/ppermute | solution.py:527
  57.0 19.8 %collective-permute-start.20 = (bf16[2,768,256]{2,1,0:T(8,128)(2,1)S(1)}, bf16[2,768,256]{2,1,0:T(8,128)(2,1)S(1)}, u32[]{:S(2)}, u32[]{:S(2)}) collective-permute-start(bf16[2,768,256]{2,1,0:T(8,128)(2,1)S(1)} %copy-done), channel_id=1, source_target_pairs={{0,4},{4,0},{8,12},{12,8},{1,5},{5,1},{9,13},{13,9},{2,6},{6,2},{1... | collective-permute-start | bytes 2359304 | tf_op jit(solution)/shard_map/ppermute | solution.py:472
  57.0 16.0 %all-to-all-start = ((bf16[8,272,128]{2,1,0:T(8,128)(2,1)}), bf16[8,272,128]{2,1,0:T(8,128)(2,1)}, u32[]{:S(2)}, u32[]{:S(2)}) async-start(bf16[8,272,128]{2,1,0:T(8,128)(2,1)} %get-tuple-element.189), calls=%async_computation | async-start | bytes 1114112 | tf_op jit(solution)/shard_map/all_to_all | solution.py:485
  73.6 18.1 %collective-permute-start.38 = (bf16[768,256]{1,0:T(8,128)(2,1)}, bf16[768,256]{1,0:T(8,128)(2,1)}, u32[]{:S(2)}, u32[]{:S(2)}) collective-permute-start(bf16[768,256]{1,0:T(8,128)(2,1)} %get-tuple-element.211), channel_id=1, source_target_pairs={{0,16},{16,0},{1,17},{17,1},{2,18},{18,2},{3,19},{19,3},{4,20},{20... | collective-permute-start | bytes 1179656 | tf_op jit(solution)/shard_map/ppermute | solution.py:464
  76.9 20.7 %collective-permute-start.39 = (bf16[768,256]{1,0:T(8,128)(2,1)}, bf16[768,256]{1,0:T(8,128)(2,1)}, u32[]{:S(2)}, u32[]{:S(2)}) collective-permute-start(bf16[768,256]{1,0:T(8,128)(2,1)} %get-tuple-element.211), channel_id=1, source_target_pairs={{0,8},{4,12},{8,0},{12,4},{1,9},{5,13},{9,1},{13,5},{2,10},{6,14},... | collective-permute-start | bytes 1179656 | tf_op jit(solution)/shard_map/ppermute | solution.py:468
  76.9 20.7 %collective-permute-start.40 = (bf16[768,256]{1,0:T(8,128)(2,1)}, bf16[768,256]{1,0:T(8,128)(2,1)}, u32[]{:S(2)}, u32[]{:S(2)}) collective-permute-start(bf16[768,256]{1,0:T(8,128)(2,1)} %get-tuple-element.211), channel_id=1, source_target_pairs={{0,24},{4,28},{8,16},{12,20},{16,8},{20,12},{24,0},{28,4},{1,25},{... | collective-permute-start | bytes 1179656 | tf_op jit(solution)/shard_map/ppermute | solution.py:476
  78.4 25.5 %collective-permute-start.9 = (bf16[512,384]{1,0:T(8,128)(2,1)}, bf16[512,384]{1,0:T(8,128)(2,1)S(1)}, u32[]{:S(2)}, u32[]{:S(2)}) collective-permute-start(bf16[512,384]{1,0:T(8,128)(2,1)} %get-tuple-element.187), channel_id=1, source_target_pairs={{0,16},{16,0},{1,17},{17,1},{2,18},{18,2},{3,19},{19,3},{4,20},{20... | collective-permute-start | bytes 1179656 | tf_op jit(solution)/shard_map/ppermute | solution.py:464
  91.0 18.5 %collective-permute-start.30 = (bf16[128,1024]{1,0:T(8,128)(2,1)}, bf16[128,1024]{1,0:T(8,128)(2,1)S(1)}, u32[]{:S(2)}, u32[]{:S(2)}) collective-permute-start(bf16[128,1024]{1,0:T(8,128)(2,1)} %get-tuple-element.204.rest_0_), channel_id=1, source_target_pairs={{0,16},{16,0},{1,17},{17,1},{2,18},{18,2},{3,19},{19,3},{4,20},{20... | collective-permute-start | bytes 786440 | tf_op jit(solution)/shard_map/ppermute | solution.py:464
  91.8 17.8 %collective-permute-start.31 = (bf16[128,1024]{1,0:T(8,128)(2,1)}, bf16[128,1024]{1,0:T(8,128)(2,1)S(1)}, u32[]{:S(2)}, u32[]{:S(2)}) collective-permute-start(bf16[128,1024]{1,0:T(8,128)(2,1)} %get-tuple-element.204.rest_0_), channel_id=1, source_target_pairs={{0,8},{4,12},{8,0},{12,4},{1,9},{5,13},{9,1},{13,5},{2,10},{6,14},... | collective-permute-start | bytes 786440 | tf_op jit(solution)/shard_map/ppermute | solution.py:468
  97.6 17.1 %collective-permute-start.32 = (bf16[128,1024]{1,0:T(8,128)(2,1)}, bf16[128,1024]{1,0:T(8,128)(2,1)}, u32[]{:S(2)}, u32[]{:S(2)}) collective-permute-start(bf16[128,1024]{1,0:T(8,128)(2,1)} %get-tuple-element.204.rest_0_), channel_id=1, source_target_pairs={{0,24},{4,28},{8,16},{12,20},{16,8},{20,12},{24,0},{28,4},{1,25},{... | collective-permute-start | bytes 786440 | tf_op jit(solution)/shard_map/ppermute | solution.py:476
  97.6 18.3 %collective-permute-start.42 = (bf16[768,256]{1,0:T(8,128)(2,1)}, bf16[768,256]{1,0:T(8,128)(2,1)S(1)}, u32[]{:S(2)}, u32[]{:S(2)}) collective-permute-start(bf16[768,256]{1,0:T(8,128)(2,1)} %collective-permute-done.38.rest_2_), channel_id=1, source_target_pairs={{0,1},{1,0},{2,3},{3,2},{4,5},{5,4},{6,7},{7,6},{8,9},{9,8},{10,11... | collective-permute-start | bytes 1179656 | tf_op jit(solution)/shard_map/ppermute | solution.py:527
  103.9 12.2 %collective-permute-start.43 = (bf16[768,256]{1,0:T(8,128)(2,1)}, bf16[768,256]{1,0:T(8,128)(2,1)S(1)}, u32[]{:S(2)}, u32[]{:S(2)}) collective-permute-start(bf16[768,256]{1,0:T(8,128)(2,1)} %collective-permute-done.39.rest_3_), channel_id=1, source_target_pairs={{0,1},{1,0},{2,3},{3,2},{4,5},{5,4},{6,7},{7,6},{8,9},{9,8},{10,11... | collective-permute-start | bytes 1179656 | tf_op jit(solution)/shard_map/ppermute | solution.py:527
  114.7 15.8 %collective-permute-start.44 = (bf16[768,256]{1,0:T(8,128)(2,1)}, bf16[768,256]{1,0:T(8,128)(2,1)S(1)}, u32[]{:S(2)}, u32[]{:S(2)}) collective-permute-start(bf16[768,256]{1,0:T(8,128)(2,1)} %collective-permute-done.40.rest_4_), channel_id=1, source_target_pairs={{0,1},{1,0},{2,3},{3,2},{4,5},{5,4},{6,7},{7,6},{8,9},{9,8},{10,11... | collective-permute-start | bytes 1179656 | tf_op jit(solution)/shard_map/ppermute | solution.py:527
  116.1 25.5 %collective-permute-start.41 = (bf16[2,768,256]{2,1,0:T(8,128)(2,1)S(1)}, bf16[2,768,256]{2,1,0:T(8,128)(2,1)S(1)}, u32[]{:S(2)}, u32[]{:S(2)}) collective-permute-start(bf16[2,768,256]{2,1,0:T(8,128)(2,1)S(1)} %copy-done.38), channel_id=1, source_target_pairs={{0,4},{4,0},{8,12},{12,8},{1,5},{5,1},{9,13},{13,9},{2,6},{6,2},{1... | collective-permute-start | bytes 2359304 | tf_op jit(solution)/shard_map/ppermute | solution.py:472
  116.6 14.5 %collective-permute-start.45 = (bf16[768,256]{1,0:T(8,128)(2,1)}, bf16[768,256]{1,0:T(8,128)(2,1)S(1)}, u32[]{:S(2)}, u32[]{:S(2)}) collective-permute-start(bf16[768,256]{1,0:T(8,128)(2,1)} %collective-permute-done.38.rest_2_), channel_id=1, source_target_pairs={{0,4},{4,0},{8,12},{12,8},{1,5},{5,1},{9,13},{13,9},{2,6},{6,2},{1... | collective-permute-start | bytes 1179656 | tf_op jit(solution)/shard_map/ppermute | solution.py:472
  118.0 13.3 %collective-permute-start.46 = (bf16[768,256]{1,0:T(8,128)(2,1)}, bf16[768,256]{1,0:T(8,128)(2,1)}, u32[]{:S(2)}, u32[]{:S(2)}) collective-permute-start(bf16[768,256]{1,0:T(8,128)(2,1)} %collective-permute-done.39.rest_3_), channel_id=1, source_target_pairs={{0,4},{4,0},{8,12},{12,8},{1,5},{5,1},{9,13},{13,9},{2,6},{6,2},{1... | collective-permute-start | bytes 1179656 | tf_op jit(solution)/shard_map/ppermute | solution.py:472
  162.6 18.6 %collective-permute-start.51 = (bf16[4,128,512]{2,1,0:T(8,128)(2,1)}, bf16[4,128,512]{2,1,0:T(8,128)(2,1)S(1)}, u32[]{:S(2)}, u32[]{:S(2)}) collective-permute-start(bf16[4,128,512]{2,1,0:T(8,128)(2,1)} %get-tuple-element.235), channel_id=1, source_target_pairs={{0,16},{16,0},{1,17},{17,1},{2,18},{18,2},{3,19},{19,3},{4,20},{20... | collective-permute-start | bytes 1572872 | tf_op jit(solution)/shard_map/ppermute | solution.py:464
  165.0 16.1 %collective-permute-start.52 = (bf16[4,128,256]{2,1,0:T(8,128)(2,1)S(1)}, bf16[4,128,256]{2,1,0:T(8,128)(2,1)S(1)}, u32[]{:S(2)}, u32[]{:S(2)}) collective-permute-start(bf16[4,128,256]{2,1,0:T(8,128)(2,1)S(1)} %get-tuple-element.421), channel_id=1, source_target_pairs={{0,4},{4,0},{8,12},{12,8},{1,5},{5,1},{9,13},{13,9},{2,6},{6,2},{1... | collective-permute-start | bytes 786440 | tf_op jit(solution)/shard_map/ppermute | solution.py:472
  165.1 16.0 %collective-permute-start.53 = (bf16[4,128,256]{2,1,0:T(8,128)(2,1)S(1)}, bf16[4,128,256]{2,1,0:T(8,128)(2,1)S(1)}, u32[]{:S(2)}, u32[]{:S(2)}) collective-permute-start(bf16[4,128,256]{2,1,0:T(8,128)(2,1)S(1)} %get-tuple-element.420), channel_id=1, source_target_pairs={{0,8},{4,12},{8,0},{12,4},{1,9},{5,13},{9,1},{13,5},{2,10},{6,14},... | collective-permute-start | bytes 786440 | tf_op jit(solution)/shard_map/ppermute | solution.py:468
  165.7 15.4 %collective-permute-start.54 = (bf16[4,128,256]{2,1,0:T(8,128)(2,1)S(1)}, bf16[4,128,256]{2,1,0:T(8,128)(2,1)S(1)}, u32[]{:S(2)}, u32[]{:S(2)}) collective-permute-start(bf16[4,128,256]{2,1,0:T(8,128)(2,1)S(1)} %get-tuple-element.419), channel_id=1, source_target_pairs={{0,12},{4,8},{8,4},{12,0},{1,13},{5,9},{9,5},{13,1},{2,14},{6,10},... | collective-permute-start | bytes 786440 | tf_op jit(solution)/shard_map/ppermute | solution.py:1221
  186.1 13.9 %collective-permute-start.57 = (bf16[128,1024]{1,0:T(8,128)(2,1)S(1)}, bf16[128,1024]{1,0:T(8,128)(2,1)S(1)}, u32[]{:S(2)}, u32[]{:S(2)}) collective-permute-start(bf16[128,1024]{1,0:T(8,128)(2,1)S(1)} %get-tuple-element.423), channel_id=1, source_target_pairs={{0,8},{4,12},{8,0},{12,4},{1,9},{5,13},{9,1},{13,5},{2,10},{6,14},... | collective-permute-start | bytes 786440 | tf_op jit(solution)/shard_map/ppermute | solution.py:468
  186.6 13.3 %collective-permute-start.58 = (bf16[128,1024]{1,0:T(8,128)(2,1)S(1)}, bf16[128,1024]{1,0:T(8,128)(2,1)S(1)}, u32[]{:S(2)}, u32[]{:S(2)}) collective-permute-start(bf16[128,1024]{1,0:T(8,128)(2,1)S(1)} %get-tuple-element.422), channel_id=1, source_target_pairs={{0,24},{4,28},{8,16},{12,20},{16,8},{20,12},{24,0},{28,4},{1,25},{... | collective-permute-start | bytes 786440 | tf_op jit(solution)/shard_map/ppermute | solution.py:476
  200.0 12.8 %collective-permute-start.61 = (bf16[4,128,512]{2,1,0:T(8,128)(2,1)S(1)}, bf16[4,128,512]{2,1,0:T(8,128)(2,1)S(1)}, u32[]{:S(2)}, u32[]{:S(2)}) collective-permute-start(bf16[4,128,512]{2,1,0:T(8,128)(2,1)S(1)} %copy-done.14), channel_id=1, source_target_pairs={{0,8},{4,12},{8,0},{12,4},{1,9},{5,13},{9,1},{13,5},{2,10},{6,14},... | collective-permute-start | bytes 1572872 | tf_op jit(solution)/shard_map/ppermute | solution.py:468
  221.7 22.3 %collective-permute-start.71 = (bf16[4,128,512]{2,1,0:T(8,128)(2,1)S(1)}, bf16[4,128,512]{2,1,0:T(8,128)(2,1)S(1)}, u32[]{:S(2)}, u32[]{:S(2)}) collective-permute-start(bf16[4,128,512]{2,1,0:T(8,128)(2,1)S(1)} %collective-permute-done.51.refs_1_), channel_id=1, source_target_pairs={{0,8},{4,12},{8,0},{12,4},{1,9},{5,13},{9,1},{13,5},{2,10},{6,14},... | collective-permute-start | bytes 1572872 | tf_op jit(solution)/shard_map/ppermute | solution.py:468
  222.5 15.7 %collective-permute-start.70 = (bf16[128,768]{1,0:T(8,128)(2,1)S(1)}, bf16[128,768]{1,0:T(8,128)(2,1)S(1)}, u32[]{:S(2)}, u32[]{:S(2)}) collective-permute-start(bf16[128,768]{1,0:T(8,128)(2,1)S(1)} %add_convert_fusion.3), channel_id=1, source_target_pairs={{0,2},{2,0},{1,3},{3,1},{4,6},{6,4},{5,7},{7,5},{8,10},{10,8},{9,1... | collective-permute-start | bytes 589832 | tf_op jit(solution)/shard_map/ppermute | solution.py:1213
  225.0 14.0 %collective-permute-start.72 = (bf16[4,128,256]{2,1,0:T(8,128)(2,1)S(1)}, bf16[4,128,256]{2,1,0:T(8,128)(2,1)S(1)}, u32[]{:S(2)}, u32[]{:S(2)}) collective-permute-start(bf16[4,128,256]{2,1,0:T(8,128)(2,1)S(1)} %collective-permute-done.52.refs_12_), channel_id=1, source_target_pairs={{0,16},{16,0},{1,17},{17,1},{2,18},{18,2},{3,19},{19,3},{4,20},{20... | collective-permute-start | bytes 786440 | tf_op jit(solution)/shard_map/ppermute | solution.py:464
  226.1 13.7 %collective-permute-start.73 = (bf16[4,128,256]{2,1,0:T(8,128)(2,1)S(1)}, bf16[4,128,256]{2,1,0:T(8,128)(2,1)S(1)}, u32[]{:S(2)}, u32[]{:S(2)}) collective-permute-start(bf16[4,128,256]{2,1,0:T(8,128)(2,1)S(1)} %collective-permute-done.53.refs_10_), channel_id=1, source_target_pairs={{0,16},{16,0},{1,17},{17,1},{2,18},{18,2},{3,19},{19,3},{4,20},{20... | collective-permute-start | bytes 786440 | tf_op jit(solution)/shard_map/ppermute | solution.py:464
  227.0 17.0 %collective-permute-start.74 = (bf16[4,128,256]{2,1,0:T(8,128)(2,1)S(1)}, bf16[4,128,256]{2,1,0:T(8,128)(2,1)S(1)}, u32[]{:S(2)}, u32[]{:S(2)}) collective-permute-start(bf16[4,128,256]{2,1,0:T(8,128)(2,1)S(1)} %collective-permute-done.54.refs_14_), channel_id=1, source_target_pairs={{0,16},{16,0},{1,17},{17,1},{2,18},{18,2},{3,19},{19,3},{4,20},{20... | collective-permute-start | bytes 786440 | tf_op jit(solution)/shard_map/ppermute | solution.py:464
  245.1 15.7 %all-to-all-start.3 = ((bf16[8,272,128]{2,1,0:T(8,128)(2,1)}), bf16[8,272,128]{2,1,0:T(8,128)(2,1)S(1)}, u32[]{:S(2)}, u32[]{:S(2)}) async-start(bf16[8,272,128]{2,1,0:T(8,128)(2,1)} %get-tuple-element.259), calls=%async_computation.3 | async-start | bytes 1114112 | tf_op jit(solution)/shard_map/all_to_all | solution.py:485
  249.0 11.8 %collective-permute-start.79 = (bf16[2,128,768]{2,1,0:T(8,128)(2,1)}, bf16[2,128,768]{2,1,0:T(8,128)(2,1)}, u32[]{:S(2)}, u32[]{:S(2)}) collective-permute-start(bf16[2,128,768]{2,1,0:T(8,128)(2,1)} %pad_maximum_fusion.mine), channel_id=1, source_target_pairs={{0,1},{1,0},{2,3},{3,2},{4,5},{5,4},{6,7},{7,6},{8,9},{9,8},{10,11... | collective-permute-start | bytes 1179656 | tf_op jit(solution)/shard_map/ppermute | solution.py:1209
  270.3 24.9 %all-to-all-start.4 = ((bf16[8,2,272,128]{3,2,1,0:T(8,128)(2,1)}), bf16[8,2,272,128]{3,2,1,0:T(8,128)(2,1)S(1)}, u32[]{:S(2)}, u32[]{:S(2)}) async-start(bf16[8,2,272,128]{3,2,1,0:T(8,128)(2,1)} %get-tuple-element.283), calls=%async_computation.4 | async-start | bytes 2228224 | tf_op jit(solution)/shard_map/all_to_all | solution.py:485
  278.0 17.2 %collective-permute-start.85 = (bf16[1,128,512]{2,1,0:T(8,128)(2,1)S(1)}, bf16[1,128,512]{2,1,0:T(8,128)(2,1)}, u32[]{:S(2)}, u32[]{:S(2)}) collective-permute-start(bf16[1,128,512]{2,1,0:T(8,128)(2,1)S(1)} %copy-done.71), channel_id=1, source_target_pairs={{0,8},{4,12},{8,0},{12,4},{1,9},{5,13},{9,1},{13,5},{2,10},{6,14},... | collective-permute-start | bytes 393224 | tf_op jit(solution)/shard_map/ppermute | solution.py:468
  301.0 14.2 %collective-permute-start.91 = (f32[128,512]{1,0:T(8,128)S(1)}, f32[128,512]{1,0:T(8,128)S(1)}, u32[]{:S(2)}, u32[]{:S(2)}) collective-permute-start(f32[128,512]{1,0:T(8,128)S(1)} %get-tuple-element.433), channel_id=1, source_target_pairs={{0,16},{16,0},{1,17},{17,1},{2,18},{18,2},{3,19},{19,3},{4,20},{20... | collective-permute-start | bytes 786440 | tf_op jit(solution)/shard_map/ppermute | solution.py:464
  312.9 17.9 %collective-permute-start.102 = (bf16[2,256,256]{2,1,0:T(8,128)(2,1)}, bf16[2,256,256]{2,1,0:T(8,128)(2,1)S(1)}, u32[]{:S(2)}, u32[]{:S(2)}) collective-permute-start(bf16[2,256,256]{2,1,0:T(8,128)(2,1)} %get-tuple-element.311), channel_id=1, source_target_pairs={{0,1},{1,0},{2,3},{3,2},{4,5},{5,4},{6,7},{7,6},{8,9},{9,8},{10,11... | collective-permute-start | bytes 786440 | tf_op jit(solution)/shard_map/ppermute | solution.py:1209
  314.2 12.9 %collective-permute-start.99 = (bf16[384,256]{1,0:T(8,128)(2,1)S(1)}, bf16[384,256]{1,0:T(8,128)(2,1)S(1)}, u32[]{:S(2)}, u32[]{:S(2)}) collective-permute-start(bf16[384,256]{1,0:T(8,128)(2,1)S(1)} %copy-done.62), channel_id=1, source_target_pairs={{0,2},{2,0},{1,3},{3,1},{4,6},{6,4},{5,7},{7,5},{8,10},{10,8},{9,1... | collective-permute-start | bytes 589832 | tf_op jit(solution)/shard_map/ppermute | solution.py:1213
  314.8 12.4 %collective-permute-start.100 = (bf16[512,384]{1,0:T(8,128)(2,1)S(1)}, bf16[512,384]{1,0:T(8,128)(2,1)S(1)}, u32[]{:S(2)}, u32[]{:S(2)}) collective-permute-start(bf16[512,384]{1,0:T(8,128)(2,1)S(1)} %copy-done.111), channel_id=1, source_target_pairs={{0,16},{16,0},{1,17},{17,1},{2,18},{18,2},{3,19},{19,3},{4,20},{20... | collective-permute-start | bytes 1179656 | tf_op jit(solution)/shard_map/ppermute | solution.py:464
  331.5 11.8 %collective-permute-start.106 = (bf16[2,272,128]{2,1,0:T(8,128)(2,1)S(1)}, bf16[2,272,128]{2,1,0:T(8,128)(2,1)S(1)}, u32[]{:S(2)}, u32[]{:S(2)}) collective-permute-start(bf16[2,272,128]{2,1,0:T(8,128)(2,1)S(1)} %add_convert_fusion.6.rest_0_), channel_id=1, source_target_pairs={{0,4},{4,0},{8,12},{12,8},{1,5},{5,1},{9,13},{13,9},{2,6},{6,2},{1... | collective-permute-start | bytes 417800 | tf_op jit(solution)/shard_map/ppermute | solution.py:472
  344.0 13.9 %collective-permute-start.112 = (bf16[2,384,256]{2,1,0:T(8,128)(2,1)S(1)}, bf16[2,384,256]{2,1,0:T(8,128)(2,1)S(1)}, u32[]{:S(2)}, u32[]{:S(2)}) collective-permute-start(bf16[2,384,256]{2,1,0:T(8,128)(2,1)S(1)} %pad_maximum_fusion.1.mine), channel_id=1, source_target_pairs={{0,1},{1,0},{2,3},{3,2},{4,5},{5,4},{6,7},{7,6},{8,9},{9,8},{10,11... | collective-permute-start | bytes 1179656 | tf_op jit(solution)/shard_map/ppermute | solution.py:1209
  344.0 11.8 %collective-permute-start.111 = (bf16[256,256]{1,0:T(8,128)(2,1)}, bf16[256,256]{1,0:T(8,128)(2,1)}, u32[]{:S(2)}, u32[]{:S(2)}) collective-permute-start(bf16[256,256]{1,0:T(8,128)(2,1)} %get-tuple-element.324), channel_id=1, source_target_pairs={{0,2},{2,0},{1,3},{3,1},{4,6},{6,4},{5,7},{7,5},{8,10},{10,8},{9,1... | collective-permute-start | bytes 393224 | tf_op jit(solution)/shard_map/ppermute | solution.py:1213
  348.6 17.9 %collective-permute-start.110 = (bf16[1024,261]{0,1:T(8,128)(2,1)S(1)}, bf16[1024,261]{0,1:T(8,128)(2,1)S(1)}, u32[]{:S(2)}, u32[]{:S(2)}) collective-permute-start(bf16[1024,261]{0,1:T(8,128)(2,1)S(1)} %copy.57), channel_id=1, source_target_pairs={{0,16},{16,0},{1,17},{17,1},{2,18},{18,2},{3,19},{19,3},{4,20},{20... | collective-permute-start | bytes 1603592 | tf_op jit(solution)/shard_map/ppermute | solution.py:464
  (184 other events, 1688.5 us)

commit v3 on v2

--- a/solution.py
+++ b/solution.py
@@ -1485,16 +1485,23 @@
     far = swap_far(total)
     early_far = swap_far(early_next)
     last_near = swap_near(last_give)
-    total, early_done = hold((plus(total, far), plus(early_mine, early_far)), pair)
+    total, early_done, last_next = hold(
+        (
+            plus(total, far), plus(early_mine, early_far), plus(last_keep[1], last_near[1]),
+        ),
+        pair,
+    )
     total_parts = gather_eight(total)
     early_other = swap_far(early_done)
-    early_half, last_mine, last_next, *total_parts = hold(
+    last_far = swap_far(last_next)
+    early_half, last_done, *total_parts = hold(
         [
-            jnp.stack([early_done, early_other]), plus(last_keep[0], last_near[0]),
-            plus(last_keep[1], last_near[1]),
+            jnp.stack([early_done, early_other]),
+            plus(plus(last_keep[0], last_near[0]), last_far),
         ] + total_parts,
     )
     early_rest = swap_near(early_half)
+    last_other = swap_far(last_done)
     grad_rows = after(grad_rows, *total_parts[1:])
     last_far = swap_far(last_next)
     grad_cross_query, grad_cross_key, grad_cross_out, grad_cross_value, gain_grads = kernel(
@@ -1511,8 +1518,6 @@
     half = D // 2
     gains_mine = lax.dynamic_slice_in_dim(gain_grads, row * half, half, 1)
 
-    last_done, grad_cross_query = hold((plus(last_mine, last_far), grad_cross_query), early_rest)
-    last_other = swap_far(last_done)
     early_sums = kernel(
         weight_out_kernel, [((512, WIDE), f32), ((WIDE, 512), f32), ((WIDE, 512), f32)],
         small, early_half, early_rest,

time: 381 us -> 386 us (1.013)
  waiting for transfers between devices: 114 us -> 119 us
    ppermute x7, waiting for transfers between devices: 21 us -> 34.9 us  [swap_far(): return lax.ppermute(value, 'dp', SEQ_FAR)]
    ppermute x7, waiting for transfers between devices: 17.4 us -> 12.2 us  [swap_near(): return lax.ppermute(value, 'dp', SEQ_NEAR)]
    ppermute x7, starting transfers between devices: 10.8 us -> 6.12 us  [swap_far(): return lax.ppermute(value, 'dp', SEQ_FAR)]
    unnamed x228 -> x218, local copies, waits for them, and re-layouts: 13.7 us -> 15.2 us
  transfers between devices with their start and end apart: 119 -> 119, of which waited for: 44 -> 39; matrix products, arithmetic and copies ran while one was open for 7% -> 7% of each run, Pallas kernels for 25% -> 25%
where the time goes in v3:
time: 386 us; the launch traced here: 380 us
  waiting for transfers between devices  119 us (31%)
  Pallas kernels  106 us (27%)
  starting transfers between devices  103 us (27%)
  local copies, waits for them, and re-layouts  29.4 us (8%)
  blocking collectives  10.6 us (3%)
  other arithmetic  9.97 us (3%)
    pallas_call x20, Pallas kernels, kernel(): pl.pallas_call(body, out_shape=tuple((jax.ShapeDtypeStruct(shape, kind) f...  106 us
    ppermute x7, waiting for transfers between devices, swap_far(): return lax.ppermute(value, 'dp', SEQ_FAR)  34.9 us
    ppermute x26, starting transfers between devices, swap_row(): return lax.ppermute(value, 'row', ROW_SWAP)  32.3 us
    ppermute x26, waiting for transfers between devices, swap_row(): return lax.ppermute(value, 'row', ROW_SWAP)  24.3 us
    ppermute x14, waiting for transfers between devices, swap_chip(): return lax.ppermute(value, 'col', col_step(2))  19 us
    all_to_all x4, starting transfers between devices, exchange(): return lax.all_to_all(value, GROUP, 0, 0, tiled=True)  15.3 us
    unnamed x218, local copies, waits for them, and re-layouts  15.2 us
    ppermute x14, starting transfers between devices, swap_chip(): return lax.ppermute(value, 'col', col_step(2))  13.1 us
  transfers between devices with their start and end apart: 119, of which 39 were waited for; matrix products, arithmetic and copies ran while one was open for 7% of the time, Pallas kernels for 25%

profile of v3, /device:TPU:0, one launch (start us, length us, event | category | flops | bytes accessed | tf_op | source)
XLA Modules:
  0.0 379.9 jit_solution(1600665896133499247)
XLA Ops:
  0.7 3.0 collective-permute-start.2
  8.2 2.6 copy.54
  12.0 3.5 shard_map.368
  20.3 3.4 shard_map.369
  25.6 2.2 collective-permute-start.19
  30.5 4.6 %shard_map.370 = (bf16[128,1024]{1,0:T(8,128)(2,1)}, bf16[128,1024]{1,0:T(8,128)(2,1)}, bf16[272,1024]{1,0:T(8,128)(2,1)}, bf16[272,128]{1,0:T(8,128)(2,1)}) custom-call(s32[6]{0:T(128)} %stack.69.scalars, bf16[256,512]{1,0:T(8,128)(2,1)} %bitcast.94, bf16[128,512]{1,0:T(8,128)(2,1)} %copy-done.76, f32[4,1024]{1,0:T(4,128)} %maximum_select_fusion.7.gains, ...), custom_call_target="tpu_custom_call" | custom-call | tf_op jit(solution)/shard_map/pallas_call | solution.py:510
  36.5 2.1 collective-permute-start.12
  38.7 4.8 %collective-permute-done.18.rest_3_.rest_19_ = bf16[768,256]{1,0:T(8,128)(2,1)S(1)} collective-permute-done((bf16[768,256]{1,0:T(8,128)(2,1)}, bf16[768,256]{1,0:T(8,128)(2,1)S(1)}, u32[]{:S(2)}, u32[]{:S(2)}) %collective-permute-start.18) | collective-permute-done | bytes 393248 | tf_op jit(solution)/shard_map/ppermute | solution.py:468
  50.4 6.6 %shard_map.371 = (bf16[8,272,128]{2,1,0:T(8,128)(2,1)}, bf16[8,272,128]{2,1,0:T(8,128)(2,1)}) custom-call(s32[6]{0:T(128)} %stack.69.scalars, s32[8,1,128]{2,1,0:T(1,128)} %maximum_bitcast_fusion.limits, bf16[1024,272]{1,0:T(8,128)(2,1)} %get-tuple-element.177.rest_6_.rest_0_.plain, bf16[272,1024]{1,0:T(8,128)(2,1)} %get-tuple-element.186.turned, ...), custom_call_target="tpu_custom_call" | custom-call | tf_op jit(solution)/shard_map/pallas_call | solution.py:510
  57.0 4.4 %all-to-all-start = ((bf16[8,272,128]{2,1,0:T(8,128)(2,1)}), bf16[8,272,128]{2,1,0:T(8,128)(2,1)}, u32[]{:S(2)}, u32[]{:S(2)}) async-start(bf16[8,272,128]{2,1,0:T(8,128)(2,1)} %get-tuple-element.187), calls=%async_computation | async-start | bytes 1114112 | tf_op jit(solution)/shard_map/all_to_all | solution.py:485
  63.5 9.5 %collective-permute-done.23.rest_7_.rest_23_ = bf16[768,256]{1,0:T(8,128)(2,1)} collective-permute-done((bf16[768,256]{1,0:T(8,128)(2,1)S(1)}, bf16[768,256]{1,0:T(8,128)(2,1)}, u32[]{:S(2)}, u32[]{:S(2)}) %collective-permute-start.23) | collective-permute-done | bytes 393248 | tf_op jit(solution)/shard_map/ppermute | solution.py:527
  73.6 3.2 collective-permute-start.38
  81.2 4.3 %shard_map.372.folded_out = bf16[272,1024]{1,0:T(8,128)(2,1)} custom-call(s32[6]{0:T(128)} %stack.69.scalars, bf16[261,1024]{1,0:T(8,128)(2,1)} %value.5, bf16[2,768,256]{2,1,0:T(8,128)(2,1)} %get-tuple-element.192.rest_0_.rest_16_, bf16[2,768,256]{2,1,0:T(8,128)(2,1)} %copy-done.1, bf16[768,256]{1,0:T(8,128)(2,1)} %copy-done.2, bf16[768,256]{1,0:T(8,128)(2,1)} %copy-done.3, ...), custom_call_target="tpu_custom_call" | custom-call | tf_op jit(solution)/shard_map/pallas_call | solution.py:510
  85.6 5.5 %shard_map.373 = (bf16[272,128]{1,0:T(8,128)(2,1)}, f32[1,128]{1,0:T(1,128)}, f32[128,1024]{1,0:T(8,128)}, bf16[128,1024]{1,0:T(8,128)(2,1)}, f32[128,1024]{1,0:...) custom-call(s32[6]{0:T(128)} %stack.69.scalars, ...), custom_call_target="tpu_custom_call" | custom-call | tf_op jit(solution)/shard_map/pallas_call | solution.py:510
  92.2 5.4 %collective-permute-done.39.rest_3_ = bf16[768,256]{1,0:T(8,128)(2,1)} collective-permute-done((bf16[768,256]{1,0:T(8,128)(2,1)}, bf16[768,256]{1,0:T(8,128)(2,1)}, u32[]{:S(2)}, u32[]{:S(2)}) %collective-permute-start.39) | collective-permute-done | bytes 393248 | tf_op jit(solution)/shard_map/ppermute | solution.py:468
  99.2 4.8 %collective-permute-done.9.theirs = bf16[512,384]{1,0:T(8,128)(2,1)S(1)} collective-permute-done((bf16[512,384]{1,0:T(8,128)(2,1)}, bf16[512,384]{1,0:T(8,128)(2,1)S(1)}, u32[]{:S(2)}, u32[]{:S(2)}) %collective-permute-start.9) | collective-permute-done | bytes 393248 | tf_op jit(solution)/shard_map/ppermute | solution.py:464
  105.5 4.0 %collective-permute-done.30.rest_1_ = bf16[128,1024]{1,0:T(8,128)(2,1)S(1)} collective-permute-done((bf16[128,1024]{1,0:T(8,128)(2,1)}, bf16[128,1024]{1,0:T(8,128)(2,1)S(1)}, u32[]{:S(2)}, u32[]{:S(2)}) %collective-permute-start.30) | collective-permute-done | bytes 262176 | tf_op jit(solution)/shard_map/ppermute | solution.py:464
  110.1 4.6 %collective-permute-done.32.rest_3_ = bf16[128,1024]{1,0:T(8,128)(2,1)} collective-permute-done((bf16[128,1024]{1,0:T(8,128)(2,1)}, bf16[128,1024]{1,0:T(8,128)(2,1)}, u32[]{:S(2)}, u32[]{:S(2)}) %collective-permute-start.32) | collective-permute-done | bytes 262176 | tf_op jit(solution)/shard_map/ppermute | solution.py:476
  122.4 8.1 %shard_map.374 = (bf16[1024,1024]{1,0:T(8,128)(2,1)}, bf16[1024,384]{1,0:T(8,128)(2,1)}, bf16[1024,384]{1,0:T(8,128)(2,1)}, f32[128,1024]{1,0:T(8,128)}, f32[1,1...) custom-call(s32[6]{0:T(128)} %stack.69.scalars, bf16[512,384]{1,0:T(8,128)(2,1)} %get-tuple-element.178.mine, ...), custom_call_target="tpu_custom_call" | custom-call | tf_op jit(solution)/shard_map/pallas_call | solution.py:510
  131.7 3.6 all-to-all-start.1
  137.0 4.6 %all-to-all-done.1.parts = bf16[8,128,128]{2,1,0:T(8,128)(2,1)S(1)} async-done(((bf16[8,128,128]{2,1,0:T(8,128)(2,1)}), bf16[8,128,128]{2,1,0:T(8,128)(2,1)S(1)}, u32[]{:S(2)}, u32[]{:S(2)}) %all-to-all-start.1) | async-done | bytes 262176 | tf_op jit(solution)/shard_map/all_to_all | solution.py:485
  142.7 9.3 %shard_map.375 = (bf16[128,1024]{1,0:T(8,128)(2,1)}, bf16[4,128,512]{2,1,0:T(8,128)(2,1)}, bf16[4,128,512]{2,1,0:T(8,128)(2,1)}, bf16[4,4,128,256]{3,2,1,0:T(8,1...) custom-call(s32[6]{0:T(128)} %stack.69.scalars, bf16[8,128,128]{2,1,0:T(8,128)(2,1)} %copy-done.36, ...), custom_call_target="tpu_custom_call" | custom-call | tf_op jit(solution)/shard_map/pallas_call | solution.py:510
  152.0 10.6 %all_to_all.25.parts = bf16[8,128,128]{2,1,0:T(8,128)(2,1)} all-to-all(bf16[8,128,128]{2,1,0:T(8,128)(2,1)} %get-tuple-element.223), channel_id=1, replica_groups=mesh['row'=2,'col'=4,'dp'=4] {'col','row'}, dimensions={0} | all-to-all | bytes 524288 | tf_op jit(solution)/shard_map/all_to_all | solution.py:485
  166.9 10.1 %shard_map.376 = (bf16[1024,384]{1,0:T(8,128)(2,1)}, bf16[2,4,128,1024]{3,2,1,0:T(8,128)(2,1)}) custom-call(s32[6]{0:T(128)} %stack.69.scalars, bf16[8,128,128]{2,1,0:T(8,128)(2,1)} %all_to_all.25.parts, bf16[1024,384]{1,0:T(8,128)(2,1)} %get-tuple-element.217.qkv, f32[128,1024]{1,0:T(8,128)} %get-tuple-element.224.mixed, f32[1,1024]{1,0:T(1,128)} %get-tuple-element.225.lse, ...), custom_call_target="tpu_custom_call" | custom-call | tf_op jit(solution)/shard_map/pallas_call | solution.py:510
  177.0 4.1 %shard_map.377 = (bf16[2,128,768]{2,1,0:T(8,128)(2,1)}, bf16[2,128,768]{2,1,0:T(8,128)(2,1)}) custom-call(s32[6]{0:T(128)} %stack.69.scalars, bf16[1024,1024]{1,0:T(8,128)(2,1)} %get-tuple-element.228.rows, bf16[1024,384]{1,0:T(8,128)(2,1)} %get-tuple-element.229.grads), custom_call_target="tpu_custom_call" | custom-call | tf_op jit(solution)/shard_map/pallas_call | solution.py:510
  188.7 5.0 %collective-permute-done.59 = bf16[2,128,768]{2,1,0:T(8,128)(2,1)S(1)} collective-permute-done((bf16[2,128,768]{2,1,0:T(8,128)(2,1)S(1)}, bf16[2,128,768]{2,1,0:T(8,128)(2,1)S(1)}, u32[]{:S(2)}, u32[]{:S(2)}) %collective-permute-start.59) | collective-permute-done | bytes 393248 | tf_op jit(solution)/shard_map/ppermute | solution.py:1209
  194.4 5.6 %collective-permute-done.57.by_chip = bf16[128,1024]{1,0:T(8,128)(2,1)S(1)} collective-permute-done((bf16[128,1024]{1,0:T(8,128)(2,1)S(1)}, bf16[128,1024]{1,0:T(8,128)(2,1)S(1)}, u32[]{:S(2)}, u32[]{:S(2)}) %collective-permute-start.57) | collective-permute-done | bytes 262176 | tf_op jit(solution)/shard_map/ppermute | solution.py:468
  201.7 2.6 collective-permute-start.60
  204.3 7.3 %shard_map.378 = (f32[2,1024]{1,0:T(2,128)}, bf16[1,128,512]{2,1,0:T(8,128)(2,1)}, bf16[1,128,512]{2,1,0:T(8,128)(2,1)}, bf16[4,1,128,256]{3,2,1,0:T(8,128)(2,1)...) custom-call(s32[6]{0:T(128)} %stack.69.scalars, ...), custom_call_target="tpu_custom_call" | custom-call | tf_op jit(solution)/shard_map/pallas_call | solution.py:510
  222.4 2.5 collective-permute-start.70
  228.1 10.0 %shard_map.379 = (bf16[1024,261]{1,0:T(8,128)(2,1)}, f32[1,261]{1,0:T(1,128)}, bf16[8,272,128]{2,1,0:T(8,128)(2,1)}) custom-call(s32[6]{0:T(128)} %stack.69.scalars, bf16[8,272,128]{2,1,0:T(8,128)(2,1)} %get-tuple-element.222.queries, s32[8,1,128]{2,1,0:T(1,128)} %maximum_bitcast_fusion.limits, bf16[1024,272]{1,0:T(8,128)(2,1)} %get-tuple-element.177.rest_6_.rest_0_.plain, ...), custom_call_target="tpu_custom_call" | custom-call | tf_op jit(solution)/shard_map/pallas_call | solution.py:510
  239.8 4.2 %collective-permute-done.74.refs_15_ = bf16[4,128,256]{2,1,0:T(8,128)(2,1)S(1)} collective-permute-done((bf16[4,128,256]{2,1,0:T(8,128)(2,1)S(1)}, bf16[4,128,256]{2,1,0:T(8,128)(2,1)S(1)}, u32[]{:S(2)}, u32[]{:S(2)}) %collective-permute-start.74) | collective-permute-done | bytes 262176 | tf_op jit(solution)/shard_map/ppermute | solution.py:464
  245.1 3.8 all-to-all-start.3
  250.4 5.5 %shard_map.380 = (bf16[2,384,256]{2,1,0:T(8,128)(2,1)}, bf16[2,384,256]{2,1,0:T(8,128)(2,1)}) custom-call(s32[6]{0:T(128)} %stack.69.scalars, bf16[4,128,512]{2,1,0:T(8,128)(2,1)} %get-tuple-element.259.refs_0_, bf16[4,128,512]{2,1,0:T(8,128)(2,1)} %copy-done.15, bf16[4,128,512]{2,1,0:T(8,128)(2,1)} %copy-done.16, bf16[4,128,512]{2,1,0:T(8,128)(2,1)} %copy-done.17, ...), custom_call_target="tpu_custom_call" | custom-call | tf_op jit(solution)/shard_map/pallas_call | solution.py:510
  255.9 4.9 %collective-permute-done.79.theirs = bf16[2,128,768]{2,1,0:T(8,128)(2,1)} collective-permute-done((bf16[2,128,768]{2,1,0:T(8,128)(2,1)}, bf16[2,128,768]{2,1,0:T(8,128)(2,1)}, u32[]{:S(2)}, u32[]{:S(2)}) %collective-permute-start.79) | collective-permute-done | bytes 393248 | tf_op jit(solution)/shard_map/ppermute | solution.py:1209
  267.5 3.6 shard_map.381
  271.1 3.6 all-to-all-start.4
  275.4 2.2 shard_map.384
  284.1 2.2 collective-permute-done.93
  288.7 3.0 collective-permute-done.86.refs_25_
  305.4 5.1 %shard_map.383 = (bf16[2,256,256]{2,1,0:T(8,128)(2,1)}, bf16[2,256,256]{2,1,0:T(8,128)(2,1)}) custom-call(s32[6]{0:T(128)} %stack.69.scalars, bf16[4,128,512]{2,1,0:T(8,128)(2,1)} %get-tuple-element.259.refs_0_, bf16[4,128,512]{2,1,0:T(8,128)(2,1)} %copy-done.15, bf16[4,128,512]{2,1,0:T(8,128)(2,1)} %copy-done.16, bf16[4,128,512]{2,1,0:T(8,128)(2,1)} %copy-done.17, ...), custom_call_target="tpu_custom_call" | custom-call | tf_op jit(solution)/shard_map/pallas_call | solution.py:510
  316.9 3.6 collective-permute-done.98
  320.6 7.4 %collective-permute-done.99 = bf16[384,256]{1,0:T(8,128)(2,1)S(1)} collective-permute-done((bf16[384,256]{1,0:T(8,128)(2,1)S(1)}, bf16[384,256]{1,0:T(8,128)(2,1)S(1)}, u32[]{:S(2)}, u32[]{:S(2)}) %collective-permute-start.99) | collective-permute-done | bytes 196640 | tf_op jit(solution)/shard_map/ppermute | solution.py:1213
  331.7 8.9 %collective-permute-done.103 = bf16[256,256]{1,0:T(8,128)(2,1)S(1)} collective-permute-done((bf16[256,256]{1,0:T(8,128)(2,1)S(1)}, bf16[256,256]{1,0:T(8,128)(2,1)S(1)}, u32[]{:S(2)}, u32[]{:S(2)}) %collective-permute-start.103) | collective-permute-done | bytes 131104 | tf_op jit(solution)/shard_map/ppermute | solution.py:1213
  341.4 10.4 %collective-permute-done.102 = bf16[384,256]{1,0:T(8,128)(2,1)S(1)} collective-permute-done((bf16[384,256]{1,0:T(8,128)(2,1)S(1)}, bf16[384,256]{1,0:T(8,128)(2,1)S(1)}, u32[]{:S(2)}, u32[]{:S(2)}) %collective-permute-start.102) | collective-permute-done | bytes 196640 | tf_op jit(solution)/shard_map/ppermute | solution.py:1213
  357.1 3.6 collective-permute-done.112
  361.6 6.7 %shard_map.385 = (f32[512,256]{1,0:T(8,128)}, f32[261,1024]{1,0:T(8,128)}, f32[256,512]{1,0:T(8,128)}, f32[261,1024]{1,0:T(8,128)}, f32[5,1024]{1,0:T(8,128)}) custom-call(s32[6]{0:T(128)} %stack.69.scalars, bf16[261,1024]{1,0:T(8,128)(2,1)} %key.5, bf16[261,1024]{1,0:T(8,128)(2,1)} %value.5, bf16[2,272,128]{2,1,0:T(8,128)(2,1)} %copy-done.41, ...), custom_call_target="tpu_custom_call" | custom-call | tf_op jit(solution)/shard_map/pallas_call | solution.py:510
  371.9 2.4 shard_map.387
  (470 shorter events, 134.7 us)
Async XLA Ops:
  0.7 14.8 %collective-permute-start.2 = (bf16[512,256]{1,0:T(8,128)(2,1)}, bf16[512,256]{1,0:T(8,128)(2,1)S(1)}, u32[]{:S(2)}, u32[]{:S(2)}) collective-permute-start(bf16[512,256]{1,0:T(8,128)(2,1)} %rest_8_.1), channel_id=1, source_target_pairs={{0,16},{16,0},{1,17},{17,1},{2,18},{18,2},{3,19},{19,3},{4,20},{20... | collective-permute-start | bytes 786440 | tf_op jit(solution)/shard_map/ppermute | solution.py:464
  3.7 12.7 %collective-permute-start.3 = (bf16[512,256]{1,0:T(8,128)(2,1)}, bf16[512,256]{1,0:T(8,128)(2,1)S(1)}, u32[]{:S(2)}, u32[]{:S(2)}) collective-permute-start(bf16[512,256]{1,0:T(8,128)(2,1)} %rest_8_.1), channel_id=1, source_target_pairs={{0,8},{4,12},{8,0},{12,4},{1,9},{5,13},{9,1},{13,5},{2,10},{6,14},... | collective-permute-start | bytes 786440 | tf_op jit(solution)/shard_map/ppermute | solution.py:468
  5.2 13.0 %collective-permute-start.4 = (bf16[512,256]{1,0:T(8,128)(2,1)}, bf16[512,256]{1,0:T(8,128)(2,1)S(1)}, u32[]{:S(2)}, u32[]{:S(2)}) collective-permute-start(bf16[512,256]{1,0:T(8,128)(2,1)} %rest_8_.1), channel_id=1, source_target_pairs={{0,24},{4,28},{8,16},{12,20},{16,8},{20,12},{24,0},{28,4},{1,25},{... | collective-permute-start | bytes 786440 | tf_op jit(solution)/shard_map/ppermute | solution.py:476
  6.2 18.2 %collective-permute-start = (bf16[128,512]{1,0:T(8,128)(2,1)S(1)}, bf16[128,512]{1,0:T(8,128)(2,1)S(1)}, u32[]{:S(2)}, u32[]{:S(2)}) collective-permute-start(bf16[128,512]{1,0:T(8,128)(2,1)S(1)} %dynamic-slice_bitcast_fusion.4), channel_id=1, source_target_pairs={{0,16},{16,0},{1,17},{17,1},{2,18},{18,2},{3,19},{19,3},{4,20},{20... | collective-permute-start | bytes 393224 | tf_op jit(solution)/shard_map/ppermute | solution.py:464
  24.3 12.2 %collective-permute-start.17 = (bf16[768,256]{1,0:T(8,128)(2,1)}, bf16[768,256]{1,0:T(8,128)(2,1)S(1)}, u32[]{:S(2)}, u32[]{:S(2)}) collective-permute-start(bf16[768,256]{1,0:T(8,128)(2,1)} %get-tuple-element.191), channel_id=1, source_target_pairs={{0,16},{16,0},{1,17},{17,1},{2,18},{18,2},{3,19},{19,3},{4,20},{20... | collective-permute-start | bytes 1179656 | tf_op jit(solution)/shard_map/ppermute | solution.py:464
  24.9 18.7 %collective-permute-start.18 = (bf16[768,256]{1,0:T(8,128)(2,1)}, bf16[768,256]{1,0:T(8,128)(2,1)S(1)}, u32[]{:S(2)}, u32[]{:S(2)}) collective-permute-start(bf16[768,256]{1,0:T(8,128)(2,1)} %get-tuple-element.191), channel_id=1, source_target_pairs={{0,8},{4,12},{8,0},{12,4},{1,9},{5,13},{9,1},{13,5},{2,10},{6,14},... | collective-permute-start | bytes 1179656 | tf_op jit(solution)/shard_map/ppermute | solution.py:468
  25.6 19.4 %collective-permute-start.19 = (bf16[768,256]{1,0:T(8,128)(2,1)}, bf16[768,256]{1,0:T(8,128)(2,1)S(1)}, u32[]{:S(2)}, u32[]{:S(2)}) collective-permute-start(bf16[768,256]{1,0:T(8,128)(2,1)} %get-tuple-element.191), channel_id=1, source_target_pairs={{0,24},{4,28},{8,16},{12,20},{16,8},{20,12},{24,0},{28,4},{1,25},{... | collective-permute-start | bytes 1179656 | tf_op jit(solution)/shard_map/ppermute | solution.py:476
  45.0 17.2 %collective-permute-start.21 = (bf16[768,256]{1,0:T(8,128)(2,1)S(1)}, bf16[768,256]{1,0:T(8,128)(2,1)S(1)}, u32[]{:S(2)}, u32[]{:S(2)}) collective-permute-start(bf16[768,256]{1,0:T(8,128)(2,1)S(1)} %collective-permute-done.17.rest_2_.rest_18_), channel_id=1, source_target_pairs={{0,1},{1,0},{2,3},{3,2},{4,5},{5,4},{6,7},{7,6},{8,9},{9,8},{10,11... | collective-permute-start | bytes 1179656 | tf_op jit(solution)/shard_map/ppermute | solution.py:527
  48.2 15.4 %collective-permute-start.22 = (bf16[768,256]{1,0:T(8,128)(2,1)S(1)}, bf16[768,256]{1,0:T(8,128)(2,1)S(1)}, u32[]{:S(2)}, u32[]{:S(2)}) collective-permute-start(bf16[768,256]{1,0:T(8,128)(2,1)S(1)} %collective-permute-done.18.rest_3_.rest_19_), channel_id=1, source_target_pairs={{0,1},{1,0},{2,3},{3,2},{4,5},{5,4},{6,7},{7,6},{8,9},{9,8},{10,11... | collective-permute-start | bytes 1179656 | tf_op jit(solution)/shard_map/ppermute | solution.py:527
  57.0 19.8 %collective-permute-start.20 = (bf16[2,768,256]{2,1,0:T(8,128)(2,1)S(1)}, bf16[2,768,256]{2,1,0:T(8,128)(2,1)S(1)}, u32[]{:S(2)}, u32[]{:S(2)}) collective-permute-start(bf16[2,768,256]{2,1,0:T(8,128)(2,1)S(1)} %copy-done), channel_id=1, source_target_pairs={{0,4},{4,0},{8,12},{12,8},{1,5},{5,1},{9,13},{13,9},{2,6},{6,2},{1... | collective-permute-start | bytes 2359304 | tf_op jit(solution)/shard_map/ppermute | solution.py:472
  57.0 16.0 %all-to-all-start = ((bf16[8,272,128]{2,1,0:T(8,128)(2,1)}), bf16[8,272,128]{2,1,0:T(8,128)(2,1)}, u32[]{:S(2)}, u32[]{:S(2)}) async-start(bf16[8,272,128]{2,1,0:T(8,128)(2,1)} %get-tuple-element.187), calls=%async_computation | async-start | bytes 1114112 | tf_op jit(solution)/shard_map/all_to_all | solution.py:485
  73.6 18.1 %collective-permute-start.38 = (bf16[768,256]{1,0:T(8,128)(2,1)}, bf16[768,256]{1,0:T(8,128)(2,1)}, u32[]{:S(2)}, u32[]{:S(2)}) collective-permute-start(bf16[768,256]{1,0:T(8,128)(2,1)} %get-tuple-element.209), channel_id=1, source_target_pairs={{0,16},{16,0},{1,17},{17,1},{2,18},{18,2},{3,19},{19,3},{4,20},{20... | collective-permute-start | bytes 1179656 | tf_op jit(solution)/shard_map/ppermute | solution.py:464
  76.9 20.7 %collective-permute-start.39 = (bf16[768,256]{1,0:T(8,128)(2,1)}, bf16[768,256]{1,0:T(8,128)(2,1)}, u32[]{:S(2)}, u32[]{:S(2)}) collective-permute-start(bf16[768,256]{1,0:T(8,128)(2,1)} %get-tuple-element.209), channel_id=1, source_target_pairs={{0,8},{4,12},{8,0},{12,4},{1,9},{5,13},{9,1},{13,5},{2,10},{6,14},... | collective-permute-start | bytes 1179656 | tf_op jit(solution)/shard_map/ppermute | solution.py:468
  76.9 20.7 %collective-permute-start.40 = (bf16[768,256]{1,0:T(8,128)(2,1)}, bf16[768,256]{1,0:T(8,128)(2,1)}, u32[]{:S(2)}, u32[]{:S(2)}) collective-permute-start(bf16[768,256]{1,0:T(8,128)(2,1)} %get-tuple-element.209), channel_id=1, source_target_pairs={{0,24},{4,28},{8,16},{12,20},{16,8},{20,12},{24,0},{28,4},{1,25},{... | collective-permute-start | bytes 1179656 | tf_op jit(solution)/shard_map/ppermute | solution.py:476
  78.4 25.5 %collective-permute-start.9 = (bf16[512,384]{1,0:T(8,128)(2,1)}, bf16[512,384]{1,0:T(8,128)(2,1)S(1)}, u32[]{:S(2)}, u32[]{:S(2)}) collective-permute-start(bf16[512,384]{1,0:T(8,128)(2,1)} %get-tuple-element.185), channel_id=1, source_target_pairs={{0,16},{16,0},{1,17},{17,1},{2,18},{18,2},{3,19},{19,3},{4,20},{20... | collective-permute-start | bytes 1179656 | tf_op jit(solution)/shard_map/ppermute | solution.py:464
  91.0 18.5 %collective-permute-start.30 = (bf16[128,1024]{1,0:T(8,128)(2,1)}, bf16[128,1024]{1,0:T(8,128)(2,1)S(1)}, u32[]{:S(2)}, u32[]{:S(2)}) collective-permute-start(bf16[128,1024]{1,0:T(8,128)(2,1)} %get-tuple-element.202.rest_0_), channel_id=1, source_target_pairs={{0,16},{16,0},{1,17},{17,1},{2,18},{18,2},{3,19},{19,3},{4,20},{20... | collective-permute-start | bytes 786440 | tf_op jit(solution)/shard_map/ppermute | solution.py:464
  91.8 17.8 %collective-permute-start.31 = (bf16[128,1024]{1,0:T(8,128)(2,1)}, bf16[128,1024]{1,0:T(8,128)(2,1)S(1)}, u32[]{:S(2)}, u32[]{:S(2)}) collective-permute-start(bf16[128,1024]{1,0:T(8,128)(2,1)} %get-tuple-element.202.rest_0_), channel_id=1, source_target_pairs={{0,8},{4,12},{8,0},{12,4},{1,9},{5,13},{9,1},{13,5},{2,10},{6,14},... | collective-permute-start | bytes 786440 | tf_op jit(solution)/shard_map/ppermute | solution.py:468
  97.6 17.1 %collective-permute-start.32 = (bf16[128,1024]{1,0:T(8,128)(2,1)}, bf16[128,1024]{1,0:T(8,128)(2,1)}, u32[]{:S(2)}, u32[]{:S(2)}) collective-permute-start(bf16[128,1024]{1,0:T(8,128)(2,1)} %get-tuple-element.202.rest_0_), channel_id=1, source_target_pairs={{0,24},{4,28},{8,16},{12,20},{16,8},{20,12},{24,0},{28,4},{1,25},{... | collective-permute-start | bytes 786440 | tf_op jit(solution)/shard_map/ppermute | solution.py:476
  97.6 18.3 %collective-permute-start.42 = (bf16[768,256]{1,0:T(8,128)(2,1)}, bf16[768,256]{1,0:T(8,128)(2,1)S(1)}, u32[]{:S(2)}, u32[]{:S(2)}) collective-permute-start(bf16[768,256]{1,0:T(8,128)(2,1)} %collective-permute-done.38.rest_2_), channel_id=1, source_target_pairs={{0,1},{1,0},{2,3},{3,2},{4,5},{5,4},{6,7},{7,6},{8,9},{9,8},{10,11... | collective-permute-start | bytes 1179656 | tf_op jit(solution)/shard_map/ppermute | solution.py:527
  114.7 15.8 %collective-permute-start.44 = (bf16[768,256]{1,0:T(8,128)(2,1)}, bf16[768,256]{1,0:T(8,128)(2,1)S(1)}, u32[]{:S(2)}, u32[]{:S(2)}) collective-permute-start(bf16[768,256]{1,0:T(8,128)(2,1)} %collective-permute-done.40.rest_4_), channel_id=1, source_target_pairs={{0,1},{1,0},{2,3},{3,2},{4,5},{5,4},{6,7},{7,6},{8,9},{9,8},{10,11... | collective-permute-start | bytes 1179656 | tf_op jit(solution)/shard_map/ppermute | solution.py:527
  116.1 25.5 %collective-permute-start.41 = (bf16[2,768,256]{2,1,0:T(8,128)(2,1)S(1)}, bf16[2,768,256]{2,1,0:T(8,128)(2,1)S(1)}, u32[]{:S(2)}, u32[]{:S(2)}) collective-permute-start(bf16[2,768,256]{2,1,0:T(8,128)(2,1)S(1)} %copy-done.38), channel_id=1, source_target_pairs={{0,4},{4,0},{8,12},{12,8},{1,5},{5,1},{9,13},{13,9},{2,6},{6,2},{1... | collective-permute-start | bytes 2359304 | tf_op jit(solution)/shard_map/ppermute | solution.py:472
  116.6 14.5 %collective-permute-start.45 = (bf16[768,256]{1,0:T(8,128)(2,1)}, bf16[768,256]{1,0:T(8,128)(2,1)S(1)}, u32[]{:S(2)}, u32[]{:S(2)}) collective-permute-start(bf16[768,256]{1,0:T(8,128)(2,1)} %collective-permute-done.38.rest_2_), channel_id=1, source_target_pairs={{0,4},{4,0},{8,12},{12,8},{1,5},{5,1},{9,13},{13,9},{2,6},{6,2},{1... | collective-permute-start | bytes 1179656 | tf_op jit(solution)/shard_map/ppermute | solution.py:472
  118.0 13.3 %collective-permute-start.46 = (bf16[768,256]{1,0:T(8,128)(2,1)}, bf16[768,256]{1,0:T(8,128)(2,1)}, u32[]{:S(2)}, u32[]{:S(2)}) collective-permute-start(bf16[768,256]{1,0:T(8,128)(2,1)} %collective-permute-done.39.rest_3_), channel_id=1, source_target_pairs={{0,4},{4,0},{8,12},{12,8},{1,5},{5,1},{9,13},{13,9},{2,6},{6,2},{1... | collective-permute-start | bytes 1179656 | tf_op jit(solution)/shard_map/ppermute | solution.py:472
  162.5 18.6 %collective-permute-start.51 = (bf16[4,128,512]{2,1,0:T(8,128)(2,1)}, bf16[4,128,512]{2,1,0:T(8,128)(2,1)S(1)}, u32[]{:S(2)}, u32[]{:S(2)}) collective-permute-start(bf16[4,128,512]{2,1,0:T(8,128)(2,1)} %get-tuple-element.233), channel_id=1, source_target_pairs={{0,16},{16,0},{1,17},{17,1},{2,18},{18,2},{3,19},{19,3},{4,20},{20... | collective-permute-start | bytes 1572872 | tf_op jit(solution)/shard_map/ppermute | solution.py:464
  165.0 16.1 %collective-permute-start.52 = (bf16[4,128,256]{2,1,0:T(8,128)(2,1)S(1)}, bf16[4,128,256]{2,1,0:T(8,128)(2,1)S(1)}, u32[]{:S(2)}, u32[]{:S(2)}) collective-permute-start(bf16[4,128,256]{2,1,0:T(8,128)(2,1)S(1)} %get-tuple-element.417), channel_id=1, source_target_pairs={{0,4},{4,0},{8,12},{12,8},{1,5},{5,1},{9,13},{13,9},{2,6},{6,2},{1... | collective-permute-start | bytes 786440 | tf_op jit(solution)/shard_map/ppermute | solution.py:472
  165.1 16.0 %collective-permute-start.53 = (bf16[4,128,256]{2,1,0:T(8,128)(2,1)S(1)}, bf16[4,128,256]{2,1,0:T(8,128)(2,1)S(1)}, u32[]{:S(2)}, u32[]{:S(2)}) collective-permute-start(bf16[4,128,256]{2,1,0:T(8,128)(2,1)S(1)} %get-tuple-element.416), channel_id=1, source_target_pairs={{0,8},{4,12},{8,0},{12,4},{1,9},{5,13},{9,1},{13,5},{2,10},{6,14},... | collective-permute-start | bytes 786440 | tf_op jit(solution)/shard_map/ppermute | solution.py:468
  165.7 15.4 %collective-permute-start.54 = (bf16[4,128,256]{2,1,0:T(8,128)(2,1)S(1)}, bf16[4,128,256]{2,1,0:T(8,128)(2,1)S(1)}, u32[]{:S(2)}, u32[]{:S(2)}) collective-permute-start(bf16[4,128,256]{2,1,0:T(8,128)(2,1)S(1)} %get-tuple-element.415), channel_id=1, source_target_pairs={{0,12},{4,8},{8,4},{12,0},{1,13},{5,9},{9,5},{13,1},{2,14},{6,10},... | collective-permute-start | bytes 786440 | tf_op jit(solution)/shard_map/ppermute | solution.py:1221
  186.0 13.9 %collective-permute-start.57 = (bf16[128,1024]{1,0:T(8,128)(2,1)S(1)}, bf16[128,1024]{1,0:T(8,128)(2,1)S(1)}, u32[]{:S(2)}, u32[]{:S(2)}) collective-permute-start(bf16[128,1024]{1,0:T(8,128)(2,1)S(1)} %get-tuple-element.419), channel_id=1, source_target_pairs={{0,8},{4,12},{8,0},{12,4},{1,9},{5,13},{9,1},{13,5},{2,10},{6,14},... | collective-permute-start | bytes 786440 | tf_op jit(solution)/shard_map/ppermute | solution.py:468
  186.6 13.3 %collective-permute-start.58 = (bf16[128,1024]{1,0:T(8,128)(2,1)S(1)}, bf16[128,1024]{1,0:T(8,128)(2,1)S(1)}, u32[]{:S(2)}, u32[]{:S(2)}) collective-permute-start(bf16[128,1024]{1,0:T(8,128)(2,1)S(1)} %get-tuple-element.418), channel_id=1, source_target_pairs={{0,24},{4,28},{8,16},{12,20},{16,8},{20,12},{24,0},{28,4},{1,25},{... | collective-permute-start | bytes 786440 | tf_op jit(solution)/shard_map/ppermute | solution.py:476
  200.0 12.8 %collective-permute-start.61 = (bf16[4,128,512]{2,1,0:T(8,128)(2,1)S(1)}, bf16[4,128,512]{2,1,0:T(8,128)(2,1)S(1)}, u32[]{:S(2)}, u32[]{:S(2)}) collective-permute-start(bf16[4,128,512]{2,1,0:T(8,128)(2,1)S(1)} %copy-done.14), channel_id=1, source_target_pairs={{0,8},{4,12},{8,0},{12,4},{1,9},{5,13},{9,1},{13,5},{2,10},{6,14},... | collective-permute-start | bytes 1572872 | tf_op jit(solution)/shard_map/ppermute | solution.py:468
  221.7 22.3 %collective-permute-start.71 = (bf16[4,128,512]{2,1,0:T(8,128)(2,1)S(1)}, bf16[4,128,512]{2,1,0:T(8,128)(2,1)S(1)}, u32[]{:S(2)}, u32[]{:S(2)}) collective-permute-start(bf16[4,128,512]{2,1,0:T(8,128)(2,1)S(1)} %collective-permute-done.51.refs_1_), channel_id=1, source_target_pairs={{0,8},{4,12},{8,0},{12,4},{1,9},{5,13},{9,1},{13,5},{2,10},{6,14},... | collective-permute-start | bytes 1572872 | tf_op jit(solution)/shard_map/ppermute | solution.py:468
  222.4 15.7 %collective-permute-start.70 = (bf16[128,768]{1,0:T(8,128)(2,1)S(1)}, bf16[128,768]{1,0:T(8,128)(2,1)S(1)}, u32[]{:S(2)}, u32[]{:S(2)}) collective-permute-start(bf16[128,768]{1,0:T(8,128)(2,1)S(1)} %add_convert_fusion.3), channel_id=1, source_target_pairs={{0,2},{2,0},{1,3},{3,1},{4,6},{6,4},{5,7},{7,5},{8,10},{10,8},{9,1... | collective-permute-start | bytes 589832 | tf_op jit(solution)/shard_map/ppermute | solution.py:1213
  225.0 14.0 %collective-permute-start.72 = (bf16[4,128,256]{2,1,0:T(8,128)(2,1)S(1)}, bf16[4,128,256]{2,1,0:T(8,128)(2,1)S(1)}, u32[]{:S(2)}, u32[]{:S(2)}) collective-permute-start(bf16[4,128,256]{2,1,0:T(8,128)(2,1)S(1)} %collective-permute-done.52.refs_12_), channel_id=1, source_target_pairs={{0,16},{16,0},{1,17},{17,1},{2,18},{18,2},{3,19},{19,3},{4,20},{20... | collective-permute-start | bytes 786440 | tf_op jit(solution)/shard_map/ppermute | solution.py:464
  226.1 13.7 %collective-permute-start.73 = (bf16[4,128,256]{2,1,0:T(8,128)(2,1)S(1)}, bf16[4,128,256]{2,1,0:T(8,128)(2,1)S(1)}, u32[]{:S(2)}, u32[]{:S(2)}) collective-permute-start(bf16[4,128,256]{2,1,0:T(8,128)(2,1)S(1)} %collective-permute-done.53.refs_10_), channel_id=1, source_target_pairs={{0,16},{16,0},{1,17},{17,1},{2,18},{18,2},{3,19},{19,3},{4,20},{20... | collective-permute-start | bytes 786440 | tf_op jit(solution)/shard_map/ppermute | solution.py:464
  227.0 17.0 %collective-permute-start.74 = (bf16[4,128,256]{2,1,0:T(8,128)(2,1)S(1)}, bf16[4,128,256]{2,1,0:T(8,128)(2,1)S(1)}, u32[]{:S(2)}, u32[]{:S(2)}) collective-permute-start(bf16[4,128,256]{2,1,0:T(8,128)(2,1)S(1)} %collective-permute-done.54.refs_14_), channel_id=1, source_target_pairs={{0,16},{16,0},{1,17},{17,1},{2,18},{18,2},{3,19},{19,3},{4,20},{20... | collective-permute-start | bytes 786440 | tf_op jit(solution)/shard_map/ppermute | solution.py:464
  245.1 15.7 %all-to-all-start.3 = ((bf16[8,272,128]{2,1,0:T(8,128)(2,1)}), bf16[8,272,128]{2,1,0:T(8,128)(2,1)S(1)}, u32[]{:S(2)}, u32[]{:S(2)}) async-start(bf16[8,272,128]{2,1,0:T(8,128)(2,1)} %get-tuple-element.257), calls=%async_computation.3 | async-start | bytes 1114112 | tf_op jit(solution)/shard_map/all_to_all | solution.py:485
  271.1 24.9 %all-to-all-start.4 = ((bf16[8,2,272,128]{3,2,1,0:T(8,128)(2,1)}), bf16[8,2,272,128]{3,2,1,0:T(8,128)(2,1)S(1)}, u32[]{:S(2)}, u32[]{:S(2)}) async-start(bf16[8,2,272,128]{3,2,1,0:T(8,128)(2,1)} %get-tuple-element.281), calls=%async_computation.4 | async-start | bytes 2228224 | tf_op jit(solution)/shard_map/all_to_all | solution.py:485
  278.7 17.4 %collective-permute-start.85 = (bf16[1,128,512]{2,1,0:T(8,128)(2,1)}, bf16[1,128,512]{2,1,0:T(8,128)(2,1)}, u32[]{:S(2)}, u32[]{:S(2)}) collective-permute-start(bf16[1,128,512]{2,1,0:T(8,128)(2,1)} %collective-permute-done.80.refs_17_), channel_id=1, source_target_pairs={{0,8},{4,12},{8,0},{12,4},{1,9},{5,13},{9,1},{13,5},{2,10},{6,14},... | collective-permute-start | bytes 393224 | tf_op jit(solution)/shard_map/ppermute | solution.py:468
  301.9 14.2 %collective-permute-start.91 = (f32[128,512]{1,0:T(8,128)S(1)}, f32[128,512]{1,0:T(8,128)S(1)}, u32[]{:S(2)}, u32[]{:S(2)}) collective-permute-start(f32[128,512]{1,0:T(8,128)S(1)} %get-tuple-element.427), channel_id=1, source_target_pairs={{0,16},{16,0},{1,17},{17,1},{2,18},{18,2},{3,19},{19,3},{4,20},{20... | collective-permute-start | bytes 786440 | tf_op jit(solution)/shard_map/ppermute | solution.py:464
  313.7 14.3 %collective-permute-start.100 = (bf16[2,256,256]{2,1,0:T(8,128)(2,1)}, bf16[2,256,256]{2,1,0:T(8,128)(2,1)S(1)}, u32[]{:S(2)}, u32[]{:S(2)}) collective-permute-start(bf16[2,256,256]{2,1,0:T(8,128)(2,1)} %get-tuple-element.307), channel_id=1, source_target_pairs={{0,1},{1,0},{2,3},{3,2},{4,5},{5,4},{6,7},{7,6},{8,9},{9,8},{10,11... | collective-permute-start | bytes 786440 | tf_op jit(solution)/shard_map/ppermute | solution.py:1209
  315.1 12.9 %collective-permute-start.99 = (bf16[384,256]{1,0:T(8,128)(2,1)S(1)}, bf16[384,256]{1,0:T(8,128)(2,1)S(1)}, u32[]{:S(2)}, u32[]{:S(2)}) collective-permute-start(bf16[384,256]{1,0:T(8,128)(2,1)S(1)} %copy-done.62), channel_id=1, source_target_pairs={{0,2},{2,0},{1,3},{3,1},{4,6},{6,4},{5,7},{7,5},{8,10},{10,8},{9,1... | collective-permute-start | bytes 589832 | tf_op jit(solution)/shard_map/ppermute | solution.py:1213
  315.7 12.4 %collective-permute-start.101 = (bf16[512,384]{1,0:T(8,128)(2,1)S(1)}, bf16[512,384]{1,0:T(8,128)(2,1)S(1)}, u32[]{:S(2)}, u32[]{:S(2)}) collective-permute-start(bf16[512,384]{1,0:T(8,128)(2,1)S(1)} %copy-done.106), channel_id=1, source_target_pairs={{0,16},{16,0},{1,17},{17,1},{2,18},{18,2},{3,19},{19,3},{4,20},{20... | collective-permute-start | bytes 1179656 | tf_op jit(solution)/shard_map/ppermute | solution.py:464
  328.1 12.5 %collective-permute-start.104 = (bf16[2,272,128]{2,1,0:T(8,128)(2,1)S(1)}, bf16[2,272,128]{2,1,0:T(8,128)(2,1)S(1)}, u32[]{:S(2)}, u32[]{:S(2)}) collective-permute-start(bf16[2,272,128]{2,1,0:T(8,128)(2,1)S(1)} %add_convert_fusion.6.rest_0_), channel_id=1, source_target_pairs={{0,16},{16,0},{1,17},{17,1},{2,18},{18,2},{3,19},{19,3},{4,20},{20... | collective-permute-start | bytes 417800 | tf_op jit(solution)/shard_map/ppermute | solution.py:464
  328.5 12.3 %collective-permute-start.105 = (bf16[2,272,128]{2,1,0:T(8,128)(2,1)S(1)}, bf16[2,272,128]{2,1,0:T(8,128)(2,1)S(1)}, u32[]{:S(2)}, u32[]{:S(2)}) collective-permute-start(bf16[2,272,128]{2,1,0:T(8,128)(2,1)S(1)} %add_convert_fusion.6.rest_0_), channel_id=1, source_target_pairs={{0,8},{4,12},{8,0},{12,4},{1,9},{5,13},{9,1},{13,5},{2,10},{6,14},... | collective-permute-start | bytes 417800 | tf_op jit(solution)/shard_map/ppermute | solution.py:468
  331.7 20.2 %collective-permute-start.107 = (bf16[2,272,128]{2,1,0:T(8,128)(2,1)S(1)}, bf16[2,272,128]{2,1,0:T(8,128)(2,1)S(1)}, u32[]{:S(2)}, u32[]{:S(2)}) collective-permute-start(bf16[2,272,128]{2,1,0:T(8,128)(2,1)S(1)} %add_convert_fusion.6.rest_0_), channel_id=1, source_target_pairs={{0,4},{4,0},{8,12},{12,8},{1,5},{5,1},{9,13},{13,9},{2,6},{6,2},{1... | collective-permute-start | bytes 417800 | tf_op jit(solution)/shard_map/ppermute | solution.py:472
  353.8 23.3 %collective-permute-start.111 = (bf16[1024,261]{0,1:T(8,128)(2,1)}, bf16[1024,261]{0,1:T(8,128)(2,1)S(1)}, u32[]{:S(2)}, u32[]{:S(2)}) collective-permute-start(bf16[1024,261]{0,1:T(8,128)(2,1)} %copy.57), channel_id=1, source_target_pairs={{0,16},{16,0},{1,17},{17,1},{2,18},{18,2},{3,19},{19,3},{4,20},{20... | collective-permute-start | bytes 1603592 | tf_op jit(solution)/shard_map/ppermute | solution.py:464
  355.2 16.0 %collective-permute-start.114 = (bf16[2,384,256]{2,1,0:T(8,128)(2,1)S(1)}, bf16[2,384,256]{2,1,0:T(8,128)(2,1)S(1)}, u32[]{:S(2)}, u32[]{:S(2)}) collective-permute-start(bf16[2,384,256]{2,1,0:T(8,128)(2,1)S(1)} %pad_maximum_fusion.1.mine), channel_id=1, source_target_pairs={{0,1},{1,0},{2,3},{3,2},{4,5},{5,4},{6,7},{7,6},{8,9},{9,8},{10,11... | collective-permute-start | bytes 1179656 | tf_op jit(solution)/shard_map/ppermute | solution.py:1209
  360.7 13.6 %collective-permute-start.113 = (bf16[2,256,256]{2,1,0:T(8,128)(2,1)S(1)}, bf16[2,256,256]{2,1,0:T(8,128)(2,1)S(1)}, u32[]{:S(2)}, u32[]{:S(2)}) collective-permute-start(bf16[2,256,256]{2,1,0:T(8,128)(2,1)S(1)} %pad_maximum_fusion.2.mine), channel_id=1, source_target_pairs={{0,1},{1,0},{2,3},{3,2},{4,5},{5,4},{6,7},{7,6},{8,9},{9,8},{10,11... | collective-permute-start | bytes 786440 | tf_op jit(solution)/shard_map/ppermute | solution.py:1209
  (179 other events, 1699.8 us)
